TPU v7x, 32 devices: a whole 2x2x4 slice. The times are simulated.
32 devices in a mesh: pop: 8 (over y, x, core), row: 4 (over z).
Axes of the slice: x: 2, y: 2, z: 4, core: 2. Of those that a mesh axis runs over, the one named last changes fastest.
Arguments:
- tokens: bfloat16 [384, 16, 4096], P('pop'), may hold values from -6 to 6
- weight: bfloat16 [14336, 4096], P('row', 'pop'), may hold values from -0.09375 to 0.09375
- bank_in: bfloat16 [4096, 128], P('row'), may hold values from -0.09375 to 0.09375
- bank_out: bfloat16 [14336, 128], P('row'), may hold values from -6 to 6
- fitness: int32 [384], P('pop'), may hold values from 0 to 191
- past_seeds: int32 [384, 2, 8], P('pop'), may hold values from 0 to 127
- new_seeds: int32 [384, 2, 8], P('pop'), may hold values from 0 to 127
Outputs:
- hidden: bfloat16 [384, 16, 14336], P('pop', None, 'row')
- new_weight: bfloat16 [14336, 4096], P('row', 'pop')
All inputs are finite; a program needn't handle non-finite values.
Results may differ from a plain program's by a relative error of at most 0.012.
Values may be sent and summed in bfloat16 or wider, within the bound.
No kernel may reach another device: no remote copies, remote signals or barrier semaphores. Data moves between devices by JAX's collectives and lax.ppermute only.
A program may use at most 128 MiB of HBM per device.

v0:
```python
import jax
import jax.numpy as jnp
from jax import lax
from jax.sharding import PartitionSpec as P

NOISE_SCALE = 0.1
STEP_SCALE = 0.03


def one_hots(seeds, width):
    levels = jnp.arange(width, dtype=jnp.int32)
    out_hits = (seeds[:, 0, :, None] == levels).astype(jnp.float32)
    in_hits = (seeds[:, 1, :, None] == levels).astype(jnp.float32)
    return (out_hits, in_hits)


def shards(tokens, weight, bank_in, bank_out, fitness, past_seeds, new_seeds):
    members = fitness.shape[0]
    overall = members * lax.axis_size("pop")
    width = bank_out.shape[1]
    everyone = lax.all_gather(fitness, "pop", axis=0, tiled=True)
    lower_count = jnp.sum((everyone[None, :] < fitness[:, None]).astype(jnp.float32), axis=1)
    equal_count = jnp.sum((everyone[None, :] == fitness[:, None]).astype(jnp.float32), axis=1)
    centered = (lower_count + 0.5 * (equal_count - 1.0)) / (overall - 1.0) - 0.5
    out_hits, in_hits = one_hots(past_seeds, width)
    local_coupling = STEP_SCALE * jnp.einsum("m,mki,mkj->ij", centered, out_hits, in_hits)
    coupling = lax.psum(local_coupling, "pop")
    full_in = lax.all_gather(bank_in, "row", axis=0, tiled=True)
    left_part = jnp.dot(bank_out.astype(jnp.float32), coupling, precision=lax.Precision.HIGHEST)
    features = tokens.shape[2]
    flat_tokens = tokens.reshape(members * tokens.shape[1], features)
    own_offset = lax.axis_index("pop") * weight.shape[1]
    columns = lax.dynamic_slice_in_dim(full_in, own_offset, weight.shape[1], 0).astype(jnp.float32)
    update = jnp.dot(left_part, columns.T, precision=lax.Precision.HIGHEST)
    new_weight = (weight.astype(jnp.float32) + update).astype(jnp.bfloat16)
    columns = flat_tokens
    base_part = lax.dot_general(
        columns,
        lax.all_gather(new_weight, "pop", axis=1, tiled=True),
        (((1,), (1,)), ((), ())),
        preferred_element_type=jnp.float32,
    )
    projected = jnp.dot(flat_tokens, full_in, preferred_element_type=jnp.float32).reshape(
        members, tokens.shape[1], width
    )
    hidden_hits, feature_hits = one_hots(new_seeds, width)
    mixing = jnp.einsum("mkb,mkc->mbc", feature_hits, hidden_hits)
    low_term = (NOISE_SCALE * jnp.einsum("mtb,mbc->mtc", projected, mixing)).astype(jnp.bfloat16)
    extra = lax.dot_general(
        low_term.reshape(flat_tokens.shape[0], width),
        bank_out,
        (((1,), (1,)), ((), ())),
        preferred_element_type=jnp.float32,
    )
    hidden = (
        (base_part + extra).astype(jnp.bfloat16).reshape(members, tokens.shape[1], weight.shape[0])
    )
    return (hidden, new_weight)


def solution(mesh):
    placed = (
        P("pop", None, None),
        P("row", "pop"),
        P("row", None),
        P("row", None),
        P("pop"),
        P("pop", None, None),
        P("pop", None, None),
    )
    return jax.shard_map(
        shards,
        mesh=mesh,
        in_specs=placed,
        out_specs=(P("pop", None, "row"), P("row", "pop")),
        check_vma=False,
    )
```

profile of v0, /device:TPU:0, one launch (start us, length us, event | category | flops | bytes accessed | tf_op | source)
XLA Modules:
  0.0 272.2 jit_solution(11762700354457997980)
XLA Ops:
  8.0 0.0 copy-start
  8.0 0.0 all-reduce.3.cloned.1.call-start
  8.1 1.3 dynamic-slice
  10.0 0.9 dynamic-update-slice
  10.9 9.5 %all-reduce = s32[384]{0:T(512)S(1)} all-reduce(s32[384]{0:T(512)S(1)} %dynamic-update-slice), channel_id=1, replica_groups=mesh['pop'=8,'row'=4] {'pop'}, use_global_device_ids=true, to_apply=%add | all-reduce | flops 384 | bytes 3072
  20.4 0.8 convert_reduce_fusion
  21.2 0.7 slice_bitcast_fusion.3
  21.9 0.1 copy.13
  22.0 0.1 copy.14
  22.1 1.0 fusion.16
  23.1 0.0 all-reduce.3.cloned.1.call-update
  23.2 0.0 all-gather.3.cloned.1.call-start
  23.2 0.5 all-gather.3.cloned.1.call-update
  23.7 0.0 all-gather.5.cloned.1.call-start
  23.8 52.4 %all-reduce.3.cloned.1.call-done = f32[128,128]{1,0:T(8,128)} async-done(((f32[128,128]{1,0:T(8,128)}), f32[128,128]{1,0:T(8,128)}) %all-reduce.3.cloned.1.call-update) | async-done | bytes 65552 | tf_op jit(solution)/shard_map/psum | solution.py:27
  76.2 0.0 copy-done
  76.2 1.8 fusion.31
  77.9 0.0 copy-start.1
  77.9 0.0 all-gather.3.cloned.1.call-done
  78.0 6.2 %add_convert_fusion = bf16[3584,512]{1,0:T(8,128)(2,1)} fusion(bf16[3584,512]{1,0:T(8,128)(2,1)} %param.8, f32[128,3584]{1,0:T(8,128)S(1)} %fusion.31, bf16[4096,128]{1,0:T(8,128)(2,1)} %all-gather.3.cloned.1.call-done, s32[]{:T(128)S(6)} %select_n.3), kind=kOutput, calls=%fused_computation.2 | convolution fusion | flops 2824077312 | bytes 9306116 | tf_op jit(solution)/shard_map/dot_general | solution.py:34
  84.2 0.0 all-gather.5.cloned.1.call-update
  84.2 0.0 copy-done.1
  84.2 0.1 copy.15
  84.3 0.1 copy.16
  84.4 6.3 %fusion.11 = bf16[48,16,128]{2,1,0:T(8,128)(2,1)S(1)} fusion(bf16[48,16,4096]{2,1,0:T(8,128)(2,1)} %param.7, bf16[4096,128]{1,0:T(8,128)(2,1)} %all-gather.3.cloned.1.call-done, s32[48,8]{1,0:T(8,128)S(1)} %copy.16, s32[48,8]{1,0:T(8,128)S(1)} %copy.15), kind=kOutput, calls=%fused_computation.7 | convolution fusion | flops 843350016 | bytes 7539712 | tf_op jit(solution)/shard_map/mtb,mbc->mtc/dot_general | solution.py:48
  90.7 141.8 %all-gather.5.cloned.1.call-done = bf16[3584,4096]{1,0:T(8,128)(2,1)} async-done(((bf16[3584,512]{1,0:T(8,128)(2,1)}), bf16[3584,4096]{1,0:T(8,128)(2,1)}) %all-gather.5.cloned.1.call-update) | async-done | bytes 29360144 | tf_op jit(solution)/shard_map/all_gather | solution.py:39
  232.5 28.2 %fusion.32 = f32[3584,768]{0,1:T(8,128)S(1)} fusion(bf16[3584,4096]{1,0:T(8,128)(2,1)} %all-gather.5.cloned.1.call-done, bf16[768,4096]{1,0:T(8,128)(2,1)} %bitcast.34), kind=kOutput, calls=%fused_computation.33 | convolution fusion | flops 22548578304 | bytes 46661632 | tf_op jit(solution)/shard_map/dot_general | solution.py:37
  260.7 4.0 %fusion = bf16[768,3584]{1,0:T(8,128)(2,1)} fusion(f32[3584,768]{0,1:T(8,128)S(1)} %fusion.32, bf16[768,128]{1,0:T(8,128)(2,1)S(1)} %bitcast.33, bf16[3584,128]{1,0:T(8,128)(2,1)S(1)} %copy-done), kind=kOutput, calls=%fused_computation.1 | convolution fusion | flops 710148096 | bytes 17629184 | tf_op jit(solution)/shard_map/dot_general | solution.py:49
  (3 shorter events, 0.0 us)
Async XLA Ops:
  8.0 68.2 %copy-start = (bf16[3584,128]{1,0:T(8,128)(2,1)S(1)}, bf16[3584,128]{1,0:T(8,128)(2,1)}, u32[]{:S(2)}) copy-start(bf16[3584,128]{1,0:T(8,128)(2,1)} %param.10) | copy-start | bytes 2752516
  8.0 68.1 %all-reduce.3.cloned.1.call-start = ((), (), s32[]{:S(2)}) async-start(), calls=%async_computation | async-start | bytes 131072 | tf_op jit(solution)/shard_map/psum | solution.py:27
  23.2 54.8 %all-gather.3.cloned.1.call-start = ((), (), s32[]{:S(2)}) async-start(), calls=%async_computation.1 | async-start | bytes 1310720 | tf_op jit(solution)/shard_map/all_gather | solution.py:28
  23.7 208.8 %all-gather.5.cloned.1.call-start = ((), (), s32[]{:S(2)}) async-start(), calls=%async_computation.2 | async-start | bytes 33030144 | tf_op jit(solution)/shard_map/all_gather | solution.py:39
  77.9 6.3 %copy-start.1 = (s32[48,2,8]{0,2,1:T(8,128)S(1)}, s32[48,2,8]{0,2,1:T(8,128)}, u32[]{:S(2)}) copy-start(s32[48,2,8]{0,2,1:T(8,128)} %param.13) | copy-start | bytes 9220
Sparse Core Ops, SparseCore 0:
  23.3 52.8 all-reduce.2
  84.3 148.1 all-gather.4
Sparse Core Ops, SparseCore 1:
  25.2 27.5 all-gather.2
where the time goes:
time: 272 us
  waiting for transfers between devices  195 us (72%)
  matrix products  47.6 us (18%)
  between operations  16.2 us (6%)
  blocking collectives  9.49 us (3%)
  local copies, waits for them, and re-layouts  3.23 us (1%)
    all_gather x1, waiting for transfers between devices, shards(): lax.all_gather(new_weight, 'pop', axis=1, tiled=True)  142 us
    psum x1, waiting for transfers between devices, shards(): coupling = lax.psum(local_coupling, 'pop')  52.4 us
    dot_general x1, matrix products, shards(): lax.dot_general(columns, lax.all_gather(new_weight, 'pop', axis=1, tiled=...  28.2 us
    unnamed x1, blocking collectives  9.49 us
    dot_general x1, matrix products, shards(): jnp.einsum('mtb,mbc->mtc', projected, mixing)  6.34 us
    dot_general x1, matrix products, shards(): update = jnp.dot(left_part, columns.T, precision=lax.Precision.HIGHEST)  6.22 us
  transfers between devices with their start and end apart: 3, of which 2 were waited for; matrix products, arithmetic and copies ran while one was open for 3% of the time, Pallas kernels for 0%

commit v1 on v0

v1 whole, which is shorter than its diff:
```python
import functools

import jax
import jax.numpy as jnp
from jax import lax
from jax.experimental import pallas as pl
from jax.experimental.pallas import tpu as pltpu
from jax.sharding import PartitionSpec as P


NOISE_SCALE = 0.1
STEP_SCALE = 0.03


def one_hots(seeds, width):
    levels = jnp.arange(width, dtype=jnp.int32)
    out_hits = (seeds[:, 0, :, None] == levels).astype(jnp.float32)
    in_hits = (seeds[:, 1, :, None] == levels).astype(jnp.float32)
    return (out_hits, in_hits)


DIMS = (((1,), (1,)), ((), ()))
LAST = 2
VMEM_LIMIT = 16 * 1024 * 1024


def cut(rows, tile):
    tiles = rows // tile
    if rows % tile or tiles < 6 or tiles % 2:
        return None
    last = min(LAST, tiles // 2 - 1)
    lengths = [tiles // 2 - last] * 2 + [last] * 2
    pieces, start = [], 0
    for length in lengths:
        pieces.append((start * tile, length * tile))
        start += length
    return pieces


def product_kernel(counts, half, tile, offset, final, resident, at_ref, tokens_ref, *refs):
    whole, split, with_low, with_partial = counts
    refs = list(refs)
    out_ref = refs.pop()
    step = pl.program_id(0)
    here = pl.ds(pl.multiple_of(step * tile, tile), tile)
    place = 0

    def term(block_ref, place):
        depth = block_ref.shape[1]
        columns = pl.ds(pl.multiple_of(at_ref[place] * depth, 128), depth)
        return lax.dot_general(tokens_ref[:, columns], block_ref[...], DIMS, preferred_element_type=jnp.float32)

    def store(value):
        if final:
            out_ref[...] = value.astype(out_ref.dtype)
        else:
            out_ref[:, here] = value

    total = None
    if with_low:
        low_ref, bank_ref = refs.pop(0), refs.pop(0)
        bank = bank_ref[...]
        total = lax.dot_general(low_ref[...], jnp.concatenate([bank, bank], axis=1), DIMS, preferred_element_type=jnp.float32)
    if with_partial:
        part = refs.pop(0)[:, pl.ds(pl.multiple_of(offset + step * tile, tile), tile)]
        total = part if total is None else total + part
    for place in whole:
        value = term(refs.pop(0), place)
        total = value if total is None else total + value
    if not split:
        store(total)
        return
    groups = [(places, (refs.pop(0), refs.pop(0))) for places in split]

    def finish(pick):
        done = total
        for places, pair in groups:
            block = pair[pick]
            if resident:
                block = block.at[pl.ds(pl.multiple_of((step - pick * half) * tile, tile), tile)]
            value = term(block, places[pick])
            done = value if done is None else done + value
        store(done)

    pl.when(step < half)(lambda: finish(0))
    pl.when(step >= half)(lambda: finish(1))


def product(at, tokens, start, length, tile, rows, whole=(), split=(), low=None, bank_out=None, partial=None, offset=0, final=False, hidden=None, resident=False):
    lines = tokens.shape[0]
    base, half = start // tile, length // tile // 2
    specs, operands, depth_sum = [pl.BlockSpec(memory_space=pltpu.VMEM)], [tokens], 0

    def add(operand, spec):
        operands.append(operand)
        specs.append(spec)

    if low is not None:
        add(low, pl.BlockSpec(memory_space=pltpu.VMEM))
        add(bank_out, pl.BlockSpec((tile, bank_out.shape[1]), lambda i, at: (base + i, 0)))
    if partial is not None:
        add(partial, pl.BlockSpec(memory_space=pltpu.VMEM))
    for place, block, first in whole:
        depth = block.shape[1]
        depth_sum += depth
        add(block, pl.BlockSpec((tile, depth), functools.partial(lambda i, at, skip: (skip + i, 0), skip=first // tile)))
    for _, upper, lower in split:
        depth = upper.shape[1]
        depth_sum += depth
        if resident:
            add(upper, pl.BlockSpec(memory_space=pltpu.VMEM))
            add(lower, pl.BlockSpec(memory_space=pltpu.VMEM))
            continue
        add(upper, pl.BlockSpec((tile, depth), lambda i, at: (jnp.minimum(i, half - 1), 0)))
        add(lower, pl.BlockSpec((tile, depth), lambda i, at: (jnp.maximum(i - half, 0), 0)))
    aliases = {}
    if hidden is not None:
        aliases = {len(operands) + 1: 0}
        add(hidden, pl.BlockSpec(memory_space=pl.ANY))
    counts = ([p for p, _, _ in whole], [p for p, _, _ in split], low is not None, partial is not None)

    def kernel(at_ref, *refs):
        refs = list(refs)
        if hidden is not None:
            refs.pop(-2)
        product_kernel(counts, half, tile, offset, final, resident, at_ref, *refs)

    if final:
        out_shape = jax.ShapeDtypeStruct((lines, rows), jnp.bfloat16)
        out_spec = pl.BlockSpec((lines, tile), lambda i, at: (0, base + i))
    else:
        out_shape = jax.ShapeDtypeStruct((lines, length), jnp.float32)
        out_spec = pl.BlockSpec(memory_space=pltpu.VMEM)
    return pl.pallas_call(
        kernel,
        grid_spec=pltpu.PrefetchScalarGridSpec(num_scalar_prefetch=1, grid=(length // tile,), in_specs=specs, out_specs=out_spec),
        out_shape=out_shape,
        input_output_aliases=aliases,
        compiler_params=pltpu.CompilerParams(vmem_limit_bytes=VMEM_LIMIT),
        cost_estimate=pl.CostEstimate(
            flops=2 * lines * length * depth_sum,
            bytes_accessed=2 * (lines * depth_sum + length * depth_sum + lines * length),
            transcendentals=0,
        ),
    )(at, *operands)


def take_kernel(pieces, source_ref, *refs):
    outs, sems = refs[: len(pieces)], refs[len(pieces)]
    copies = [pltpu.make_async_copy(source_ref.at[pl.ds(start, length)], out, sems.at[j]) for j, ((start, length), out) in enumerate(zip(pieces, outs))]
    for copy in copies:
        copy.start()
    for copy in copies:
        copy.wait()


def take(source, pieces):
    depth = source.shape[1]
    size = sum(length for _, length in pieces) * depth * 2
    return pl.pallas_call(
        functools.partial(take_kernel, pieces),
        in_specs=[pl.BlockSpec(memory_space=pl.ANY)],
        out_specs=[pl.BlockSpec(memory_space=pltpu.VMEM)] * len(pieces),
        out_shape=[jax.ShapeDtypeStruct((length, depth), source.dtype) for _, length in pieces],
        scratch_shapes=[pltpu.SemaphoreType.DMA((len(pieces),))],
        compiler_params=pltpu.CompilerParams(vmem_limit_bytes=VMEM_LIMIT),
        cost_estimate=pl.CostEstimate(flops=size, bytes_accessed=2 * size, transcendentals=0),
    )(source)


def update_kernel(weight_ref, bank_ref, right_ref, out_ref):
    bank = bank_ref[...]
    update = jnp.dot(jnp.concatenate([bank, bank], axis=1), right_ref[...], preferred_element_type=jnp.float32)
    out_ref[...] = (weight_ref[...].astype(jnp.float32) + update).astype(out_ref.dtype)


def updated(weight, bank_out, right_part):
    rows, depth = weight.shape
    width = bank_out.shape[1]
    tile = rows // 4 if rows % 64 == 0 else rows
    return pl.pallas_call(
        update_kernel,
        grid=(rows // tile,),
        in_specs=[
            pl.BlockSpec((tile, depth), lambda i: (i, 0)),
            pl.BlockSpec((tile, width), lambda i: (i, 0)),
            pl.BlockSpec(right_part.shape, lambda i: (0, 0)),
        ],
        out_specs=pl.BlockSpec((tile, depth), lambda i: (i, 0)),
        out_shape=jax.ShapeDtypeStruct(weight.shape, weight.dtype),
        compiler_params=pltpu.CompilerParams(vmem_limit_bytes=12 * 1024 * 1024),
        cost_estimate=pl.CostEstimate(flops=4 * rows * depth * width, bytes_accessed=4 * rows * depth, transcendentals=0),
        name="update",
    )(weight, bank_out, right_part)


def project_kernel(steps, pick_ref, tokens_ref, *refs):
    blocks, out_ref, columns_ref = refs[:steps], refs[steps], refs[steps + 1]
    total = None
    for j, block_ref in enumerate(blocks):
        span = block_ref.shape[0]
        place = pl.ds(pl.multiple_of(pick_ref[j] * span, 128), span)
        term = jnp.dot(tokens_ref[:, place], block_ref[...], preferred_element_type=jnp.float32)
        total = term if total is None else total + term
    out_ref[...] = total
    depth = columns_ref.shape[0]
    for j, block_ref in enumerate(blocks):

        @pl.when((pl.program_id(0) == 0) & (pick_ref[steps] == pick_ref[j]))
        def _(block_ref=block_ref):
            columns_ref[...] = block_ref[pl.ds(pl.multiple_of(pick_ref[steps + 1], 16), depth), :]


def projections(pick, tokens, blocks, depth):
    lines, features = tokens.shape
    width = blocks[0].shape[1]
    tile = 256 if lines % 256 == 0 else lines
    return pl.pallas_call(
        functools.partial(project_kernel, len(blocks)),
        grid_spec=pltpu.PrefetchScalarGridSpec(
            num_scalar_prefetch=1,
            grid=(lines // tile,),
            in_specs=[pl.BlockSpec((tile, features), lambda i, pick: (i, 0))]
            + [pl.BlockSpec(b.shape, lambda i, pick: (0, 0)) for b in blocks],
            out_specs=[pl.BlockSpec((tile, width), lambda i, pick: (i, 0)), pl.BlockSpec((depth, width), lambda i, pick: (0, 0))],
        ),
        out_shape=[jax.ShapeDtypeStruct((lines, width), jnp.float32), jax.ShapeDtypeStruct((depth, width), blocks[0].dtype)],
        compiler_params=pltpu.CompilerParams(vmem_limit_bytes=16 * 1024 * 1024),
        cost_estimate=pl.CostEstimate(flops=2 * lines * features * width, bytes_accessed=2 * lines * features, transcendentals=0),
        name="project",
    )(pick, tokens, *blocks)


def lowrank_kernel(ranks, projected_ref, coupling_ref, seeds_ref, columns_ref, low_ref, right_ref):
    projected, coupling = projected_ref[...], coupling_ref[...]
    members = seeds_ref.shape[0]
    lines, width = projected.shape
    grouped = projected.reshape(members, lines // members, width)
    levels = lax.broadcasted_iota(jnp.int32, (members, 1, width), 2)
    mixed = None
    for k in range(ranks):
        feature_hit = (seeds_ref[:, 1:2, k : k + 1] == levels).astype(jnp.float32)
        hidden_hit = (seeds_ref[:, 0:1, k : k + 1] == levels).astype(jnp.float32)
        term = jnp.sum(grouped * feature_hit, axis=2, keepdims=True) * hidden_hit
        mixed = term if mixed is None else mixed + term
    low_ref[:, :width] = (NOISE_SCALE * mixed).reshape(lines, width).astype(low_ref.dtype)
    shift = lax.dot_general(projected, coupling, DIMS, precision=lax.Precision.HIGHEST, preferred_element_type=jnp.float32)
    low_ref[:, width:] = shift.astype(low_ref.dtype)
    right = lax.dot_general(coupling, columns_ref[...].astype(jnp.float32), DIMS, precision=lax.Precision.HIGHEST, preferred_element_type=jnp.float32)
    upper = right.astype(right_ref.dtype)
    right_ref[:width, :] = upper
    right_ref[width:, :] = (right - upper.astype(jnp.float32)).astype(right_ref.dtype)


def lowrank(projected, coupling, seeds, columns):
    lines, width = projected.shape
    depth = columns.shape[0]
    return pl.pallas_call(
        functools.partial(lowrank_kernel, seeds.shape[2]),
        out_shape=[jax.ShapeDtypeStruct((lines, 2 * width), jnp.bfloat16), jax.ShapeDtypeStruct((2 * width, depth), jnp.bfloat16)],
        compiler_params=pltpu.CompilerParams(vmem_limit_bytes=16 * 1024 * 1024),
        cost_estimate=pl.CostEstimate(flops=20 * lines * width * width, bytes_accessed=8 * lines * width, transcendentals=0),
        name="lowrank",
    )(projected, coupling, seeds, columns)


def shards(tokens, weight, bank_in, bank_out, fitness, past_seeds, new_seeds):
    members = fitness.shape[0]
    pops, lanes = lax.axis_size("pop"), lax.axis_size("row")
    me, lane = lax.axis_index("pop"), lax.axis_index("row")
    overall = members * pops
    width = bank_out.shape[1]
    features = tokens.shape[2]
    rows, depth = weight.shape
    flat_tokens = tokens.reshape(members * tokens.shape[1], features)
    tile = 256
    chunks = cut(rows, tile)
    planned = pops == 8 and chunks is not None

    def flip(block, mask):
        return lax.ppermute(block, "pop", [(i, i ^ mask) for i in range(pops)])

    at = (me ^ jnp.arange(pops, dtype=jnp.int32)).astype(jnp.int32)
    packed = jnp.concatenate([fitness[:, None], past_seeds.reshape(members, -1)], axis=1)

    held = {}
    if planned:
        core, one, two = 1, 2, 4
        own = take(weight, chunks[:1]) + take(weight, chunks[1:])
        for c, piece in enumerate(own):
            held[c, one] = flip(piece, one)
            held[c, two] = flip(piece, two)
        partner = flip(weight, core)
        for c in range(len(chunks)):
            held[c, one | two] = flip(held[c, two], one) if c % 2 else flip(held[c, one], two)
            for mask in (one, two, one | two):
                held[c, mask | core] = flip(held[c, mask], core)
        both = jnp.concatenate([packed, flip(packed, core)], axis=0)
        side = lax.ppermute(both, "pop", [(i, i ^ (two if i & core else one)) for i in range(pops)])
        across = lax.ppermute(both, "pop", [(i, i ^ (one | two)) for i in range(0, pops, 2)])
        mine = jnp.concatenate([side, across], axis=0)
        theirs = flip(mine, core)
        rest = both.shape[0]
        everyone = jnp.concatenate([both, side, theirs[:rest], across + theirs[rest:]], axis=0)
    else:
        everyone = lax.all_gather(packed, "pop", axis=0, tiled=True)

    every_fitness = everyone[:, 0]
    every_seeds = everyone[:, 1:].reshape((overall,) + past_seeds.shape[1:])
    lower_count = jnp.sum((every_fitness[None, :] < every_fitness[:, None]).astype(jnp.float32), axis=1)
    equal_count = jnp.sum((every_fitness[None, :] == every_fitness[:, None]).astype(jnp.float32), axis=1)
    centered = (lower_count + 0.5 * (equal_count - 1.0)) / (overall - 1.0) - 0.5
    out_hits, in_hits = one_hots(every_seeds, width)
    scaled = (STEP_SCALE * centered)[:, None, None] * out_hits
    coupling = lax.dot_general(
        scaled.reshape(-1, width),
        in_hits.reshape(-1, width),
        (((0,), (0,)), ((), ())),
        precision=lax.Precision.HIGHEST,
    )

    span = bank_in.shape[0]
    banks = [bank_in]
    for step in range(1, lanes):
        banks.append(lax.ppermute(bank_in, "row", [(i, (i - step) % lanes) for i in range(lanes)]))
    if span % depth == 0:
        ring = (lane + jnp.arange(lanes, dtype=jnp.int32)) % lanes
        pick = jnp.concatenate([ring, jnp.stack([me * depth // span, me * depth % span])]).astype(jnp.int32)
        projected, columns = projections(pick, flat_tokens, banks, depth)
    else:
        full_in = jnp.zeros((features, width), bank_in.dtype)
        for step, block in enumerate(banks):
            full_in = lax.dynamic_update_slice_in_dim(full_in, block, ((lane + step) % lanes) * span, 0)
        projected = jnp.dot(flat_tokens, full_in, preferred_element_type=jnp.float32)
        columns = lax.dynamic_slice_in_dim(full_in, me * depth, depth, 0)
    low, right_part = lowrank(projected, coupling, new_seeds, columns)
    new_weight = updated(weight, bank_out, right_part)

    if planned:
        hidden = None

        def pair(c, upper, lower):
            return [((u, l), held[c, u], held[c + 1, l]) for u, l in zip(upper, lower)]

        def wide(c):
            start = chunks[c][0]
            return dict(start=start, length=2 * chunks[c][1], tile=tile, rows=rows), [(0, weight, start), (core, partner, start)]

        sizes, own = wide(0)
        partial = product(at, flat_tokens, **sizes, whole=own, split=pair(0, (2, 3, 4, 5), (2, 3, 4, 5)), low=low, bank_out=bank_out)
        for c in (0, 1):
            start, length = chunks[c]
            far = [(m, held[c, m], 0) for m in (6, 7)]
            hidden = product(at, flat_tokens, start, length, tile, rows, whole=far, partial=partial, offset=start, final=True, hidden=hidden)
        sizes, own = wide(2)
        partial = product(at, flat_tokens, **sizes, whole=own, split=pair(2, (2, 3), (4, 5)), low=low, bank_out=bank_out)
        partial = product(at, flat_tokens, **sizes, split=pair(2, (4, 5), (2, 3)), partial=partial)
        hidden = product(at, flat_tokens, **sizes, split=pair(2, (6, 7), (6, 7)), partial=partial, final=True, hidden=hidden, resident=True)
    else:
        blocks = {0: weight}
        for bit in range((pops - 1).bit_length()):
            if pops & (pops - 1) == 0:
                blocks.update({m | 1 << bit: flip(b, 1 << bit) for m, b in list(blocks.items())})
        if len(blocks) == pops:
            full = jnp.zeros((rows, features), weight.dtype)
            for m, b in blocks.items():
                full = lax.dynamic_update_slice_in_dim(full, b, (me ^ m) * depth, 1)
        else:
            full = lax.all_gather(weight, "pop", axis=1, tiled=True)
        hidden = lax.dot_general(flat_tokens, full, DIMS, preferred_element_type=jnp.float32)
        hidden += lax.dot_general(low, jnp.concatenate([bank_out, bank_out], axis=1), DIMS, preferred_element_type=jnp.float32)
        hidden = hidden.astype(jnp.bfloat16)
    return (hidden.reshape(members, tokens.shape[1], rows), new_weight)


def solution(mesh):
    placed = (
        P("pop", None, None),
        P("row", "pop"),
        P("row", None),
        P("row", None),
        P("pop"),
        P("pop", None, None),
        P("pop", None, None),
    )
    return jax.shard_map(
        shards,
        mesh=mesh,
        in_specs=placed,
        out_specs=(P("pop", None, "row"), P("row", "pop")),
        check_vma=False,
    )
```

time: 272 us -> 195 us (0.72)
  waiting for transfers between devices: 195 us -> 97.4 us
  Pallas kernels: 0 us -> 57.5 us
  matrix products: 47.6 us -> 1.29 us
  starting transfers between devices: 0.12 us -> 26.1 us
  between operations: 16.2 us -> 1.03 us
  blocking collectives: 9.49 us -> 0 us
  local copies, waits for them, and re-layouts: 3.23 us -> 8.93 us
    all_gather x2 -> x0, waiting for transfers between devices: 142 us -> none  [the longest x1 142 us: shards(): lax.all_gather(new_weight, 'pop', axis=1, tiled=True)]
    ppermute x0 -> x32, waiting for transfers between devices: none -> 97.4 us  [the longest x27 82 us: flip(): return lax.ppermute(block, 'pop', [(i, i ^ mask) for i in range(pops)])]
    pallas_call x0 -> x11, Pallas kernels: none -> 57.5 us  [the longest x6 43.8 us: product(): pl.pallas_call(kernel, grid_spec=pltpu.PrefetchScalarGridSpec(num_scalar_...]
    psum x1 -> x0, waiting for transfers between devices: 52.4 us -> none  [shards(): coupling = lax.psum(local_coupling, 'pop')]
    dot_general x6 -> x1, matrix products: 47.6 us -> 1.29 us  [shards(): lax.dot_general(scaled.reshape(-1, width), in_hits.reshape(-1, width), ((...]
    ppermute x0 -> x32, starting transfers between devices: none -> 26.1 us  [the longest x27 12.6 us: flip(): return lax.ppermute(block, 'pop', [(i, i ^ mask) for i in range(pops)])]
    unnamed x1 -> x0, blocking collectives: 9.49 us -> none
    unnamed x7 -> x53, local copies, waits for them, and re-layouts: 2.19 us -> 8.12 us
  transfers between devices with their start and end apart: 3 -> 32, of which waited for: 2 -> 8; matrix products, arithmetic and copies ran while one was open for 3% -> 2% of each run, Pallas kernels for 0% -> 27%
where the time goes in v1:
time: 195 us
  waiting for transfers between devices  97.4 us (50%)
  Pallas kernels  57.5 us (29%)
  starting transfers between devices  26.1 us (13%)
  local copies, waits for them, and re-layouts  8.93 us (5%)
  other arithmetic  2.53 us (1%)
    ppermute x27, waiting for transfers between devices, flip(): return lax.ppermute(block, 'pop', [(i, i ^ mask) for i in range(pops)])  82 us
    pallas_call x6, Pallas kernels, product(): pl.pallas_call(kernel, grid_spec=pltpu.PrefetchScalarGridSpec(num_scalar_...  43.8 us
    ppermute x3, waiting for transfers between devices, shards(): lax.ppermute(bank_in, 'row', [(i, (i - step) % lanes) for i in range(lane...  15.4 us
    ppermute x27, starting transfers between devices, flip(): return lax.ppermute(block, 'pop', [(i, i ^ mask) for i in range(pops)])  12.6 us
    unnamed x53, local copies, waits for them, and re-layouts  8.12 us
    ppermute x3, starting transfers between devices, shards(): lax.ppermute(bank_in, 'row', [(i, (i - step) % lanes) for i in range(lane...  7.3 us
    pallas_call x1, Pallas kernels, updated(): pl.pallas_call(update_kernel, grid=(rows // tile,), in_specs=[pl.BlockSpe...  5.42 us
  transfers between devices with their start and end apart: 32, of which 8 were waited for; matrix products, arithmetic and copies ran while one was open for 2% of the time, Pallas kernels for 27%

profile of v1, /device:TPU:0, one launch (start us, length us, event | category | flops | bytes accessed | tf_op | source)
XLA Modules:
  0.0 194.8 jit_solution(5868760885805159902)
XLA Ops:
  0.6 0.7 pad_add_fusion.1
  1.3 0.5 collective-permute-start.3
  1.8 0.8 collective-permute-done.3
  2.7 0.8 pad_add_fusion.2
  3.4 2.8 %collective-permute-start.4 = (s32[96,17]{0,1:T(8,128)S(1)}, s32[96,17]{0,1:T(8,128)S(1)}, u32[]{:S(2)}, u32[]{:S(2)}) collective-permute-start(s32[96,17]{0,1:T(8,128)S(1)} %pad_add_fusion.2), channel_id=1, source_target_pairs={{0,8},{4,20},{8,0},{12,28},{16,24},{20,4},{24,16},{28,12},{1,9},{5... | collective-permute-start | bytes 19592 | tf_op jit(solution)/shard_map/ppermute | solution.py:299
  6.3 3.4 %collective-permute-start.5 = (s32[96,17]{0,1:T(8,128)S(1)}, s32[96,17]{0,1:T(8,128)S(1)}, u32[]{:S(2)}, u32[]{:S(2)}) collective-permute-start(s32[96,17]{0,1:T(8,128)S(1)} %pad_add_fusion.2), channel_id=1, source_target_pairs={{0,24},{8,16},{16,8},{24,0},{1,25},{9,17},{17,9},{25,1},{2,26},{10... | collective-permute-start | bytes 19592 | tf_op jit(solution)/shard_map/ppermute | solution.py:300
  9.7 3.7 %collective-permute-start = (bf16[1024,128]{1,0:T(8,128)(2,1)}, bf16[1024,128]{1,0:T(8,128)(2,1)S(1)}, u32[]{:S(2)}, u32[]{:S(2)}) collective-permute-start(bf16[1024,128]{1,0:T(8,128)(2,1)} %refs_0_.1), channel_id=1, source_target_pairs={{0,3},{1,0},{2,1},{3,2},{4,7},{5,4},{6,5},{7,6},{8,11},{9,8},{10,9... | collective-permute-start | bytes 786440 | tf_op jit(solution)/shard_map/ppermute | solution.py:325
  13.3 0.1 pad_add_fusion
  13.4 0.0 collective-permute-start.6
  13.4 1.7 shard_map.86
  15.1 1.6 collective-permute-start.8
  16.6 0.5 collective-permute-start.9
  17.2 2.1 %collective-permute-start.1 = (bf16[1024,128]{1,0:T(8,128)(2,1)S(1)}, bf16[1024,128]{1,0:T(8,128)(2,1)S(1)}, u32[]{:S(2)}, u32[]{:S(2)}) collective-permute-start(bf16[1024,128]{1,0:T(8,128)(2,1)S(1)} %copy-done.14), channel_id=1, source_target_pairs={{0,2},{1,3},{2,0},{3,1},{4,6},{5,7},{6,4},{7,5},{8,10},{9,11},{10,... | collective-permute-start | bytes 786440 | tf_op jit(solution)/shard_map/ppermute | solution.py:325
  19.2 1.6 collective-permute-start.2
  20.8 0.7 copy-done.15
  21.5 0.5 collective-permute-start.12
  22.0 15.4 %collective-permute-done.1.refs_2_ = bf16[1024,128]{1,0:T(8,128)(2,1)S(1)} collective-permute-done((bf16[1024,128]{1,0:T(8,128)(2,1)S(1)}, bf16[1024,128]{1,0:T(8,128)(2,1)S(1)}, u32[]{:S(2)}, u32[]{:S(2)}) %collective-permute-start.1) | collective-permute-done | bytes 262176 | tf_op jit(solution)/shard_map/ppermute | solution.py:325
  37.4 0.7 copy-done.17
  38.1 1.0 collective-permute-start.25
  39.1 0.7 copy-done.19
  39.8 1.1 collective-permute-start.21
  40.9 1.0 collective-permute-start.13
  41.9 0.8 collective-permute-done.12.refs_2_
  42.7 38.8 %collective-permute-done.13.refs_3_ = bf16[512,512]{1,0:T(8,128)(2,1)S(1)} collective-permute-done((bf16[512,512]{1,0:T(8,128)(2,1)S(1)}, bf16[512,512]{1,0:T(8,128)(2,1)S(1)}, u32[]{:S(2)}, u32[]{:S(2)}) %collective-permute-start.13) | collective-permute-done | bytes 524320 | tf_op jit(solution)/shard_map/ppermute | solution.py:281
  81.5 0.8 copy-done.10
  82.3 0.5 collective-permute-start.14
  82.8 1.3 shard_map.89
  84.2 0.8 copy-done.12
  85.0 0.6 collective-permute-start.20
  85.6 0.8 copy-done.8
  86.4 0.4 collective-permute-start.24
  86.8 0.5 collective-permute-start.23
  87.3 0.1 copy.12.seeds_ref
  87.4 0.1 pad_add_fusion.3.pick_ref
  87.5 28.3 %collective-permute-done.20.refs_5_ = bf16[1280,512]{1,0:T(8,128)(2,1)} collective-permute-done((bf16[1280,512]{1,0:T(8,128)(2,1)S(1)}, bf16[1280,512]{1,0:T(8,128)(2,1)}, u32[]{:S(2)}, u32[]{:S(2)}) %collective-permute-start.20) | collective-permute-done | bytes 1310752 | tf_op jit(solution)/shard_map/ppermute | solution.py:281
  115.8 1.0 collective-permute-done.24.refs_9_
  116.8 0.4 collective-permute-start.30
  117.2 0.7 copy-done.21
  117.9 1.4 collective-permute-start.28
  119.3 0.6 slice_add_fusion
  119.9 0.8 concatenate.20
  120.7 0.0 copy-start.16
  120.7 0.3 convert_reduce_fusion
  121.0 1.3 fusion.2.coupling_ref
  122.3 0.0 copy-start
  122.4 2.8 %copy-done = bf16[48,16,4096]{2,1,0:T(8,128)(2,1)S(1)} copy-done((bf16[48,16,4096]{2,1,0:T(8,128)(2,1)S(1)}, bf16[48,16,4096]{2,1,0:T(8,128)(2,1)}, u32[]{:S(2)}) %copy-start) | copy-done | bytes 6291480
  125.1 2.9 %project.1 = (f32[768,128]{1,0:T(8,128)S(1)}, bf16[512,128]{1,0:T(8,128)(2,1)S(1)}) custom-call(s32[6]{0:T(128)S(1)} %pad_add_fusion.3.pick_ref, bf16[768,4096]{1,0:T(8,128)(2,1)S(1)} %bitcast.14, bf16[1024,128]{1,0:T(8,128)(2,1)S(1)} %copy-done.14, bf16[1024,128]{1,0:T(8,128)(2,1)S(1)} %copy-done.16, bf16[1024,128]{1,0:T(8,128)(2,1)S(1)} %copy-done.18, ...), custom_call_target="tpu_custom_call" | custom-call | flops 805306368 | bytes 6291456 | tf_op jit(solution)/shard_map/project/pallas_call | solution.py:218
  128.1 2.3 %lowrank.1 = (bf16[768,256]{1,0:T(8,128)(2,1)S(1)}, bf16[256,512]{1,0:T(8,128)(2,1)S(1)}) custom-call(f32[768,128]{1,0:T(8,128)S(1)} %get-tuple-element.9.projected_ref, f32[128,128]{1,0:T(8,128)S(1)} %fusion.2.coupling_ref, s32[48,2,8]{2,1,0:T(2,128)S(1)} %copy.12.seeds_ref, bf16[512,128]{1,0:T(8,128)(2,1)S(1)} %get-tuple-element.10.columns_ref), custom_call_target="tpu_custom_call" | custom-call | flops 251658240 | bytes 786432 | tf_op jit(solution)/shard_map/lowrank/pallas_call | solution.py:258
  130.5 0.0 slice-start.1
  130.5 0.0 copy-start.22
  130.5 5.4 %update.1 = bf16[3584,512]{1,0:T(8,128)(2,1)} custom-call(bf16[3584,512]{1,0:T(8,128)(2,1)} %weight_ref.1, bf16[3584,128]{1,0:T(8,128)(2,1)S(1)} %copy-done.1, bf16[256,512]{1,0:T(8,128)(2,1)S(1)} %get-tuple-element.15.right_ref), custom_call_target="tpu_custom_call" | custom-call | flops 939524096 | bytes 7340032 | tf_op jit(solution)/shard_map/update/pallas_call | solution.py:181
  135.9 1.0 collective-permute-start.16
  136.9 0.6 collective-permute-start.17
  137.5 11.1 %collective-permute-done.30.refs_2_ = bf16[1280,512]{1,0:T(8,128)(2,1)S(1)} collective-permute-done((bf16[1280,512]{1,0:T(8,128)(2,1)}, bf16[1280,512]{1,0:T(8,128)(2,1)S(1)}, u32[]{:S(2)}, u32[]{:S(2)}) %collective-permute-start.30) | collective-permute-done | bytes 1310752 | tf_op jit(solution)/shard_map/ppermute | solution.py:281
  148.7 1.1 collective-permute-done.28.refs_2_
  149.7 0.5 collective-permute-start.29
  150.3 20.1 %shard_map.90.refs_1_ = f32[768,2560]{1,0:T(8,128)S(1)} custom-call(s32[8]{0:T(128)S(1)} %iota_xor_fusion.at_ref, bf16[768,4096]{1,0:T(8,128)(2,1)S(1)} %bitcast.17, bf16[768,256]{1,0:T(8,128)(2,1)S(1)} %get-tuple-element.11.refs_1_, bf16[3584,128]{1,0:T(8,128)(2,1)S(1)} %copy-done.1, bf16[3584,512]{1,0:T(8,128)(2,1)} %weight_ref.1, ...), custom_call_target="tpu_custom_call" | custom-call | flops 12079595520 | bytes 24379392 | tf_op jit(solution)/shard_map/pallas_call | solution.py:134
  170.5 7.0 %shard_map.87.refs_1_ = f32[768,1024]{1,0:T(8,128)S(1)} custom-call(s32[8]{0:T(128)S(1)} %iota_xor_fusion.at_ref, bf16[768,4096]{1,0:T(8,128)(2,1)S(1)} %bitcast.18, bf16[768,256]{1,0:T(8,128)(2,1)S(1)} %get-tuple-element.11.refs_1_, bf16[3584,128]{1,0:T(8,128)(2,1)S(1)} %copy-done.1, bf16[3584,512]{1,0:T(8,128)(2,1)} %weight_ref.1, ...), custom_call_target="tpu_custom_call" | custom-call | flops 3221225472 | bytes 8912896 | tf_op jit(solution)/shard_map/pallas_call | solution.py:134
  177.5 0.1 collective-permute-start.18
  177.6 0.5 collective-permute-start.19
  178.1 3.3 %shard_map.88.refs_1_ = f32[768,1024]{1,0:T(8,128)S(1)} custom-call(s32[8]{0:T(128)S(1)} %iota_xor_fusion.at_ref, bf16[768,4096]{1,0:T(8,128)(2,1)S(1)} %bitcast.19, f32[768,1024]{1,0:T(8,128)S(1)} %shard_map.87.refs_1_, bf16[512,512]{1,0:T(8,128)(2,1)S(1)} %copy-done.5, bf16[512,512]{1,0:T(8,128)(2,1)S(1)} %copy-done.7, bf16[512,512]{1,0:T(8,128)(2,1)S(1)} %copy-done.9, ...), custom_call_target="tpu_custom_call" | custom-call | flops 1610612736 | bytes 5242880 | tf_op jit(solution)/shard_map/pallas_call | solution.py:134
  181.4 4.6 %shard_map.91.refs_4_ = bf16[768,3584]{1,0:T(8,128)(2,1)} custom-call(s32[8]{0:T(128)S(1)} %iota_xor_fusion.at_ref, bf16[768,4096]{1,0:T(8,128)(2,1)S(1)} %bitcast.20, f32[768,2560]{1,0:T(8,128)S(1)} %shard_map.90.refs_1_, bf16[1280,512]{1,0:T(8,128)(2,1)S(1)} %collective-permute-done.30.refs_2_, bf16[1280,512]{1,0:T(8,128)(2,1)S(1)} %collective-permute-done.31.refs_3_), custom_call_target="tpu_custom_call" | custom-call | flops 2013265920 | bytes 6160384 | tf_op jit(solution)/shard_map/pallas_call | solution.py:134
  186.0 4.6 %shard_map.92.refs_6_ = bf16[768,3584]{1,0:T(8,128)(2,1)} custom-call(s32[8]{0:T(128)S(1)} %iota_xor_fusion.at_ref, bf16[768,4096]{1,0:T(8,128)(2,1)S(1)} %bitcast.21, f32[768,2560]{1,0:T(8,128)S(1)} %shard_map.90.refs_1_, bf16[1280,512]{1,0:T(8,128)(2,1)S(1)} %collective-permute-done.28.refs_2_, ...), custom_call_target="tpu_custom_call", output_to_operand_aliasing={{}: (5, {})} | custom-call | flops 2013265920 | bytes 6160384 | tf_op jit(solution)/shard_map/pallas_call | solution.py:134
  190.7 4.1 %shard_map.93 = bf16[768,3584]{1,0:T(8,128)(2,1)} custom-call(s32[8]{0:T(128)S(1)} %iota_xor_fusion.at_ref, bf16[768,4096]{1,0:T(8,128)(2,1)S(1)} %bitcast.22, f32[768,1024]{1,0:T(8,128)S(1)} %shard_map.88.refs_1_, bf16[512,512]{1,0:T(8,128)(2,1)S(1)} %collective-permute-done.16.refs_2_, ...), custom_call_target="tpu_custom_call", output_to_operand_aliasing={{}: (7, {})} | custom-call | flops 1610612736 | bytes 5242880 | tf_op jit(solution)/shard_map/pallas_call | solution.py:134
  (79 shorter events, 0.2 us)
Async XLA Ops:
  1.3 1.3 collective-permute-start.3
  3.4 9.9 %collective-permute-start.4 = (s32[96,17]{0,1:T(8,128)S(1)}, s32[96,17]{0,1:T(8,128)S(1)}, u32[]{:S(2)}, u32[]{:S(2)}) collective-permute-start(s32[96,17]{0,1:T(8,128)S(1)} %pad_add_fusion.2), channel_id=1, source_target_pairs={{0,8},{4,20},{8,0},{12,28},{16,24},{20,4},{24,16},{28,12},{1,9},{5... | collective-permute-start | bytes 19592 | tf_op jit(solution)/shard_map/ppermute | solution.py:299
  6.3 7.1 %collective-permute-start.5 = (s32[96,17]{0,1:T(8,128)S(1)}, s32[96,17]{0,1:T(8,128)S(1)}, u32[]{:S(2)}, u32[]{:S(2)}) collective-permute-start(s32[96,17]{0,1:T(8,128)S(1)} %pad_add_fusion.2), channel_id=1, source_target_pairs={{0,24},{8,16},{16,8},{24,0},{1,25},{9,17},{17,9},{25,1},{2,26},{10... | collective-permute-start | bytes 19592 | tf_op jit(solution)/shard_map/ppermute | solution.py:300
  9.7 11.2 %collective-permute-start = (bf16[1024,128]{1,0:T(8,128)(2,1)}, bf16[1024,128]{1,0:T(8,128)(2,1)S(1)}, u32[]{:S(2)}, u32[]{:S(2)}) collective-permute-start(bf16[1024,128]{1,0:T(8,128)(2,1)} %refs_0_.1), channel_id=1, source_target_pairs={{0,3},{1,0},{2,1},{3,2},{4,7},{5,4},{6,5},{7,6},{8,11},{9,8},{10,9... | collective-permute-start | bytes 786440 | tf_op jit(solution)/shard_map/ppermute | solution.py:325
  13.4 3.8 %copy-start.14 = (bf16[1024,128]{1,0:T(8,128)(2,1)S(1)}, bf16[1024,128]{1,0:T(8,128)(2,1)}, u32[]{:S(2)}) copy-start(bf16[1024,128]{1,0:T(8,128)(2,1)} %refs_0_.1) | copy-start | bytes 786436
  13.4 5.8 %collective-permute-start.6 = (s32[192,17]{0,1:T(8,128)S(1)}, s32[192,17]{0,1:T(8,128)S(1)}, u32[]{:S(2)}, u32[]{:S(2)}) collective-permute-start(s32[192,17]{0,1:T(8,128)S(1)} %pad_add_fusion), channel_id=1, source_target_pairs={{0,4},{4,0},{8,12},{12,8},{16,20},{20,16},{24,28},{28,24},{1,5},{5... | collective-permute-start | bytes 39176 | tf_op jit(solution)/shard_map/ppermute | solution.py:281
  15.1 25.8 %collective-permute-start.8 = (bf16[512,512]{1,0:T(8,128)(2,1)S(1)}, bf16[512,512]{1,0:T(8,128)(2,1)S(1)}, u32[]{:S(2)}, u32[]{:S(2)}) collective-permute-start(bf16[512,512]{1,0:T(8,128)(2,1)S(1)} %get-tuple-element.12), channel_id=1, source_target_pairs={{0,8},{4,12},{8,0},{12,4},{16,24},{20,28},{24,16},{28,20},{1,9},{5... | collective-permute-start | bytes 1572872 | tf_op jit(solution)/shard_map/ppermute | solution.py:281
  16.6 25.2 %collective-permute-start.9 = (bf16[512,512]{1,0:T(8,128)(2,1)S(1)}, bf16[512,512]{1,0:T(8,128)(2,1)S(1)}, u32[]{:S(2)}, u32[]{:S(2)}) collective-permute-start(bf16[512,512]{1,0:T(8,128)(2,1)S(1)} %get-tuple-element.13), channel_id=1, source_target_pairs={{0,16},{4,20},{8,24},{12,28},{16,0},{20,4},{24,8},{28,12},{1,17},{... | collective-permute-start | bytes 1572872 | tf_op jit(solution)/shard_map/ppermute | solution.py:281
  17.2 20.2 %collective-permute-start.1 = (bf16[1024,128]{1,0:T(8,128)(2,1)S(1)}, bf16[1024,128]{1,0:T(8,128)(2,1)S(1)}, u32[]{:S(2)}, u32[]{:S(2)}) collective-permute-start(bf16[1024,128]{1,0:T(8,128)(2,1)S(1)} %copy-done.14), channel_id=1, source_target_pairs={{0,2},{1,3},{2,0},{3,1},{4,6},{5,7},{6,4},{7,5},{8,10},{9,11},{10,... | collective-permute-start | bytes 786440 | tf_op jit(solution)/shard_map/ppermute | solution.py:325
  19.2 19.9 %collective-permute-start.2 = (bf16[1024,128]{1,0:T(8,128)(2,1)S(1)}, bf16[1024,128]{1,0:T(8,128)(2,1)S(1)}, u32[]{:S(2)}, u32[]{:S(2)}) collective-permute-start(bf16[1024,128]{1,0:T(8,128)(2,1)S(1)} %copy-done.14), channel_id=1, source_target_pairs={{0,1},{1,2},{2,3},{3,0},{4,5},{5,6},{6,7},{7,4},{8,9},{9,10},{10,1... | collective-permute-start | bytes 786440 | tf_op jit(solution)/shard_map/ppermute | solution.py:325
  20.8 0.7 copy-start.15
  21.5 21.2 %collective-permute-start.12 = (bf16[512,512]{1,0:T(8,128)(2,1)S(1)}, bf16[512,512]{1,0:T(8,128)(2,1)S(1)}, u32[]{:S(2)}, u32[]{:S(2)}) collective-permute-start(bf16[512,512]{1,0:T(8,128)(2,1)S(1)} %get-tuple-element.12), channel_id=1, source_target_pairs={{0,16},{4,20},{8,24},{12,28},{16,0},{20,4},{24,8},{28,12},{1,17},{... | collective-permute-start | bytes 1572872 | tf_op jit(solution)/shard_map/ppermute | solution.py:281
  37.4 0.7 copy-start.17
  38.1 49.2 %copy-start.23 = (s32[48,2,8]{0,2,1:T(8,128)S(1)}, s32[48,2,8]{0,2,1:T(8,128)}, u32[]{:S(2)}) copy-start(s32[48,2,8]{0,2,1:T(8,128)} %param.13) | copy-start | bytes 9220
  38.1 48.7 %collective-permute-start.25 = (bf16[1280,512]{1,0:T(8,128)(2,1)S(1)}, bf16[1280,512]{1,0:T(8,128)(2,1)}, u32[]{:S(2)}, u32[]{:S(2)}) collective-permute-start(bf16[1280,512]{1,0:T(8,128)(2,1)S(1)} %get-tuple-element.14), channel_id=1, source_target_pairs={{0,16},{4,20},{8,24},{12,28},{16,0},{20,4},{24,8},{28,12},{1,17},{... | collective-permute-start | bytes 3932168 | tf_op jit(solution)/shard_map/ppermute | solution.py:281
  39.1 0.7 copy-start.19
  39.8 47.0 %collective-permute-start.21 = (bf16[1280,512]{1,0:T(8,128)(2,1)S(1)}, bf16[1280,512]{1,0:T(8,128)(2,1)}, u32[]{:S(2)}, u32[]{:S(2)}) collective-permute-start(bf16[1280,512]{1,0:T(8,128)(2,1)S(1)} %get-tuple-element.14), channel_id=1, source_target_pairs={{0,8},{4,12},{8,0},{12,4},{16,24},{20,28},{24,16},{28,20},{1,9},{5... | collective-permute-start | bytes 3932168 | tf_op jit(solution)/shard_map/ppermute | solution.py:281
  40.9 40.6 %copy-start.2 = (bf16[512,512]{1,0:T(8,128)(2,1)}, bf16[512,512]{1,0:T(8,128)(2,1)S(1)}, u32[]{:S(2)}) copy-start(bf16[512,512]{1,0:T(8,128)(2,1)S(1)} %collective-permute-done.8.refs_5_) | copy-start | bytes 1572868
  40.9 40.6 %collective-permute-start.13 = (bf16[512,512]{1,0:T(8,128)(2,1)S(1)}, bf16[512,512]{1,0:T(8,128)(2,1)S(1)}, u32[]{:S(2)}, u32[]{:S(2)}) collective-permute-start(bf16[512,512]{1,0:T(8,128)(2,1)S(1)} %get-tuple-element.13), channel_id=1, source_target_pairs={{0,8},{4,12},{8,0},{12,4},{16,24},{20,28},{24,16},{28,20},{1,9},{5... | collective-permute-start | bytes 1572872 | tf_op jit(solution)/shard_map/ppermute | solution.py:281
  41.9 39.6 %collective-permute-start.10 = (bf16[512,512]{1,0:T(8,128)(2,1)S(1)}, bf16[512,512]{1,0:T(8,128)(2,1)S(1)}, u32[]{:S(2)}, u32[]{:S(2)}) collective-permute-start(bf16[512,512]{1,0:T(8,128)(2,1)S(1)} %collective-permute-done.8.refs_5_), channel_id=1, source_target_pairs={{0,4},{4,0},{8,12},{12,8},{16,20},{20,16},{24,28},{28,24},{1,5},{5... | collective-permute-start | bytes 1572872 | tf_op jit(solution)/shard_map/ppermute | solution.py:281
  42.7 41.4 %copy-start.4 = (bf16[512,512]{1,0:T(8,128)(2,1)}, bf16[512,512]{1,0:T(8,128)(2,1)S(1)}, u32[]{:S(2)}) copy-start(bf16[512,512]{1,0:T(8,128)(2,1)S(1)} %collective-permute-done.12.refs_2_) | copy-start | bytes 1572868
  42.7 107.1 %collective-permute-start.7 = (bf16[3584,512]{1,0:T(8,128)(2,1)}, bf16[3584,512]{1,0:T(8,128)(2,1)}, u32[]{:S(2)}, u32[]{:S(2)}) collective-permute-start(bf16[3584,512]{1,0:T(8,128)(2,1)} %weight_ref.1), channel_id=1, source_target_pairs={{0,4},{4,0},{8,12},{12,8},{16,20},{20,16},{24,28},{28,24},{1,5},{5... | collective-permute-start | bytes 11010056 | tf_op jit(solution)/shard_map/ppermute | solution.py:281
  81.5 2.7 %copy-start.6 = (bf16[512,512]{1,0:T(8,128)(2,1)}, bf16[512,512]{1,0:T(8,128)(2,1)S(1)}, u32[]{:S(2)}) copy-start(bf16[512,512]{1,0:T(8,128)(2,1)S(1)} %collective-permute-done.13.refs_3_) | copy-start | bytes 1572868
  81.5 2.7 %collective-permute-start.11 = (bf16[512,512]{1,0:T(8,128)(2,1)S(1)}, bf16[512,512]{1,0:T(8,128)(2,1)S(1)}, u32[]{:S(2)}, u32[]{:S(2)}) collective-permute-start(bf16[512,512]{1,0:T(8,128)(2,1)S(1)} %collective-permute-done.9.refs_6_), channel_id=1, source_target_pairs={{0,4},{4,0},{8,12},{12,8},{16,20},{20,16},{24,28},{28,24},{1,5},{5... | collective-permute-start | bytes 1572872 | tf_op jit(solution)/shard_map/ppermute | solution.py:281
  81.5 0.8 copy-start.10
  82.3 3.3 %collective-permute-start.14 = (bf16[512,512]{1,0:T(8,128)(2,1)S(1)}, bf16[512,512]{1,0:T(8,128)(2,1)S(1)}, u32[]{:S(2)}, u32[]{:S(2)}) collective-permute-start(bf16[512,512]{1,0:T(8,128)(2,1)S(1)} %collective-permute-done.12.refs_2_), channel_id=1, source_target_pairs={{0,4},{4,0},{8,12},{12,8},{16,20},{20,16},{24,28},{28,24},{1,5},{5... | collective-permute-start | bytes 1572872 | tf_op jit(solution)/shard_map/ppermute | solution.py:281
  84.2 0.8 copy-start.12
  85.0 30.8 %collective-permute-start.20 = (bf16[1280,512]{1,0:T(8,128)(2,1)S(1)}, bf16[1280,512]{1,0:T(8,128)(2,1)}, u32[]{:S(2)}, u32[]{:S(2)}) collective-permute-start(bf16[1280,512]{1,0:T(8,128)(2,1)S(1)} %shard_map.89), channel_id=1, source_target_pairs={{0,8},{4,12},{8,0},{12,4},{16,24},{20,28},{24,16},{28,20},{1,9},{5... | collective-permute-start | bytes 3932168 | tf_op jit(solution)/shard_map/ppermute | solution.py:281
  85.6 0.8 copy-start.8
  86.4 30.4 %collective-permute-start.24 = (bf16[1280,512]{1,0:T(8,128)(2,1)S(1)}, bf16[1280,512]{1,0:T(8,128)(2,1)S(1)}, u32[]{:S(2)}, u32[]{:S(2)}) collective-permute-start(bf16[1280,512]{1,0:T(8,128)(2,1)S(1)} %shard_map.89), channel_id=1, source_target_pairs={{0,16},{4,20},{8,24},{12,28},{16,0},{20,4},{24,8},{28,12},{1,17},{... | collective-permute-start | bytes 3932168 | tf_op jit(solution)/shard_map/ppermute | solution.py:281
  86.8 31.1 %collective-permute-start.27 = (bf16[1280,512]{1,0:T(8,128)(2,1)}, bf16[1280,512]{1,0:T(8,128)(2,1)}, u32[]{:S(2)}, u32[]{:S(2)}) collective-permute-start(bf16[1280,512]{1,0:T(8,128)(2,1)} %collective-permute-done.25.refs_10_), channel_id=1, source_target_pairs={{0,4},{4,0},{8,12},{12,8},{16,20},{20,16},{24,28},{28,24},{1,5},{5... | collective-permute-start | bytes 3932168 | tf_op jit(solution)/shard_map/ppermute | solution.py:281
  86.8 32.5 %collective-permute-start.23 = (bf16[1280,512]{1,0:T(8,128)(2,1)}, bf16[1280,512]{1,0:T(8,128)(2,1)}, u32[]{:S(2)}, u32[]{:S(2)}) collective-permute-start(bf16[1280,512]{1,0:T(8,128)(2,1)} %collective-permute-done.21.refs_6_), channel_id=1, source_target_pairs={{0,4},{4,0},{8,12},{12,8},{16,20},{20,16},{24,28},{28,24},{1,5},{5... | collective-permute-start | bytes 3932168 | tf_op jit(solution)/shard_map/ppermute | solution.py:281
  115.8 20.1 %collective-permute-start.22 = (bf16[1280,512]{1,0:T(8,128)(2,1)}, bf16[1280,512]{1,0:T(8,128)(2,1)}, u32[]{:S(2)}, u32[]{:S(2)}) collective-permute-start(bf16[1280,512]{1,0:T(8,128)(2,1)} %collective-permute-done.20.refs_5_), channel_id=1, source_target_pairs={{0,4},{4,0},{8,12},{12,8},{16,20},{20,16},{24,28},{28,24},{1,5},{5... | collective-permute-start | bytes 3932168 | tf_op jit(solution)/shard_map/ppermute | solution.py:281
  116.8 1.1 copy-start.21
  116.8 31.9 %collective-permute-start.30 = (bf16[1280,512]{1,0:T(8,128)(2,1)}, bf16[1280,512]{1,0:T(8,128)(2,1)S(1)}, u32[]{:S(2)}, u32[]{:S(2)}) collective-permute-start(bf16[1280,512]{1,0:T(8,128)(2,1)} %collective-permute-done.20.refs_5_), channel_id=1, source_target_pairs={{0,16},{4,20},{8,24},{12,28},{16,0},{20,4},{24,8},{28,12},{1,17},{... | collective-permute-start | bytes 3932168 | tf_op jit(solution)/shard_map/ppermute | solution.py:281
  117.9 31.9 %collective-permute-start.28 = (bf16[1280,512]{1,0:T(8,128)(2,1)}, bf16[1280,512]{1,0:T(8,128)(2,1)S(1)}, u32[]{:S(2)}, u32[]{:S(2)}) collective-permute-start(bf16[1280,512]{1,0:T(8,128)(2,1)} %collective-permute-done.25.refs_10_), channel_id=1, source_target_pairs={{0,8},{4,12},{8,0},{12,4},{16,24},{20,28},{24,16},{28,20},{1,9},{5... | collective-permute-start | bytes 3932168 | tf_op jit(solution)/shard_map/ppermute | solution.py:281
  119.3 17.6 %collective-permute-start.26 = (bf16[1280,512]{1,0:T(8,128)(2,1)}, bf16[1280,512]{1,0:T(8,128)(2,1)}, u32[]{:S(2)}, u32[]{:S(2)}) collective-permute-start(bf16[1280,512]{1,0:T(8,128)(2,1)} %copy-done.21), channel_id=1, source_target_pairs={{0,4},{4,0},{8,12},{12,8},{16,20},{20,16},{24,28},{28,24},{1,5},{5... | collective-permute-start | bytes 3932168 | tf_op jit(solution)/shard_map/ppermute | solution.py:281
  120.7 1.6 copy-start.16
  120.7 1.6 copy-start.18
  120.7 1.6 copy-start.20
  122.3 2.8 %copy-start = (bf16[48,16,4096]{2,1,0:T(8,128)(2,1)S(1)}, bf16[48,16,4096]{2,1,0:T(8,128)(2,1)}, u32[]{:S(2)}) copy-start(bf16[48,16,4096]{2,1,0:T(8,128)(2,1)} %param.7) | copy-start | bytes 18874372
  125.1 5.3 %copy-start.1 = (bf16[3584,128]{1,0:T(8,128)(2,1)S(1)}, bf16[3584,128]{1,0:T(8,128)(2,1)}, u32[]{:S(2)}) copy-start(bf16[3584,128]{1,0:T(8,128)(2,1)} %bank_ref.1) | copy-start | bytes 2752516
  125.1 25.1 %slice-start = ((s8[6291456]{0:T(1024)(128)(4,1)}), s8[4194304]{0:T(1024)(128)(4,1)S(1)}, s32[]{:S(2)}) async-start(s8[6291456]{0:T(1024)(128)(4,1)} %bitcast.15), calls=%async_computation | async-start | bytes 8388608
  130.4 5.5 %copy-start.3 = (bf16[512,512]{1,0:T(8,128)(2,1)S(1)}, bf16[512,512]{1,0:T(8,128)(2,1)}, u32[]{:S(2)}) copy-start(bf16[512,512]{1,0:T(8,128)(2,1)} %copy-done.2) | copy-start | bytes 1572868
  130.5 18.2 %copy-start.7 = (bf16[512,512]{1,0:T(8,128)(2,1)S(1)}, bf16[512,512]{1,0:T(8,128)(2,1)}, u32[]{:S(2)}) copy-start(bf16[512,512]{1,0:T(8,128)(2,1)} %copy-done.6) | copy-start | bytes 1572868
  130.5 19.8 %slice-start.1 = ((s8[6291456]{0:T(1024)(128)(4,1)}), s8[2097152]{0:T(1024)(128)(4,1)S(1)}, s32[]{:S(2)}) async-start(s8[6291456]{0:T(1024)(128)(4,1)} %bitcast.15), calls=%async_computation.1 | async-start | bytes 4194304
  130.5 19.8 %copy-start.22 = (bf16[1280,512]{1,0:T(8,128)(2,1)S(1)}, bf16[1280,512]{1,0:T(8,128)(2,1)}, u32[]{:S(2)}) copy-start(bf16[1280,512]{1,0:T(8,128)(2,1)} %copy-done.21) | copy-start | bytes 3932164
  135.9 41.6 %collective-permute-start.16 = (bf16[512,512]{1,0:T(8,128)(2,1)S(1)}, bf16[512,512]{1,0:T(8,128)(2,1)S(1)}, u32[]{:S(2)}, u32[]{:S(2)}) collective-permute-start(bf16[512,512]{1,0:T(8,128)(2,1)S(1)} %copy-done.3), channel_id=1, source_target_pairs={{0,16},{4,20},{8,24},{12,28},{16,0},{20,4},{24,8},{28,12},{1,17},{... | collective-permute-start | bytes 1572872 | tf_op jit(solution)/shard_map/ppermute | solution.py:281
  136.9 40.7 %collective-permute-start.17 = (bf16[512,512]{1,0:T(8,128)(2,1)S(1)}, bf16[512,512]{1,0:T(8,128)(2,1)S(1)}, u32[]{:S(2)}, u32[]{:S(2)}) collective-permute-start(bf16[512,512]{1,0:T(8,128)(2,1)S(1)} %collective-permute-done.9.refs_6_), channel_id=1, source_target_pairs={{0,8},{4,12},{8,0},{12,4},{16,24},{20,28},{24,16},{28,20},{1,9},{5... | collective-permute-start | bytes 1572872 | tf_op jit(solution)/shard_map/ppermute | solution.py:281
  148.7 29.4 %collective-permute-start.15 = (bf16[512,512]{1,0:T(8,128)(2,1)S(1)}, bf16[512,512]{1,0:T(8,128)(2,1)S(1)}, u32[]{:S(2)}, u32[]{:S(2)}) collective-permute-start(bf16[512,512]{1,0:T(8,128)(2,1)S(1)} %copy-done.7), channel_id=1, source_target_pairs={{0,4},{4,0},{8,12},{12,8},{16,20},{20,16},{24,28},{28,24},{1,5},{5... | collective-permute-start | bytes 1572872 | tf_op jit(solution)/shard_map/ppermute | solution.py:281
  149.7 31.7 %collective-permute-start.31 = (bf16[1280,512]{1,0:T(8,128)(2,1)S(1)}, bf16[1280,512]{1,0:T(8,128)(2,1)S(1)}, u32[]{:S(2)}, u32[]{:S(2)}) collective-permute-start(bf16[1280,512]{1,0:T(8,128)(2,1)S(1)} %collective-permute-done.30.refs_2_), channel_id=1, source_target_pairs={{0,4},{4,0},{8,12},{12,8},{16,20},{20,16},{24,28},{28,24},{1,5},{5... | collective-permute-start | bytes 3932168 | tf_op jit(solution)/shard_map/ppermute | solution.py:281
  149.7 36.3 %collective-permute-start.29 = (bf16[1280,512]{1,0:T(8,128)(2,1)S(1)}, bf16[1280,512]{1,0:T(8,128)(2,1)S(1)}, u32[]{:S(2)}, u32[]{:S(2)}) collective-permute-start(bf16[1280,512]{1,0:T(8,128)(2,1)S(1)} %collective-permute-done.28.refs_2_), channel_id=1, source_target_pairs={{0,4},{4,0},{8,12},{12,8},{16,20},{20,16},{24,28},{28,24},{1,5},{5... | collective-permute-start | bytes 3932168 | tf_op jit(solution)/shard_map/ppermute | solution.py:281
  150.3 20.2 %copy-start.11 = (bf16[512,512]{1,0:T(8,128)(2,1)S(1)}, bf16[512,512]{1,0:T(8,128)(2,1)}, u32[]{:S(2)}) copy-start(bf16[512,512]{1,0:T(8,128)(2,1)} %copy-done.10) | copy-start | bytes 1572868
  150.3 20.2 %copy-start.13 = (bf16[512,512]{1,0:T(8,128)(2,1)S(1)}, bf16[512,512]{1,0:T(8,128)(2,1)}, u32[]{:S(2)}) copy-start(bf16[512,512]{1,0:T(8,128)(2,1)} %copy-done.12) | copy-start | bytes 1572868
  170.4 7.6 %copy-start.5 = (bf16[512,512]{1,0:T(8,128)(2,1)S(1)}, bf16[512,512]{1,0:T(8,128)(2,1)}, u32[]{:S(2)}) copy-start(bf16[512,512]{1,0:T(8,128)(2,1)} %copy-done.4) | copy-start | bytes 1572868
  170.4 7.6 %copy-start.9 = (bf16[512,512]{1,0:T(8,128)(2,1)S(1)}, bf16[512,512]{1,0:T(8,128)(2,1)}, u32[]{:S(2)}) copy-start(bf16[512,512]{1,0:T(8,128)(2,1)} %copy-done.8) | copy-start | bytes 1572868
  177.5 13.2 %collective-permute-start.18 = (bf16[512,512]{1,0:T(8,128)(2,1)S(1)}, bf16[512,512]{1,0:T(8,128)(2,1)S(1)}, u32[]{:S(2)}, u32[]{:S(2)}) collective-permute-start(bf16[512,512]{1,0:T(8,128)(2,1)S(1)} %collective-permute-done.16.refs_2_), channel_id=1, source_target_pairs={{0,4},{4,0},{8,12},{12,8},{16,20},{20,16},{24,28},{28,24},{1,5},{5... | collective-permute-start | bytes 1572872 | tf_op jit(solution)/shard_map/ppermute | solution.py:281
  177.6 13.1 %collective-permute-start.19 = (bf16[512,512]{1,0:T(8,128)(2,1)S(1)}, bf16[512,512]{1,0:T(8,128)(2,1)S(1)}, u32[]{:S(2)}, u32[]{:S(2)}) collective-permute-start(bf16[512,512]{1,0:T(8,128)(2,1)S(1)} %collective-permute-done.17.refs_3_), channel_id=1, source_target_pairs={{0,4},{4,0},{8,12},{12,8},{16,20},{20,16},{24,28},{28,24},{1,5},{5... | collective-permute-start | bytes 1572872 | tf_op jit(solution)/shard_map/ppermute | solution.py:281

commit v2 on v1

--- a/solution.py
+++ b/solution.py
@@ -20,16 +20,17 @@
 
 
 DIMS = (((1,), (1,)), ((), ()))
-LAST = 2
-VMEM_LIMIT = 16 * 1024 * 1024
+TILE = 256
+CORE, ONE, TWO = 1, 2, 4
+VMEM_LIMIT = 10 * 1024 * 1024
 
 
 def cut(rows, tile):
     tiles = rows // tile
-    if rows % tile or tiles < 6 or tiles % 2:
+    if rows % tile or tiles < 8:
         return None
-    last = min(LAST, tiles // 2 - 1)
-    lengths = [tiles // 2 - last] * 2 + [last] * 2
+    second = (tiles - 4) * 3 // 10
+    lengths = [tiles - 4 - second, second, 2, 2]
     pieces, start = [], 0
     for length in lengths:
         pieces.append((start * tile, length * tile))
@@ -37,58 +38,42 @@
     return pieces
 
 
-def product_kernel(counts, half, tile, offset, final, resident, at_ref, tokens_ref, *refs):
-    whole, split, with_low, with_partial = counts
+def source_of(place, me):
+    swap = (me ^ place) & CORE
+    there = place & CORE
+    for axis in (ONE, TWO):
+        if place & axis:
+            there = there ^ (axis + swap * ((axis ^ ONE ^ TWO) - axis))
+    return me ^ there
+
+
+def product_kernel(places, tile, with_low, with_partial, final, resident, tokens_ref, *refs):
     refs = list(refs)
     out_ref = refs.pop()
-    step = pl.program_id(0)
-    here = pl.ds(pl.multiple_of(step * tile, tile), tile)
-    place = 0
-
-    def term(block_ref, place):
-        depth = block_ref.shape[1]
-        columns = pl.ds(pl.multiple_of(at_ref[place] * depth, 128), depth)
-        return lax.dot_general(tokens_ref[:, columns], block_ref[...], DIMS, preferred_element_type=jnp.float32)
-
-    def store(value):
-        if final:
-            out_ref[...] = value.astype(out_ref.dtype)
-        else:
-            out_ref[:, here] = value
-
+    me = lax.axis_index("pop")
+    here = pl.ds(pl.multiple_of(pl.program_id(0) * tile, tile), tile)
     total = None
     if with_low:
         low_ref, bank_ref = refs.pop(0), refs.pop(0)
         bank = bank_ref[...]
         total = lax.dot_general(low_ref[...], jnp.concatenate([bank, bank], axis=1), DIMS, preferred_element_type=jnp.float32)
     if with_partial:
-        part = refs.pop(0)[:, pl.ds(pl.multiple_of(offset + step * tile, tile), tile)]
-        total = part if total is None else total + part
-    for place in whole:
-        value = term(refs.pop(0), place)
-        total = value if total is None else total + value
-    if not split:
-        store(total)
-        return
-    groups = [(places, (refs.pop(0), refs.pop(0))) for places in split]
-
-    def finish(pick):
-        done = total
-        for places, pair in groups:
-            block = pair[pick]
-            if resident:
-                block = block.at[pl.ds(pl.multiple_of((step - pick * half) * tile, tile), tile)]
-            value = term(block, places[pick])
-            done = value if done is None else done + value
-        store(done)
-
-    pl.when(step < half)(lambda: finish(0))
-    pl.when(step >= half)(lambda: finish(1))
-
-
-def product(at, tokens, start, length, tile, rows, whole=(), split=(), low=None, bank_out=None, partial=None, offset=0, final=False, hidden=None, resident=False):
+        total = refs.pop(0)[:, here]
+    for place, block_ref in zip(places, refs):
+        depth = block_ref.shape[1]
+        columns = pl.ds(pl.multiple_of(source_of(place, me) * depth, 128), depth)
+        block = block_ref[here, :] if resident else block_ref[...]
+        term = lax.dot_general(tokens_ref[:, columns], block, DIMS, preferred_element_type=jnp.float32)
+        total = term if total is None else total + term
+    if final:
+        out_ref[...] = total.astype(out_ref.dtype)
+    else:
+        out_ref[:, here] = total
+
+
+def product(tokens, start, length, tile, rows, blocks, low=None, bank_out=None, partial=None, hidden=None, resident=False):
     lines = tokens.shape[0]
-    base, half = start // tile, length // tile // 2
+    base, final = start // tile, partial is not None
     specs, operands, depth_sum = [pl.BlockSpec(memory_space=pltpu.VMEM)], [tokens], 0
 
     def add(operand, spec):
@@ -97,43 +82,39 @@
 
     if low is not None:
         add(low, pl.BlockSpec(memory_space=pltpu.VMEM))
-        add(bank_out, pl.BlockSpec((tile, bank_out.shape[1]), lambda i, at: (base + i, 0)))
-    if partial is not None:
+        add(bank_out, pl.BlockSpec((tile, bank_out.shape[1]), lambda i: (base + i, 0)))
+    if final:
         add(partial, pl.BlockSpec(memory_space=pltpu.VMEM))
-    for place, block, first in whole:
+    for _, block, first in blocks:
         depth = block.shape[1]
         depth_sum += depth
-        add(block, pl.BlockSpec((tile, depth), functools.partial(lambda i, at, skip: (skip + i, 0), skip=first // tile)))
-    for _, upper, lower in split:
-        depth = upper.shape[1]
-        depth_sum += depth
         if resident:
-            add(upper, pl.BlockSpec(memory_space=pltpu.VMEM))
-            add(lower, pl.BlockSpec(memory_space=pltpu.VMEM))
-            continue
-        add(upper, pl.BlockSpec((tile, depth), lambda i, at: (jnp.minimum(i, half - 1), 0)))
-        add(lower, pl.BlockSpec((tile, depth), lambda i, at: (jnp.maximum(i - half, 0), 0)))
+            add(block, pl.BlockSpec(memory_space=pltpu.VMEM))
+        else:
+            add(block, pl.BlockSpec((tile, depth), functools.partial(lambda i, skip: (skip + i, 0), skip=first // tile)))
     aliases = {}
     if hidden is not None:
-        aliases = {len(operands) + 1: 0}
+        aliases = {len(operands): 0}
         add(hidden, pl.BlockSpec(memory_space=pl.ANY))
-    counts = ([p for p, _, _ in whole], [p for p, _, _ in split], low is not None, partial is not None)
-
-    def kernel(at_ref, *refs):
+    places = [place for place, _, _ in blocks]
+
+    def kernel(*refs):
         refs = list(refs)
         if hidden is not None:
             refs.pop(-2)
-        product_kernel(counts, half, tile, offset, final, resident, at_ref, *refs)
+        product_kernel(places, tile, low is not None, final, final, resident, *refs)
 
     if final:
         out_shape = jax.ShapeDtypeStruct((lines, rows), jnp.bfloat16)
-        out_spec = pl.BlockSpec((lines, tile), lambda i, at: (0, base + i))
+        out_spec = pl.BlockSpec((lines, tile), lambda i: (0, base + i))
     else:
         out_shape = jax.ShapeDtypeStruct((lines, length), jnp.float32)
         out_spec = pl.BlockSpec(memory_space=pltpu.VMEM)
     return pl.pallas_call(
         kernel,
-        grid_spec=pltpu.PrefetchScalarGridSpec(num_scalar_prefetch=1, grid=(length // tile,), in_specs=specs, out_specs=out_spec),
+        grid=(length // tile,),
+        in_specs=specs,
+        out_specs=out_spec,
         out_shape=out_shape,
         input_output_aliases=aliases,
         compiler_params=pltpu.CompilerParams(vmem_limit_bytes=VMEM_LIMIT),
@@ -142,12 +123,15 @@
             bytes_accessed=2 * (lines * depth_sum + length * depth_sum + lines * length),
             transcendentals=0,
         ),
-    )(at, *operands)
+    )(*operands)
 
 
 def take_kernel(pieces, source_ref, *refs):
     outs, sems = refs[: len(pieces)], refs[len(pieces)]
-    copies = [pltpu.make_async_copy(source_ref.at[pl.ds(start, length)], out, sems.at[j]) for j, ((start, length), out) in enumerate(zip(pieces, outs))]
+    copies = []
+    for (start, length), out in zip(pieces, outs):
+        for at in range(0, length, TILE):
+            copies.append(pltpu.make_async_copy(source_ref.at[pl.ds(start + at, TILE)], out.at[pl.ds(at, TILE)], sems.at[len(copies)]))
     for copy in copies:
         copy.start()
     for copy in copies:
@@ -162,7 +146,7 @@
         in_specs=[pl.BlockSpec(memory_space=pl.ANY)],
         out_specs=[pl.BlockSpec(memory_space=pltpu.VMEM)] * len(pieces),
         out_shape=[jax.ShapeDtypeStruct((length, depth), source.dtype) for _, length in pieces],
-        scratch_shapes=[pltpu.SemaphoreType.DMA((len(pieces),))],
+        scratch_shapes=[pltpu.SemaphoreType.DMA((sum(length for _, length in pieces) // TILE,))],
         compiler_params=pltpu.CompilerParams(vmem_limit_bytes=VMEM_LIMIT),
         cost_estimate=pl.CostEstimate(flops=size, bytes_accessed=2 * size, transcendentals=0),
     )(source)
@@ -188,7 +172,7 @@
         ],
         out_specs=pl.BlockSpec((tile, depth), lambda i: (i, 0)),
         out_shape=jax.ShapeDtypeStruct(weight.shape, weight.dtype),
-        compiler_params=pltpu.CompilerParams(vmem_limit_bytes=12 * 1024 * 1024),
+        compiler_params=pltpu.CompilerParams(vmem_limit_bytes=VMEM_LIMIT),
         cost_estimate=pl.CostEstimate(flops=4 * rows * depth * width, bytes_accessed=4 * rows * depth, transcendentals=0),
         name="update",
     )(weight, bank_out, right_part)
@@ -225,7 +209,7 @@
             out_specs=[pl.BlockSpec((tile, width), lambda i, pick: (i, 0)), pl.BlockSpec((depth, width), lambda i, pick: (0, 0))],
         ),
         out_shape=[jax.ShapeDtypeStruct((lines, width), jnp.float32), jax.ShapeDtypeStruct((depth, width), blocks[0].dtype)],
-        compiler_params=pltpu.CompilerParams(vmem_limit_bytes=16 * 1024 * 1024),
+        compiler_params=pltpu.CompilerParams(vmem_limit_bytes=VMEM_LIMIT),
         cost_estimate=pl.CostEstimate(flops=2 * lines * features * width, bytes_accessed=2 * lines * features, transcendentals=0),
         name="project",
     )(pick, tokens, *blocks)
@@ -258,7 +242,7 @@
     return pl.pallas_call(
         functools.partial(lowrank_kernel, seeds.shape[2]),
         out_shape=[jax.ShapeDtypeStruct((lines, 2 * width), jnp.bfloat16), jax.ShapeDtypeStruct((2 * width, depth), jnp.bfloat16)],
-        compiler_params=pltpu.CompilerParams(vmem_limit_bytes=16 * 1024 * 1024),
+        compiler_params=pltpu.CompilerParams(vmem_limit_bytes=VMEM_LIMIT),
         cost_estimate=pl.CostEstimate(flops=20 * lines * width * width, bytes_accessed=8 * lines * width, transcendentals=0),
         name="lowrank",
     )(projected, coupling, seeds, columns)
@@ -273,30 +257,34 @@
     features = tokens.shape[2]
     rows, depth = weight.shape
     flat_tokens = tokens.reshape(members * tokens.shape[1], features)
-    tile = 256
+    tile = TILE
     chunks = cut(rows, tile)
     planned = pops == 8 and chunks is not None
 
     def flip(block, mask):
         return lax.ppermute(block, "pop", [(i, i ^ mask) for i in range(pops)])
 
-    at = (me ^ jnp.arange(pops, dtype=jnp.int32)).astype(jnp.int32)
+    core, one, two = CORE, ONE, TWO
+
+    def send(block, axis):
+        return lax.ppermute(block, "pop", [(i, i ^ (axis ^ (one | two) if i & core else axis)) for i in range(pops)])
+
     packed = jnp.concatenate([fitness[:, None], past_seeds.reshape(members, -1)], axis=1)
 
     held = {}
     if planned:
-        core, one, two = 1, 2, 4
-        own = take(weight, chunks[:1]) + take(weight, chunks[1:])
+        early = take(weight, chunks[1:2])
+        late = take(weight, chunks[:1] + chunks[2:])
+        own = [late[0], early[0], *late[1:]]
+        partner = flip(weight, core)
         for c, piece in enumerate(own):
-            held[c, one] = flip(piece, one)
-            held[c, two] = flip(piece, two)
-        partner = flip(weight, core)
-        for c in range(len(chunks)):
-            held[c, one | two] = flip(held[c, two], one) if c % 2 else flip(held[c, one], two)
+            held[c, one] = send(piece, one)
+            held[c, two] = send(piece, two)
+            held[c, one | two] = send(held[c, one], two)
             for mask in (one, two, one | two):
                 held[c, mask | core] = flip(held[c, mask], core)
         both = jnp.concatenate([packed, flip(packed, core)], axis=0)
-        side = lax.ppermute(both, "pop", [(i, i ^ (two if i & core else one)) for i in range(pops)])
+        side = send(both, one)
         across = lax.ppermute(both, "pop", [(i, i ^ (one | two)) for i in range(0, pops, 2)])
         mine = jnp.concatenate([side, across], axis=0)
         theirs = flip(mine, core)
@@ -337,25 +325,13 @@
     new_weight = updated(weight, bank_out, right_part)
 
     if planned:
-        hidden = None
-
-        def pair(c, upper, lower):
-            return [((u, l), held[c, u], held[c + 1, l]) for u, l in zip(upper, lower)]
-
-        def wide(c):
-            start = chunks[c][0]
-            return dict(start=start, length=2 * chunks[c][1], tile=tile, rows=rows), [(0, weight, start), (core, partner, start)]
-
-        sizes, own = wide(0)
-        partial = product(at, flat_tokens, **sizes, whole=own, split=pair(0, (2, 3, 4, 5), (2, 3, 4, 5)), low=low, bank_out=bank_out)
-        for c in (0, 1):
-            start, length = chunks[c]
+        hidden, partial = None, []
+        for c, (start, length) in enumerate(chunks):
+            near = [(0, weight, start), (core, partner, start)] + [(m, held[c, m], 0) for m in range(2, 6)]
+            partial.append(product(flat_tokens, start, length, tile, rows, near, low=low, bank_out=bank_out))
+        for c, (start, length) in enumerate(chunks):
             far = [(m, held[c, m], 0) for m in (6, 7)]
-            hidden = product(at, flat_tokens, start, length, tile, rows, whole=far, partial=partial, offset=start, final=True, hidden=hidden)
-        sizes, own = wide(2)
-        partial = product(at, flat_tokens, **sizes, whole=own, split=pair(2, (2, 3), (4, 5)), low=low, bank_out=bank_out)
-        partial = product(at, flat_tokens, **sizes, split=pair(2, (4, 5), (2, 3)), partial=partial)
-        hidden = product(at, flat_tokens, **sizes, split=pair(2, (6, 7), (6, 7)), partial=partial, final=True, hidden=hidden, resident=True)
+            hidden = product(flat_tokens, start, length, tile, rows, far, partial=partial[c], hidden=hidden, resident=c > 1)
     else:
         blocks = {0: weight}
         for bit in range((pops - 1).bit_length()):

time: 195 us -> 176 us (0.903)
  waiting for transfers between devices: 97.4 us -> 83.6 us
  Pallas kernels: 57.5 us -> 52.9 us
  starting transfers between devices: 26.1 us -> 29.2 us
  local copies, waits for them, and re-layouts: 8.93 us -> 6.72 us
    ppermute x27 -> x15, waiting for transfers between devices: 82 us -> 2.78 us  [flip(): return lax.ppermute(block, 'pop', [(i, i ^ mask) for i in range(pops)])]
    ppermute x1 -> x13, waiting for transfers between devices: 0.01 us -> 60.1 us  [send(): lax.ppermute(block, 'pop', [(i, i ^ (axis ^ (one | two) if i & core else...]
    ppermute x1 -> x13, starting transfers between devices: 2.82 us -> 13.7 us  [send(): lax.ppermute(block, 'pop', [(i, i ^ (axis ^ (one | two) if i & core else...]
    ppermute x27 -> x15, starting transfers between devices: 12.6 us -> 4.37 us  [flip(): return lax.ppermute(block, 'pop', [(i, i ^ mask) for i in range(pops)])]
    pallas_call x6 -> x8, Pallas kernels: 43.8 us -> 38.4 us  [product(): pl.pallas_call(kernel, grid=(length // tile,), in_specs=specs, out_specs=...]
    ppermute x3, waiting for transfers between devices: 15.4 us -> 19.2 us  [shards(): lax.ppermute(bank_in, 'row', [(i, (i - step) % lanes) for i in range(lane...]
    unnamed x53 -> x43, local copies, waits for them, and re-layouts: 8.12 us -> 5.9 us
  transfers between devices with their start and end apart: 32 -> 32, of which waited for: 8 -> 10; matrix products, arithmetic and copies ran while one was open for 2% -> 2% of each run, Pallas kernels for 27% -> 28%
where the time goes in v2:
time: 176 us
  waiting for transfers between devices  83.6 us (48%)
  Pallas kernels  52.9 us (30%)
  starting transfers between devices  29.2 us (17%)
  local copies, waits for them, and re-layouts  6.72 us (4%)
    ppermute x13, waiting for transfers between devices, send(): lax.ppermute(block, 'pop', [(i, i ^ (axis ^ (one | two) if i & core else...  60.1 us
    pallas_call x8, Pallas kernels, product(): pl.pallas_call(kernel, grid=(length // tile,), in_specs=specs, out_specs=...  38.4 us
    ppermute x3, waiting for transfers between devices, shards(): lax.ppermute(bank_in, 'row', [(i, (i - step) % lanes) for i in range(lane...  19.2 us
    ppermute x13, starting transfers between devices, send(): lax.ppermute(block, 'pop', [(i, i ^ (axis ^ (one | two) if i & core else...  13.7 us
    ppermute x3, starting transfers between devices, shards(): lax.ppermute(bank_in, 'row', [(i, (i - step) % lanes) for i in range(lane...  7 us
    unnamed x43, local copies, waits for them, and re-layouts  5.9 us
    pallas_call x1, Pallas kernels, updated(): pl.pallas_call(update_kernel, grid=(rows // tile,), in_specs=[pl.BlockSpe...  5.33 us
    ppermute x15, starting transfers between devices, flip(): return lax.ppermute(block, 'pop', [(i, i ^ mask) for i in range(pops)])  4.37 us
  transfers between devices with their start and end apart: 32, of which 10 were waited for; matrix products, arithmetic and copies ran while one was open for 2% of the time, Pallas kernels for 28%

profile of v2, /device:TPU:0, one launch (start us, length us, event | category | flops | bytes accessed | tf_op | source)
XLA Modules:
  0.0 175.8 jit_solution(7527774337508123593)
XLA Ops:
  0.7 1.9 %shard_map.86 = (bf16[1792,512]{1,0:T(8,128)(2,1)S(1)}, bf16[512,512]{1,0:T(8,128)(2,1)S(1)}, bf16[512,512]{1,0:T(8,128)(2,1)S(1)}) custom-call(bf16[3584,512]{1,0:T(8,128)(2,1)} %weight_ref.1), custom_call_target="tpu_custom_call" | custom-call | flops 2883584 | bytes 5767168 | tf_op jit(solution)/shard_map/pallas_call | solution.py:144
  2.5 3.0 %collective-permute-start.26 = (bf16[1792,512]{1,0:T(8,128)(2,1)S(1)}, bf16[1792,512]{1,0:T(8,128)(2,1)}, u32[]{:S(2)}, u32[]{:S(2)}) collective-permute-start(bf16[1792,512]{1,0:T(8,128)(2,1)S(1)} %get-tuple-element.14), channel_id=1, source_target_pairs={{0,8},{4,20},{8,0},{12,28},{16,24},{20,4},{24,16},{28,12},{1,9},{5... | collective-permute-start | bytes 5505032 | tf_op jit(solution)/shard_map/ppermute | solution.py:270
  5.7 1.2 collective-permute-done.3
  6.8 0.1 pad_add_fusion.2
  6.9 0.7 collective-permute-start.4
  7.6 4.1 %collective-permute-start.5 = (s32[96,17]{0,1:T(8,128)S(1)}, s32[96,17]{0,1:T(8,128)S(1)}, u32[]{:S(2)}, u32[]{:S(2)}) collective-permute-start(s32[96,17]{0,1:T(8,128)S(1)} %pad_add_fusion.2), channel_id=1, source_target_pairs={{0,24},{8,16},{16,8},{24,0},{1,25},{9,17},{17,9},{25,1},{2,26},{10... | collective-permute-start | bytes 19592 | tf_op jit(solution)/shard_map/ppermute | solution.py:288
  11.8 3.7 %collective-permute-start = (bf16[1024,128]{1,0:T(8,128)(2,1)S(1)}, bf16[1024,128]{1,0:T(8,128)(2,1)S(1)}, u32[]{:S(2)}, u32[]{:S(2)}) collective-permute-start(bf16[1024,128]{1,0:T(8,128)(2,1)S(1)} %copy-done.8), channel_id=1, source_target_pairs={{0,3},{1,0},{2,1},{3,2},{4,7},{5,4},{6,5},{7,6},{8,11},{9,8},{10,9... | collective-permute-start | bytes 786440 | tf_op jit(solution)/shard_map/ppermute | solution.py:313
  15.5 11.4 %collective-permute-done.4 = s32[96,17]{0,1:T(8,128)S(1)} collective-permute-done((s32[96,17]{0,1:T(8,128)S(1)}, s32[96,17]{0,1:T(8,128)S(1)}, u32[]{:S(2)}, u32[]{:S(2)}) %collective-permute-start.4) | collective-permute-done | bytes 6560 | tf_op jit(solution)/shard_map/ppermute | solution.py:270
  26.9 1.6 collective-permute-done.5
  28.5 0.1 pad_add_fusion
  28.6 2.7 %collective-permute-start.1 = (bf16[1024,128]{1,0:T(8,128)(2,1)S(1)}, bf16[1024,128]{1,0:T(8,128)(2,1)S(1)}, u32[]{:S(2)}, u32[]{:S(2)}) collective-permute-start(bf16[1024,128]{1,0:T(8,128)(2,1)S(1)} %copy-done.8), channel_id=1, source_target_pairs={{0,2},{1,3},{2,0},{3,1},{4,6},{5,7},{6,4},{7,5},{8,10},{9,11},{10,... | collective-permute-start | bytes 786440 | tf_op jit(solution)/shard_map/ppermute | solution.py:313
  31.3 0.5 collective-permute-start.28
  31.8 0.9 collective-permute-start.7
  32.7 0.7 copy-done.10
  33.4 0.6 collective-permute-start.14
  34.0 9.8 %collective-permute-done.1.refs_2_ = bf16[1024,128]{1,0:T(8,128)(2,1)S(1)} collective-permute-done((bf16[1024,128]{1,0:T(8,128)(2,1)S(1)}, bf16[1024,128]{1,0:T(8,128)(2,1)S(1)}, u32[]{:S(2)}, u32[]{:S(2)}) %collective-permute-start.1) | collective-permute-done | bytes 262176 | tf_op jit(solution)/shard_map/ppermute | solution.py:313
  43.9 0.7 copy-done.12
  44.5 0.7 collective-permute-start.2
  45.2 9.3 %collective-permute-done.2.refs_3_ = bf16[1024,128]{1,0:T(8,128)(2,1)S(1)} collective-permute-done((bf16[1024,128]{1,0:T(8,128)(2,1)S(1)}, bf16[1024,128]{1,0:T(8,128)(2,1)S(1)}, u32[]{:S(2)}, u32[]{:S(2)}) %collective-permute-start.2) | collective-permute-done | bytes 262176 | tf_op jit(solution)/shard_map/ppermute | solution.py:313
  54.6 0.7 copy-done.14
  55.3 0.5 collective-permute-start.16
  55.8 0.8 copy-done.4
  56.6 1.5 collective-permute-start.8
  58.1 2.0 %shard_map.89 = bf16[768,512]{1,0:T(8,128)(2,1)} custom-call(bf16[3584,512]{1,0:T(8,128)(2,1)} %weight_ref.1), custom_call_target="tpu_custom_call" | custom-call | flops 786432 | bytes 1572864 | tf_op jit(solution)/shard_map/pallas_call | solution.py:144
  60.1 11.2 %collective-permute-done.16.refs_7_ = bf16[512,512]{1,0:T(8,128)(2,1)S(1)} collective-permute-done((bf16[512,512]{1,0:T(8,128)(2,1)S(1)}, bf16[512,512]{1,0:T(8,128)(2,1)S(1)}, u32[]{:S(2)}, u32[]{:S(2)}) %collective-permute-start.16) | collective-permute-done | bytes 524320 | tf_op jit(solution)/shard_map/ppermute | solution.py:270
  71.4 1.5 collective-permute-start.20
  72.9 0.5 collective-permute-start.10
  73.4 1.5 collective-permute-start.30
  74.9 11.8 %collective-permute-done.10.refs_7_ = bf16[512,512]{1,0:T(8,128)(2,1)} collective-permute-done((bf16[512,512]{1,0:T(8,128)(2,1)S(1)}, bf16[512,512]{1,0:T(8,128)(2,1)}, u32[]{:S(2)}, u32[]{:S(2)}) %collective-permute-start.10) | collective-permute-done | bytes 524320 | tf_op jit(solution)/shard_map/ppermute | solution.py:270
  86.7 0.3 collective-permute-start.22
  87.0 5.0 %collective-permute-done.20.refs_5_ = bf16[768,512]{1,0:T(8,128)(2,1)S(1)} collective-permute-done((bf16[768,512]{1,0:T(8,128)(2,1)}, bf16[768,512]{1,0:T(8,128)(2,1)S(1)}, u32[]{:S(2)}, u32[]{:S(2)}) %collective-permute-start.20) | collective-permute-done | bytes 786464 | tf_op jit(solution)/shard_map/ppermute | solution.py:270
  92.0 0.5 collective-permute-start.29
  92.5 0.1 copy.13.seeds_ref
  92.6 0.1 pad_add_fusion.3.pick_ref
  92.7 0.6 slice_add_fusion
  93.3 0.8 concatenate.20
  94.2 20.5 %collective-permute-done.22.refs_7_ = bf16[768,512]{1,0:T(8,128)(2,1)S(1)} collective-permute-done((bf16[768,512]{1,0:T(8,128)(2,1)}, bf16[768,512]{1,0:T(8,128)(2,1)S(1)}, u32[]{:S(2)}, u32[]{:S(2)}) %collective-permute-start.22) | collective-permute-done | bytes 786464 | tf_op jit(solution)/shard_map/ppermute | solution.py:270
  114.7 0.3 collective-permute-start.15
  115.0 0.3 convert_reduce_fusion
  115.3 1.6 collective-permute-done.15.refs_6_
  116.8 0.3 collective-permute-start.17
  117.1 0.3 collective-permute-start.31
  117.4 1.3 fusion.2.coupling_ref
  118.8 2.8 %copy-done = bf16[48,16,4096]{2,1,0:T(8,128)(2,1)S(1)} copy-done((bf16[48,16,4096]{2,1,0:T(8,128)(2,1)S(1)}, bf16[48,16,4096]{2,1,0:T(8,128)(2,1)}, u32[]{:S(2)}) %copy-start) | copy-done | bytes 6291480
  121.5 2.9 %project.1 = (f32[768,128]{1,0:T(8,128)S(1)}, bf16[512,128]{1,0:T(8,128)(2,1)S(1)}) custom-call(s32[6]{0:T(128)S(1)} %pad_add_fusion.3.pick_ref, bf16[768,4096]{1,0:T(8,128)(2,1)S(1)} %bitcast.14, bf16[1024,128]{1,0:T(8,128)(2,1)S(1)} %copy-done.9, bf16[1024,128]{1,0:T(8,128)(2,1)S(1)} %copy-done.11, bf16[1024,128]{1,0:T(8,128)(2,1)S(1)} %copy-done.13, ...), custom_call_target="tpu_custom_call" | custom-call | flops 805306368 | bytes 6291456 | tf_op jit(solution)/shard_map/project/pallas_call | solution.py:202
  124.5 2.3 %lowrank.1 = (bf16[768,256]{1,0:T(8,128)(2,1)S(1)}, bf16[256,512]{1,0:T(8,128)(2,1)S(1)}) custom-call(f32[768,128]{1,0:T(8,128)S(1)} %get-tuple-element.9.projected_ref, f32[128,128]{1,0:T(8,128)S(1)} %fusion.2.coupling_ref, s32[48,2,8]{2,1,0:T(2,128)S(1)} %copy.13.seeds_ref, bf16[512,128]{1,0:T(8,128)(2,1)S(1)} %get-tuple-element.10.columns_ref), custom_call_target="tpu_custom_call" | custom-call | flops 251658240 | bytes 786432 | tf_op jit(solution)/shard_map/lowrank/pallas_call | solution.py:242
  126.8 5.3 %update.1 = bf16[3584,512]{1,0:T(8,128)(2,1)} custom-call(bf16[3584,512]{1,0:T(8,128)(2,1)} %weight_ref.1, bf16[3584,128]{1,0:T(8,128)(2,1)S(1)} %copy-done.1, bf16[256,512]{1,0:T(8,128)(2,1)S(1)} %get-tuple-element.15.right_ref), custom_call_target="tpu_custom_call" | custom-call | flops 939524096 | bytes 7340032 | tf_op jit(solution)/shard_map/update/pallas_call | solution.py:165
  132.2 1.0 collective-permute-start.18
  133.2 0.4 collective-permute-start.21
  133.5 1.2 collective-permute-start.24
  134.8 0.1 collective-permute-start.23
  134.9 12.3 %shard_map.91.refs_1_ = f32[768,1792]{1,0:T(8,128)S(1)} custom-call(bf16[768,4096]{1,0:T(8,128)(2,1)S(1)} %bitcast.17, bf16[768,256]{1,0:T(8,128)(2,1)S(1)} %get-tuple-element.11.refs_1_, bf16[3584,128]{1,0:T(8,128)(2,1)S(1)} %copy-done.1, bf16[3584,512]{1,0:T(8,128)(2,1)} %weight_ref.1, bf16[3584,512]{1,0:T(8,128)(2,1)} %collective-permute-done.7.refs_4_, ...), custom_call_target="tpu_custom_call" | custom-call | flops 8455716864 | bytes 18481152 | tf_op jit(solution)/shard_map/pallas_call | solution.py:113
  147.2 0.4 collective-permute-start.9
  147.7 0.8 collective-permute-start.12
  148.5 4.1 %shard_map.88.refs_1_ = f32[768,512]{1,0:T(8,128)S(1)} custom-call(bf16[768,4096]{1,0:T(8,128)(2,1)S(1)} %bitcast.18, bf16[768,256]{1,0:T(8,128)(2,1)S(1)} %get-tuple-element.11.refs_1_, bf16[3584,128]{1,0:T(8,128)(2,1)S(1)} %copy-done.1, bf16[3584,512]{1,0:T(8,128)(2,1)} %weight_ref.1, bf16[3584,512]{1,0:T(8,128)(2,1)} %collective-permute-done.7.refs_4_, ...), custom_call_target="tpu_custom_call" | custom-call | flops 2415919104 | bytes 8650752 | tf_op jit(solution)/shard_map/pallas_call | solution.py:113
  152.6 0.6 collective-permute-start.25
  153.2 5.7 %shard_map.90.refs_1_ = f32[768,768]{1,0:T(8,128)S(1)} custom-call(bf16[768,4096]{1,0:T(8,128)(2,1)S(1)} %bitcast.19, bf16[768,256]{1,0:T(8,128)(2,1)S(1)} %get-tuple-element.11.refs_1_, bf16[3584,128]{1,0:T(8,128)(2,1)S(1)} %copy-done.1, bf16[3584,512]{1,0:T(8,128)(2,1)} %weight_ref.1, bf16[3584,512]{1,0:T(8,128)(2,1)} %collective-permute-done.7.refs_4_, ...), custom_call_target="tpu_custom_call" | custom-call | flops 3623878656 | bytes 10616832 | tf_op jit(solution)/shard_map/pallas_call | solution.py:113
  158.8 0.1 collective-permute-start.19
  158.9 0.5 collective-permute-start.13
  159.4 4.2 %shard_map.87.refs_1_ = f32[768,512]{1,0:T(8,128)S(1)} custom-call(bf16[768,4096]{1,0:T(8,128)(2,1)S(1)} %bitcast.20, bf16[768,256]{1,0:T(8,128)(2,1)S(1)} %get-tuple-element.11.refs_1_, bf16[3584,128]{1,0:T(8,128)(2,1)S(1)} %copy-done.1, bf16[3584,512]{1,0:T(8,128)(2,1)} %weight_ref.1, bf16[3584,512]{1,0:T(8,128)(2,1)} %collective-permute-done.7.refs_4_, ...), custom_call_target="tpu_custom_call" | custom-call | flops 2415919104 | bytes 8650752 | tf_op jit(solution)/shard_map/pallas_call | solution.py:113
  163.6 5.5 %shard_map.92.refs_4_ = bf16[768,3584]{1,0:T(8,128)(2,1)} custom-call(bf16[768,4096]{1,0:T(8,128)(2,1)S(1)} %bitcast.21, f32[768,1792]{1,0:T(8,128)S(1)} %shard_map.91.refs_1_, bf16[1792,512]{1,0:T(8,128)(2,1)S(1)} %collective-permute-done.30.refs_2_, bf16[1792,512]{1,0:T(8,128)(2,1)S(1)} %collective-permute-done.31.refs_3_), custom_call_target="tpu_custom_call" | custom-call | flops 2818572288 | bytes 7995392 | tf_op jit(solution)/shard_map/pallas_call | solution.py:113
  169.1 2.7 %shard_map.93.refs_4_ = bf16[768,3584]{1,0:T(8,128)(2,1)} custom-call(bf16[768,4096]{1,0:T(8,128)(2,1)S(1)} %bitcast.22, f32[768,768]{1,0:T(8,128)S(1)} %shard_map.90.refs_1_, bf16[768,512]{1,0:T(8,128)(2,1)S(1)} %collective-permute-done.24.refs_2_, bf16[768,512]{1,0:T(8,128)(2,1)S(1)} %collective-permute-done.25.refs_3_, ...), custom_call_target="tpu_custom_call", output_to_operand_aliasing={{}: (4, {})} | custom-call | flops 1207959552 | bytes 4325376 | tf_op jit(solution)/shard_map/pallas_call | solution.py:113
  171.9 2.0 %shard_map.94.refs_4_ = bf16[768,3584]{1,0:T(8,128)(2,1)} custom-call(bf16[768,4096]{1,0:T(8,128)(2,1)S(1)} %bitcast.23, f32[768,512]{1,0:T(8,128)S(1)} %shard_map.88.refs_1_, bf16[512,512]{1,0:T(8,128)(2,1)S(1)} %collective-permute-done.18.refs_2_, bf16[512,512]{1,0:T(8,128)(2,1)S(1)} %collective-permute-done.19.refs_3_, ...), custom_call_target="tpu_custom_call", output_to_operand_aliasing={{}: (4, {})} | custom-call | flops 805306368 | bytes 3407872 | tf_op jit(solution)/shard_map/pallas_call | solution.py:113
  173.9 2.0 %shard_map.95 = bf16[768,3584]{1,0:T(8,128)(2,1)} custom-call(bf16[768,4096]{1,0:T(8,128)(2,1)S(1)} %bitcast.24, f32[768,512]{1,0:T(8,128)S(1)} %shard_map.87.refs_1_, bf16[512,512]{1,0:T(8,128)(2,1)S(1)} %collective-permute-done.12.refs_2_, bf16[512,512]{1,0:T(8,128)(2,1)S(1)} %collective-permute-done.13.refs_3_, ...), custom_call_target="tpu_custom_call", output_to_operand_aliasing={{}: (4, {})} | custom-call | flops 805306368 | bytes 3407872 | tf_op jit(solution)/shard_map/pallas_call | solution.py:113
  (70 shorter events, 0.3 us)
Async XLA Ops:
  0.6 5.0 %copy-start.18 = (s32[48]{0:T(128)S(1)}, s32[48]{0:T(128)}, u32[]{:S(2)}) copy-start(s32[48]{0:T(128)} %param.11) | copy-start | bytes 580
  0.6 4.9 %copy-start.16 = (s32[48,2,8]{0,2,1:T(8,128)S(1)}, s32[48,2,8]{0,2,1:T(8,128)}, u32[]{:S(2)}) copy-start(s32[48,2,8]{0,2,1:T(8,128)} %param.12) | copy-start | bytes 9220
  0.6 11.2 %copy-start.8 = (bf16[1024,128]{1,0:T(8,128)(2,1)S(1)}, bf16[1024,128]{1,0:T(8,128)(2,1)}, u32[]{:S(2)}) copy-start(bf16[1024,128]{1,0:T(8,128)(2,1)} %refs_0_.1) | copy-start | bytes 786436
  2.5 70.8 %collective-permute-start.26 = (bf16[1792,512]{1,0:T(8,128)(2,1)S(1)}, bf16[1792,512]{1,0:T(8,128)(2,1)}, u32[]{:S(2)}, u32[]{:S(2)}) collective-permute-start(bf16[1792,512]{1,0:T(8,128)(2,1)S(1)} %get-tuple-element.14), channel_id=1, source_target_pairs={{0,8},{4,20},{8,0},{12,28},{16,24},{20,4},{24,16},{28,12},{1,9},{5... | collective-permute-start | bytes 5505032 | tf_op jit(solution)/shard_map/ppermute | solution.py:270
  5.6 1.2 collective-permute-start.3
  6.9 20.0 %collective-permute-start.4 = (s32[96,17]{0,1:T(8,128)S(1)}, s32[96,17]{0,1:T(8,128)S(1)}, u32[]{:S(2)}, u32[]{:S(2)}) collective-permute-start(s32[96,17]{0,1:T(8,128)S(1)} %pad_add_fusion.2), channel_id=1, source_target_pairs={{0,8},{4,20},{8,0},{12,28},{16,24},{20,4},{24,16},{28,12},{1,9},{5... | collective-permute-start | bytes 19592 | tf_op jit(solution)/shard_map/ppermute | solution.py:270
  7.6 20.9 %collective-permute-start.5 = (s32[96,17]{0,1:T(8,128)S(1)}, s32[96,17]{0,1:T(8,128)S(1)}, u32[]{:S(2)}, u32[]{:S(2)}) collective-permute-start(s32[96,17]{0,1:T(8,128)S(1)} %pad_add_fusion.2), channel_id=1, source_target_pairs={{0,24},{8,16},{16,8},{24,0},{1,25},{9,17},{17,9},{25,1},{2,26},{10... | collective-permute-start | bytes 19592 | tf_op jit(solution)/shard_map/ppermute | solution.py:288
  11.8 20.8 %collective-permute-start = (bf16[1024,128]{1,0:T(8,128)(2,1)S(1)}, bf16[1024,128]{1,0:T(8,128)(2,1)S(1)}, u32[]{:S(2)}, u32[]{:S(2)}) collective-permute-start(bf16[1024,128]{1,0:T(8,128)(2,1)S(1)} %copy-done.8), channel_id=1, source_target_pairs={{0,3},{1,0},{2,1},{3,2},{4,7},{5,4},{6,5},{7,6},{8,11},{9,8},{10,9... | collective-permute-start | bytes 786440 | tf_op jit(solution)/shard_map/ppermute | solution.py:313
  28.6 3.2 %collective-permute-start.6 = (s32[192,17]{0,1:T(8,128)S(1)}, s32[192,17]{0,1:T(8,128)S(1)}, u32[]{:S(2)}, u32[]{:S(2)}) collective-permute-start(s32[192,17]{0,1:T(8,128)S(1)} %pad_add_fusion), channel_id=1, source_target_pairs={{0,4},{4,0},{8,12},{12,8},{16,20},{20,16},{24,28},{28,24},{1,5},{5... | collective-permute-start | bytes 39176 | tf_op jit(solution)/shard_map/ppermute | solution.py:265
  28.6 15.2 %collective-permute-start.1 = (bf16[1024,128]{1,0:T(8,128)(2,1)S(1)}, bf16[1024,128]{1,0:T(8,128)(2,1)S(1)}, u32[]{:S(2)}, u32[]{:S(2)}) collective-permute-start(bf16[1024,128]{1,0:T(8,128)(2,1)S(1)} %copy-done.8), channel_id=1, source_target_pairs={{0,2},{1,3},{2,0},{3,1},{4,6},{5,7},{6,4},{7,5},{8,10},{9,11},{10,... | collective-permute-start | bytes 786440 | tf_op jit(solution)/shard_map/ppermute | solution.py:313
  31.3 60.7 %collective-permute-start.28 = (bf16[1792,512]{1,0:T(8,128)(2,1)S(1)}, bf16[1792,512]{1,0:T(8,128)(2,1)}, u32[]{:S(2)}, u32[]{:S(2)}) collective-permute-start(bf16[1792,512]{1,0:T(8,128)(2,1)S(1)} %get-tuple-element.14), channel_id=1, source_target_pairs={{0,16},{4,12},{8,24},{12,4},{16,0},{20,28},{24,8},{28,20},{1,17},{... | collective-permute-start | bytes 5505032 | tf_op jit(solution)/shard_map/ppermute | solution.py:270
  31.8 103.0 %collective-permute-start.7 = (bf16[3584,512]{1,0:T(8,128)(2,1)}, bf16[3584,512]{1,0:T(8,128)(2,1)}, u32[]{:S(2)}, u32[]{:S(2)}) collective-permute-start(bf16[3584,512]{1,0:T(8,128)(2,1)} %weight_ref.1), channel_id=1, source_target_pairs={{0,4},{4,0},{8,12},{12,8},{16,20},{20,16},{24,28},{28,24},{1,5},{5... | collective-permute-start | bytes 11010056 | tf_op jit(solution)/shard_map/ppermute | solution.py:265
  32.7 0.7 copy-start.10
  33.4 22.4 %collective-permute-start.14 = (bf16[512,512]{1,0:T(8,128)(2,1)S(1)}, bf16[512,512]{1,0:T(8,128)(2,1)S(1)}, u32[]{:S(2)}, u32[]{:S(2)}) collective-permute-start(bf16[512,512]{1,0:T(8,128)(2,1)S(1)} %get-tuple-element.13), channel_id=1, source_target_pairs={{0,8},{4,20},{8,0},{12,28},{16,24},{20,4},{24,16},{28,12},{1,9},{5... | collective-permute-start | bytes 1572872 | tf_op jit(solution)/shard_map/ppermute | solution.py:270
  43.9 0.7 copy-start.12
  44.5 10.0 %collective-permute-start.2 = (bf16[1024,128]{1,0:T(8,128)(2,1)S(1)}, bf16[1024,128]{1,0:T(8,128)(2,1)S(1)}, u32[]{:S(2)}, u32[]{:S(2)}) collective-permute-start(bf16[1024,128]{1,0:T(8,128)(2,1)S(1)} %copy-done.8), channel_id=1, source_target_pairs={{0,1},{1,2},{2,3},{3,0},{4,5},{5,6},{6,7},{7,4},{8,9},{9,10},{10,1... | collective-permute-start | bytes 786440 | tf_op jit(solution)/shard_map/ppermute | solution.py:313
  54.6 0.7 copy-start.14
  55.3 16.1 %collective-permute-start.16 = (bf16[512,512]{1,0:T(8,128)(2,1)S(1)}, bf16[512,512]{1,0:T(8,128)(2,1)S(1)}, u32[]{:S(2)}, u32[]{:S(2)}) collective-permute-start(bf16[512,512]{1,0:T(8,128)(2,1)S(1)} %get-tuple-element.13), channel_id=1, source_target_pairs={{0,16},{4,12},{8,24},{12,4},{16,0},{20,28},{24,8},{28,20},{1,17},{... | collective-permute-start | bytes 1572872 | tf_op jit(solution)/shard_map/ppermute | solution.py:270
  55.8 0.8 copy-start.4
  56.6 35.9 %copy-start.17 = (s32[48,2,8]{0,2,1:T(8,128)S(1)}, s32[48,2,8]{0,2,1:T(8,128)}, u32[]{:S(2)}) copy-start(s32[48,2,8]{0,2,1:T(8,128)} %param.13) | copy-start | bytes 9220
  56.6 16.2 %collective-permute-start.8 = (bf16[512,512]{1,0:T(8,128)(2,1)S(1)}, bf16[512,512]{1,0:T(8,128)(2,1)S(1)}, u32[]{:S(2)}, u32[]{:S(2)}) collective-permute-start(bf16[512,512]{1,0:T(8,128)(2,1)S(1)} %get-tuple-element.12), channel_id=1, source_target_pairs={{0,8},{4,20},{8,0},{12,28},{16,24},{20,4},{24,16},{28,12},{1,9},{5... | collective-permute-start | bytes 1572872 | tf_op jit(solution)/shard_map/ppermute | solution.py:270
  71.4 2.0 %copy-start.6 = (bf16[512,512]{1,0:T(8,128)(2,1)}, bf16[512,512]{1,0:T(8,128)(2,1)S(1)}, u32[]{:S(2)}) copy-start(bf16[512,512]{1,0:T(8,128)(2,1)S(1)} %collective-permute-done.16.refs_7_) | copy-start | bytes 1572868
  71.4 20.6 %collective-permute-start.20 = (bf16[768,512]{1,0:T(8,128)(2,1)}, bf16[768,512]{1,0:T(8,128)(2,1)S(1)}, u32[]{:S(2)}, u32[]{:S(2)}) collective-permute-start(bf16[768,512]{1,0:T(8,128)(2,1)} %shard_map.89), channel_id=1, source_target_pairs={{0,8},{4,20},{8,0},{12,28},{16,24},{20,4},{24,16},{28,12},{1,9},{5... | collective-permute-start | bytes 2359304 | tf_op jit(solution)/shard_map/ppermute | solution.py:270
  72.9 19.1 %copy-start.2 = (bf16[512,512]{1,0:T(8,128)(2,1)}, bf16[512,512]{1,0:T(8,128)(2,1)S(1)}, u32[]{:S(2)}) copy-start(bf16[512,512]{1,0:T(8,128)(2,1)S(1)} %collective-permute-done.8.refs_5_) | copy-start | bytes 1572868
  72.9 13.9 %collective-permute-start.10 = (bf16[512,512]{1,0:T(8,128)(2,1)S(1)}, bf16[512,512]{1,0:T(8,128)(2,1)}, u32[]{:S(2)}, u32[]{:S(2)}) collective-permute-start(bf16[512,512]{1,0:T(8,128)(2,1)S(1)} %get-tuple-element.12), channel_id=1, source_target_pairs={{0,16},{4,12},{8,24},{12,4},{16,0},{20,28},{24,8},{28,20},{1,17},{... | collective-permute-start | bytes 1572872 | tf_op jit(solution)/shard_map/ppermute | solution.py:270
  73.4 43.7 %collective-permute-start.30 = (bf16[1792,512]{1,0:T(8,128)(2,1)}, bf16[1792,512]{1,0:T(8,128)(2,1)S(1)}, u32[]{:S(2)}, u32[]{:S(2)}) collective-permute-start(bf16[1792,512]{1,0:T(8,128)(2,1)} %collective-permute-done.26.refs_5_), channel_id=1, source_target_pairs={{0,16},{4,12},{8,24},{12,4},{16,0},{20,28},{24,8},{28,20},{1,17},{... | collective-permute-start | bytes 5505032 | tf_op jit(solution)/shard_map/ppermute | solution.py:270
  86.7 28.0 %collective-permute-start.22 = (bf16[768,512]{1,0:T(8,128)(2,1)}, bf16[768,512]{1,0:T(8,128)(2,1)S(1)}, u32[]{:S(2)}, u32[]{:S(2)}) collective-permute-start(bf16[768,512]{1,0:T(8,128)(2,1)} %shard_map.89), channel_id=1, source_target_pairs={{0,16},{4,12},{8,24},{12,4},{16,0},{20,28},{24,8},{28,20},{1,17},{... | collective-permute-start | bytes 2359304 | tf_op jit(solution)/shard_map/ppermute | solution.py:270
  92.0 41.2 %collective-permute-start.27 = (bf16[1792,512]{1,0:T(8,128)(2,1)}, bf16[1792,512]{1,0:T(8,128)(2,1)}, u32[]{:S(2)}, u32[]{:S(2)}) collective-permute-start(bf16[1792,512]{1,0:T(8,128)(2,1)} %collective-permute-done.26.refs_5_), channel_id=1, source_target_pairs={{0,4},{4,0},{8,12},{12,8},{16,20},{20,16},{24,28},{28,24},{1,5},{5... | collective-permute-start | bytes 5505032 | tf_op jit(solution)/shard_map/ppermute | solution.py:265
  92.0 41.5 %collective-permute-start.29 = (bf16[1792,512]{1,0:T(8,128)(2,1)}, bf16[1792,512]{1,0:T(8,128)(2,1)}, u32[]{:S(2)}, u32[]{:S(2)}) collective-permute-start(bf16[1792,512]{1,0:T(8,128)(2,1)} %collective-permute-done.28.refs_7_), channel_id=1, source_target_pairs={{0,4},{4,0},{8,12},{12,8},{16,20},{20,16},{24,28},{28,24},{1,5},{5... | collective-permute-start | bytes 5505032 | tf_op jit(solution)/shard_map/ppermute | solution.py:265
  94.1 24.6 %copy-start.9 = (bf16[1024,128]{1,0:T(8,128)(2,1)S(1)}, bf16[1024,128]{1,0:T(8,128)(2,1)}, u32[]{:S(2)}) copy-start(bf16[1024,128]{1,0:T(8,128)(2,1)} %refs_0_.1) | copy-start | bytes 786436
  94.1 24.6 %copy-start.11 = (bf16[1024,128]{1,0:T(8,128)(2,1)S(1)}, bf16[1024,128]{1,0:T(8,128)(2,1)}, u32[]{:S(2)}) copy-start(bf16[1024,128]{1,0:T(8,128)(2,1)} %copy-done.10) | copy-start | bytes 786436
  94.1 24.6 %copy-start.13 = (bf16[1024,128]{1,0:T(8,128)(2,1)S(1)}, bf16[1024,128]{1,0:T(8,128)(2,1)}, u32[]{:S(2)}) copy-start(bf16[1024,128]{1,0:T(8,128)(2,1)} %copy-done.12) | copy-start | bytes 786436
  94.1 24.6 %copy-start.15 = (bf16[1024,128]{1,0:T(8,128)(2,1)S(1)}, bf16[1024,128]{1,0:T(8,128)(2,1)}, u32[]{:S(2)}) copy-start(bf16[1024,128]{1,0:T(8,128)(2,1)} %copy-done.14) | copy-start | bytes 786436
  114.7 2.1 %collective-permute-start.15 = (bf16[512,512]{1,0:T(8,128)(2,1)}, bf16[512,512]{1,0:T(8,128)(2,1)S(1)}, u32[]{:S(2)}, u32[]{:S(2)}) collective-permute-start(bf16[512,512]{1,0:T(8,128)(2,1)} %copy-done.4), channel_id=1, source_target_pairs={{0,4},{4,0},{8,12},{12,8},{16,20},{20,16},{24,28},{28,24},{1,5},{5... | collective-permute-start | bytes 1572872 | tf_op jit(solution)/shard_map/ppermute | solution.py:265
  116.8 15.3 %collective-permute-start.17 = (bf16[512,512]{1,0:T(8,128)(2,1)}, bf16[512,512]{1,0:T(8,128)(2,1)S(1)}, u32[]{:S(2)}, u32[]{:S(2)}) collective-permute-start(bf16[512,512]{1,0:T(8,128)(2,1)} %copy-done.6), channel_id=1, source_target_pairs={{0,4},{4,0},{8,12},{12,8},{16,20},{20,16},{24,28},{28,24},{1,5},{5... | collective-permute-start | bytes 1572872 | tf_op jit(solution)/shard_map/ppermute | solution.py:265
  117.1 46.5 %collective-permute-start.31 = (bf16[1792,512]{1,0:T(8,128)(2,1)S(1)}, bf16[1792,512]{1,0:T(8,128)(2,1)S(1)}, u32[]{:S(2)}, u32[]{:S(2)}) collective-permute-start(bf16[1792,512]{1,0:T(8,128)(2,1)S(1)} %collective-permute-done.30.refs_2_), channel_id=1, source_target_pairs={{0,4},{4,0},{8,12},{12,8},{16,20},{20,16},{24,28},{28,24},{1,5},{5... | collective-permute-start | bytes 5505032 | tf_op jit(solution)/shard_map/ppermute | solution.py:265
  118.8 2.8 %copy-start = (bf16[48,16,4096]{2,1,0:T(8,128)(2,1)S(1)}, bf16[48,16,4096]{2,1,0:T(8,128)(2,1)}, u32[]{:S(2)}) copy-start(bf16[48,16,4096]{2,1,0:T(8,128)(2,1)} %param.7) | copy-start | bytes 18874372
  121.5 5.3 %copy-start.1 = (bf16[3584,128]{1,0:T(8,128)(2,1)S(1)}, bf16[3584,128]{1,0:T(8,128)(2,1)}, u32[]{:S(2)}) copy-start(bf16[3584,128]{1,0:T(8,128)(2,1)} %bank_ref.1) | copy-start | bytes 2752516
  121.5 13.3 %slice-start = ((s8[6291456]{0:T(1024)(128)(4,1)}), s8[4194304]{0:T(1024)(128)(4,1)S(1)}, s32[]{:S(2)}) async-start(s8[6291456]{0:T(1024)(128)(4,1)} %bitcast.15), calls=%async_computation | async-start | bytes 8388608
  126.8 5.4 %copy-start.5 = (bf16[512,512]{1,0:T(8,128)(2,1)S(1)}, bf16[512,512]{1,0:T(8,128)(2,1)}, u32[]{:S(2)}) copy-start(bf16[512,512]{1,0:T(8,128)(2,1)} %copy-done.4) | copy-start | bytes 1572868
  126.8 8.1 %slice-start.1 = ((s8[6291456]{0:T(1024)(128)(4,1)}), s8[2097152]{0:T(1024)(128)(4,1)S(1)}, s32[]{:S(2)}) async-start(s8[6291456]{0:T(1024)(128)(4,1)} %bitcast.15), calls=%async_computation.1 | async-start | bytes 4194304
  132.2 15.0 %collective-permute-start.18 = (bf16[512,512]{1,0:T(8,128)(2,1)S(1)}, bf16[512,512]{1,0:T(8,128)(2,1)S(1)}, u32[]{:S(2)}, u32[]{:S(2)}) collective-permute-start(bf16[512,512]{1,0:T(8,128)(2,1)S(1)} %copy-done.5), channel_id=1, source_target_pairs={{0,16},{4,12},{8,24},{12,4},{16,0},{20,28},{24,8},{28,20},{1,17},{... | collective-permute-start | bytes 1572872 | tf_op jit(solution)/shard_map/ppermute | solution.py:270
  133.2 14.5 %collective-permute-start.21 = (bf16[768,512]{1,0:T(8,128)(2,1)S(1)}, bf16[768,512]{1,0:T(8,128)(2,1)S(1)}, u32[]{:S(2)}, u32[]{:S(2)}) collective-permute-start(bf16[768,512]{1,0:T(8,128)(2,1)S(1)} %collective-permute-done.20.refs_5_), channel_id=1, source_target_pairs={{0,4},{4,0},{8,12},{12,8},{16,20},{20,16},{24,28},{28,24},{1,5},{5... | collective-permute-start | bytes 2359304 | tf_op jit(solution)/shard_map/ppermute | solution.py:265
  133.5 19.1 %collective-permute-start.24 = (bf16[768,512]{1,0:T(8,128)(2,1)S(1)}, bf16[768,512]{1,0:T(8,128)(2,1)S(1)}, u32[]{:S(2)}, u32[]{:S(2)}) collective-permute-start(bf16[768,512]{1,0:T(8,128)(2,1)S(1)} %collective-permute-done.20.refs_5_), channel_id=1, source_target_pairs={{0,16},{4,12},{8,24},{12,4},{16,0},{20,28},{24,8},{28,20},{1,17},{... | collective-permute-start | bytes 2359304 | tf_op jit(solution)/shard_map/ppermute | solution.py:270
  134.8 13.7 %collective-permute-start.23 = (bf16[768,512]{1,0:T(8,128)(2,1)S(1)}, bf16[768,512]{1,0:T(8,128)(2,1)S(1)}, u32[]{:S(2)}, u32[]{:S(2)}) collective-permute-start(bf16[768,512]{1,0:T(8,128)(2,1)S(1)} %collective-permute-done.22.refs_7_), channel_id=1, source_target_pairs={{0,4},{4,0},{8,12},{12,8},{16,20},{20,16},{24,28},{28,24},{1,5},{5... | collective-permute-start | bytes 2359304 | tf_op jit(solution)/shard_map/ppermute | solution.py:265
  134.9 12.3 %copy-start.3 = (bf16[512,512]{1,0:T(8,128)(2,1)S(1)}, bf16[512,512]{1,0:T(8,128)(2,1)}, u32[]{:S(2)}) copy-start(bf16[512,512]{1,0:T(8,128)(2,1)} %copy-done.2) | copy-start | bytes 1572868
  134.9 13.6 %copy-start.7 = (bf16[512,512]{1,0:T(8,128)(2,1)S(1)}, bf16[512,512]{1,0:T(8,128)(2,1)}, u32[]{:S(2)}) copy-start(bf16[512,512]{1,0:T(8,128)(2,1)} %copy-done.6) | copy-start | bytes 1572868
  147.2 11.6 %collective-permute-start.9 = (bf16[512,512]{1,0:T(8,128)(2,1)S(1)}, bf16[512,512]{1,0:T(8,128)(2,1)S(1)}, u32[]{:S(2)}, u32[]{:S(2)}) collective-permute-start(bf16[512,512]{1,0:T(8,128)(2,1)S(1)} %copy-done.3), channel_id=1, source_target_pairs={{0,4},{4,0},{8,12},{12,8},{16,20},{20,16},{24,28},{28,24},{1,5},{5... | collective-permute-start | bytes 1572872 | tf_op jit(solution)/shard_map/ppermute | solution.py:265
  147.7 11.3 %collective-permute-start.12 = (bf16[512,512]{1,0:T(8,128)(2,1)S(1)}, bf16[512,512]{1,0:T(8,128)(2,1)S(1)}, u32[]{:S(2)}, u32[]{:S(2)}) collective-permute-start(bf16[512,512]{1,0:T(8,128)(2,1)S(1)} %copy-done.3), channel_id=1, source_target_pairs={{0,16},{4,12},{8,24},{12,4},{16,0},{20,28},{24,8},{28,20},{1,17},{... | collective-permute-start | bytes 1572872 | tf_op jit(solution)/shard_map/ppermute | solution.py:270
  148.5 11.0 %collective-permute-start.11 = (bf16[512,512]{1,0:T(8,128)(2,1)}, bf16[512,512]{1,0:T(8,128)(2,1)S(1)}, u32[]{:S(2)}, u32[]{:S(2)}) collective-permute-start(bf16[512,512]{1,0:T(8,128)(2,1)} %collective-permute-done.10.refs_7_), channel_id=1, source_target_pairs={{0,4},{4,0},{8,12},{12,8},{16,20},{20,16},{24,28},{28,24},{1,5},{5... | collective-permute-start | bytes 1572872 | tf_op jit(solution)/shard_map/ppermute | solution.py:265
  152.6 16.5 %collective-permute-start.25 = (bf16[768,512]{1,0:T(8,128)(2,1)S(1)}, bf16[768,512]{1,0:T(8,128)(2,1)S(1)}, u32[]{:S(2)}, u32[]{:S(2)}) collective-permute-start(bf16[768,512]{1,0:T(8,128)(2,1)S(1)} %collective-permute-done.24.refs_2_), channel_id=1, source_target_pairs={{0,4},{4,0},{8,12},{12,8},{16,20},{20,16},{24,28},{28,24},{1,5},{5... | collective-permute-start | bytes 2359304 | tf_op jit(solution)/shard_map/ppermute | solution.py:265
  158.8 13.0 %collective-permute-start.19 = (bf16[512,512]{1,0:T(8,128)(2,1)S(1)}, bf16[512,512]{1,0:T(8,128)(2,1)S(1)}, u32[]{:S(2)}, u32[]{:S(2)}) collective-permute-start(bf16[512,512]{1,0:T(8,128)(2,1)S(1)} %collective-permute-done.18.refs_2_), channel_id=1, source_target_pairs={{0,4},{4,0},{8,12},{12,8},{16,20},{20,16},{24,28},{28,24},{1,5},{5... | collective-permute-start | bytes 1572872 | tf_op jit(solution)/shard_map/ppermute | solution.py:265
  158.9 14.9 %collective-permute-start.13 = (bf16[512,512]{1,0:T(8,128)(2,1)S(1)}, bf16[512,512]{1,0:T(8,128)(2,1)S(1)}, u32[]{:S(2)}, u32[]{:S(2)}) collective-permute-start(bf16[512,512]{1,0:T(8,128)(2,1)S(1)} %collective-permute-done.12.refs_2_), channel_id=1, source_target_pairs={{0,4},{4,0},{8,12},{12,8},{16,20},{20,16},{24,28},{28,24},{1,5},{5... | collective-permute-start | bytes 1572872 | tf_op jit(solution)/shard_map/ppermute | solution.py:265

commit v3 on v2

--- a/solution.py
+++ b/solution.py
@@ -71,9 +71,9 @@
         out_ref[:, here] = total
 
 
-def product(tokens, start, length, tile, rows, blocks, low=None, bank_out=None, partial=None, hidden=None, resident=False):
+def product(tokens, start, length, tile, rows, blocks, low=None, bank_out=None, partial=None, final=False, hidden=None, resident=False):
     lines = tokens.shape[0]
-    base, final = start // tile, partial is not None
+    base = start // tile
     specs, operands, depth_sum = [pl.BlockSpec(memory_space=pltpu.VMEM)], [tokens], 0
 
     def add(operand, spec):
@@ -83,7 +83,10 @@
     if low is not None:
         add(low, pl.BlockSpec(memory_space=pltpu.VMEM))
         add(bank_out, pl.BlockSpec((tile, bank_out.shape[1]), lambda i: (base + i, 0)))
-    if final:
+    aliases = {}
+    if partial is not None:
+        if not final:
+            aliases = {len(operands): 0}
         add(partial, pl.BlockSpec(memory_space=pltpu.VMEM))
     for _, block, first in blocks:
         depth = block.shape[1]
@@ -92,7 +95,6 @@
             add(block, pl.BlockSpec(memory_space=pltpu.VMEM))
         else:
             add(block, pl.BlockSpec((tile, depth), functools.partial(lambda i, skip: (skip + i, 0), skip=first // tile)))
-    aliases = {}
     if hidden is not None:
         aliases = {len(operands): 0}
         add(hidden, pl.BlockSpec(memory_space=pl.ANY))
@@ -102,7 +104,7 @@
         refs = list(refs)
         if hidden is not None:
             refs.pop(-2)
-        product_kernel(places, tile, low is not None, final, final, resident, *refs)
+        product_kernel(places, tile, low is not None, partial is not None, final, resident, *refs)
 
     if final:
         out_shape = jax.ShapeDtypeStruct((lines, rows), jnp.bfloat16)
@@ -273,15 +275,16 @@
 
     held = {}
     if planned:
+        held[two] = send(weight, two)
         early = take(weight, chunks[1:2])
         late = take(weight, chunks[:1] + chunks[2:])
         own = [late[0], early[0], *late[1:]]
         partner = flip(weight, core)
+        held[two | core] = flip(held[two], core)
         for c, piece in enumerate(own):
             held[c, one] = send(piece, one)
-            held[c, two] = send(piece, two)
             held[c, one | two] = send(held[c, one], two)
-            for mask in (one, two, one | two):
+            for mask in (one, one | two):
                 held[c, mask | core] = flip(held[c, mask], core)
         both = jnp.concatenate([packed, flip(packed, core)], axis=0)
         side = send(both, one)
@@ -327,11 +330,13 @@
     if planned:
         hidden, partial = None, []
         for c, (start, length) in enumerate(chunks):
-            near = [(0, weight, start), (core, partner, start)] + [(m, held[c, m], 0) for m in range(2, 6)]
-            partial.append(product(flat_tokens, start, length, tile, rows, near, low=low, bank_out=bank_out))
+            near = [(0, weight, start), (core, partner, start)] + [(m, held[c, m], 0) for m in (one, one | core)]
+            part = product(flat_tokens, start, length, tile, rows, near, low=low, bank_out=bank_out)
+            side = [(m, held[m], start) for m in (two, two | core)]
+            partial.append(product(flat_tokens, start, length, tile, rows, side, partial=part))
         for c, (start, length) in enumerate(chunks):
             far = [(m, held[c, m], 0) for m in (6, 7)]
-            hidden = product(flat_tokens, start, length, tile, rows, far, partial=partial[c], hidden=hidden, resident=c > 1)
+            hidden = product(flat_tokens, start, length, tile, rows, far, partial=partial[c], final=True, hidden=hidden, resident=c > 1)
     else:
         blocks = {0: weight}
         for bit in range((pops - 1).bit_length()):

time: 176 us -> 202 us (1.15)
  waiting for transfers between devices: 83.6 us -> 105 us
  Pallas kernels: 52.9 us -> 63.1 us
  starting transfers between devices: 29.2 us -> 24.9 us
  local copies, waits for them, and re-layouts: 6.72 us -> 4.67 us
    ppermute x13 -> x10, waiting for transfers between devices: 60.1 us -> 76.3 us  [send(): lax.ppermute(block, 'pop', [(i, i ^ (axis ^ (one | two) if i & core else...]
    pallas_call x8 -> x12, Pallas kernels: 38.4 us -> 49.6 us  [product(): pl.pallas_call(kernel, grid=(length // tile,), in_specs=specs, out_specs=...]
    ppermute x15 -> x12, waiting for transfers between devices: 2.78 us -> 6.37 us  [flip(): return lax.ppermute(block, 'pop', [(i, i ^ mask) for i in range(pops)])]
    unnamed x43 -> x33, local copies, waits for them, and re-layouts: 5.9 us -> 3.85 us
    ppermute x13 -> x10, starting transfers between devices: 13.7 us -> 11.8 us  [send(): lax.ppermute(block, 'pop', [(i, i ^ (axis ^ (one | two) if i & core else...]
    ppermute x15 -> x12, starting transfers between devices: 4.37 us -> 2.9 us  [flip(): return lax.ppermute(block, 'pop', [(i, i ^ mask) for i in range(pops)])]
  transfers between devices with their start and end apart: 32 -> 26, of which waited for: 10 -> 9; matrix products, arithmetic and copies ran while one was open for 2% -> 2% of each run, Pallas kernels for 28% -> 30%
where the time goes in v3:
time: 202 us; the launch traced here: 201 us
  waiting for transfers between devices  105 us (52%)
  Pallas kernels  63.1 us (31%)
  starting transfers between devices  24.9 us (12%)
  local copies, waits for them, and re-layouts  4.67 us (2%)
    ppermute x10, waiting for transfers between devices, send(): lax.ppermute(block, 'pop', [(i, i ^ (axis ^ (one | two) if i & core else...  76.3 us
    pallas_call x12, Pallas kernels, product(): pl.pallas_call(kernel, grid=(length // tile,), in_specs=specs, out_specs=...  49.6 us
    ppermute x3, waiting for transfers between devices, shards(): lax.ppermute(bank_in, 'row', [(i, (i - step) % lanes) for i in range(lane...  19 us
    ppermute x10, starting transfers between devices, send(): lax.ppermute(block, 'pop', [(i, i ^ (axis ^ (one | two) if i & core else...  11.8 us
    ppermute x3, starting transfers between devices, shards(): lax.ppermute(bank_in, 'row', [(i, (i - step) % lanes) for i in range(lane...  6.88 us
    ppermute x12, waiting for transfers between devices, flip(): return lax.ppermute(block, 'pop', [(i, i ^ mask) for i in range(pops)])  6.37 us
    pallas_call x1, Pallas kernels, updated(): pl.pallas_call(update_kernel, grid=(rows // tile,), in_specs=[pl.BlockSpe...  5.33 us
  transfers between devices with their start and end apart: 26, of which 9 were waited for; matrix products, arithmetic and copies ran while one was open for 2% of the time, Pallas kernels for 30%

profile of v3, /device:TPU:0, one launch (start us, length us, event | category | flops | bytes accessed | tf_op | source)
XLA Modules:
  0.0 200.9 jit_solution(12357429227232627327)
XLA Ops:
  0.7 3.1 %collective-permute-start.10 = (bf16[3584,512]{1,0:T(8,128)(2,1)}, bf16[3584,512]{1,0:T(8,128)(2,1)}, u32[]{:S(2)}, u32[]{:S(2)}) collective-permute-start(bf16[3584,512]{1,0:T(8,128)(2,1)} %weight_ref.1), channel_id=1, source_target_pairs={{0,16},{4,12},{8,24},{12,4},{16,0},{20,28},{24,8},{28,20},{1,17},{... | collective-permute-start | bytes 11010056 | tf_op jit(solution)/shard_map/ppermute | solution.py:272
  3.7 1.8 shard_map.86
  5.6 1.6 collective-permute-start.22
  7.1 0.6 collective-permute-start.3
  7.7 3.6 %collective-permute-start = (bf16[1024,128]{1,0:T(8,128)(2,1)S(1)}, bf16[1024,128]{1,0:T(8,128)(2,1)S(1)}, u32[]{:S(2)}, u32[]{:S(2)}) collective-permute-start(bf16[1024,128]{1,0:T(8,128)(2,1)S(1)} %copy-done.4), channel_id=1, source_target_pairs={{0,3},{1,0},{2,1},{3,2},{4,7},{5,4},{6,5},{7,6},{8,11},{9,8},{10,9... | collective-permute-start | bytes 786440 | tf_op jit(solution)/shard_map/ppermute | solution.py:316
  11.3 2.6 %collective-permute-done.3 = s32[48,17]{0,1:T(8,128)S(1)} collective-permute-done((s32[48,17]{0,1:T(8,128)S(1)}, s32[48,17]{0,1:T(8,128)S(1)}, u32[]{:S(2)}, u32[]{:S(2)}) %collective-permute-start.3) | collective-permute-done | bytes 3296 | tf_op jit(solution)/shard_map/ppermute | solution.py:267
  13.9 0.1 pad_add_fusion.2
  13.9 0.5 collective-permute-start.4
  14.5 34.3 %collective-permute-done.4 = s32[96,17]{0,1:T(8,128)S(1)} collective-permute-done((s32[96,17]{0,1:T(8,128)S(1)}, s32[96,17]{0,1:T(8,128)S(1)}, u32[]{:S(2)}, u32[]{:S(2)}) %collective-permute-start.4) | collective-permute-done | bytes 6560 | tf_op jit(solution)/shard_map/ppermute | solution.py:272
  48.8 3.3 %collective-permute-start.5 = (s32[96,17]{0,1:T(8,128)S(1)}, s32[96,17]{0,1:T(8,128)S(1)}, u32[]{:S(2)}, u32[]{:S(2)}) collective-permute-start(s32[96,17]{0,1:T(8,128)S(1)} %pad_add_fusion.2), channel_id=1, source_target_pairs={{0,24},{8,16},{16,8},{24,0},{1,25},{9,17},{17,9},{25,1},{2,26},{10... | collective-permute-start | bytes 19592 | tf_op jit(solution)/shard_map/ppermute | solution.py:291
  52.1 3.3 %collective-permute-done.5 = s32[96,17]{0,1:T(8,128)S(1)} collective-permute-done((s32[96,17]{0,1:T(8,128)S(1)}, s32[96,17]{0,1:T(8,128)S(1)}, u32[]{:S(2)}, u32[]{:S(2)}) %collective-permute-start.5) | collective-permute-done | bytes 6560 | tf_op jit(solution)/shard_map/ppermute | solution.py:291
  55.4 0.1 pad_add_fusion
  55.5 0.0 collective-permute-start.6
  55.5 1.2 collective-permute-done.6
  56.7 2.6 %collective-permute-start.1 = (bf16[1024,128]{1,0:T(8,128)(2,1)S(1)}, bf16[1024,128]{1,0:T(8,128)(2,1)S(1)}, u32[]{:S(2)}, u32[]{:S(2)}) collective-permute-start(bf16[1024,128]{1,0:T(8,128)(2,1)S(1)} %copy-done.4), channel_id=1, source_target_pairs={{0,2},{1,3},{2,0},{3,1},{4,6},{5,7},{6,4},{7,5},{8,10},{9,11},{10,... | collective-permute-start | bytes 786440 | tf_op jit(solution)/shard_map/ppermute | solution.py:316
  59.3 1.5 collective-permute-start.14
  60.7 10.8 %collective-permute-done.1.refs_2_ = bf16[1024,128]{1,0:T(8,128)(2,1)S(1)} collective-permute-done((bf16[1024,128]{1,0:T(8,128)(2,1)S(1)}, bf16[1024,128]{1,0:T(8,128)(2,1)S(1)}, u32[]{:S(2)}, u32[]{:S(2)}) %collective-permute-start.1) | collective-permute-done | bytes 262176 | tf_op jit(solution)/shard_map/ppermute | solution.py:316
  71.5 0.7 collective-permute-start.2
  72.2 1.1 shard_map.91
  73.4 8.1 %collective-permute-done.2.refs_3_ = bf16[1024,128]{1,0:T(8,128)(2,1)S(1)} collective-permute-done((bf16[1024,128]{1,0:T(8,128)(2,1)S(1)}, bf16[1024,128]{1,0:T(8,128)(2,1)S(1)}, u32[]{:S(2)}, u32[]{:S(2)}) %collective-permute-start.2) | collective-permute-done | bytes 262176 | tf_op jit(solution)/shard_map/ppermute | solution.py:316
  81.6 0.7 copy-done.9
  82.3 1.5 collective-permute-start.18
  83.8 0.5 collective-permute-start.8
  84.3 15.6 %collective-permute-done.8.refs_5_ = bf16[512,512]{1,0:T(8,128)(2,1)S(1)} collective-permute-done((bf16[512,512]{1,0:T(8,128)(2,1)S(1)}, bf16[512,512]{1,0:T(8,128)(2,1)S(1)}, u32[]{:S(2)}, u32[]{:S(2)}) %collective-permute-start.8) | collective-permute-done | bytes 524320 | tf_op jit(solution)/shard_map/ppermute | solution.py:272
  99.9 0.6 collective-permute-start.24
  100.5 0.2 copy-done.2
  100.7 1.3 collective-permute-start.16
  102.0 0.1 copy.17.seeds_ref
  102.1 0.0 collective-permute-done.15.refs_6_
  102.1 0.1 collective-permute-start.9
  102.3 0.1 pad_add_fusion.3.pick_ref
  102.4 26.4 %collective-permute-done.16.refs_2_ = bf16[512,512]{1,0:T(8,128)(2,1)S(1)} collective-permute-done((bf16[512,512]{1,0:T(8,128)(2,1)}, bf16[512,512]{1,0:T(8,128)(2,1)S(1)}, u32[]{:S(2)}, u32[]{:S(2)}) %collective-permute-start.16) | collective-permute-done | bytes 524320 | tf_op jit(solution)/shard_map/ppermute | solution.py:272
  128.8 0.6 slice_add_fusion
  129.4 0.8 concatenate.20
  130.2 0.0 copy-start.6
  130.3 0.6 collective-permute-start.19
  130.8 0.3 convert_reduce_fusion
  131.1 2.6 %collective-permute-done.19.refs_6_ = bf16[768,512]{1,0:T(8,128)(2,1)S(1)} collective-permute-done((bf16[768,512]{1,0:T(8,128)(2,1)S(1)}, bf16[768,512]{1,0:T(8,128)(2,1)S(1)}, u32[]{:S(2)}, u32[]{:S(2)}) %collective-permute-start.19) | collective-permute-done | bytes 786464 | tf_op jit(solution)/shard_map/ppermute | solution.py:267
  133.7 0.5 collective-permute-start.20
  134.2 0.8 collective-permute-start.25
  135.1 1.3 fusion.2.coupling_ref
  136.4 0.0 copy-start
  136.4 2.8 %copy-done = bf16[48,16,4096]{2,1,0:T(8,128)(2,1)S(1)} copy-done((bf16[48,16,4096]{2,1,0:T(8,128)(2,1)S(1)}, bf16[48,16,4096]{2,1,0:T(8,128)(2,1)}, u32[]{:S(2)}) %copy-start) | copy-done | bytes 6291480
  139.2 2.9 %project.1 = (f32[768,128]{1,0:T(8,128)S(1)}, bf16[512,128]{1,0:T(8,128)(2,1)S(1)}) custom-call(s32[6]{0:T(128)S(1)} %pad_add_fusion.3.pick_ref, bf16[768,4096]{1,0:T(8,128)(2,1)S(1)} %bitcast.14, bf16[1024,128]{1,0:T(8,128)(2,1)S(1)} %copy-done.4, bf16[1024,128]{1,0:T(8,128)(2,1)S(1)} %copy-done.6, bf16[1024,128]{1,0:T(8,128)(2,1)S(1)} %copy-done.8, ...), custom_call_target="tpu_custom_call" | custom-call | flops 805306368 | bytes 6291456 | tf_op jit(solution)/shard_map/project/pallas_call | solution.py:204
  142.1 2.3 %lowrank.1 = (bf16[768,256]{1,0:T(8,128)(2,1)S(1)}, bf16[256,512]{1,0:T(8,128)(2,1)S(1)}) custom-call(f32[768,128]{1,0:T(8,128)S(1)} %get-tuple-element.9.projected_ref, f32[128,128]{1,0:T(8,128)S(1)} %fusion.2.coupling_ref, s32[48,2,8]{2,1,0:T(2,128)S(1)} %copy.17.seeds_ref, bf16[512,128]{1,0:T(8,128)(2,1)S(1)} %get-tuple-element.10.columns_ref), custom_call_target="tpu_custom_call" | custom-call | flops 251658240 | bytes 786432 | tf_op jit(solution)/shard_map/lowrank/pallas_call | solution.py:244
  144.4 0.0 copy-start.3
  144.4 0.0 slice-start.1
  144.4 5.3 %update.1 = bf16[3584,512]{1,0:T(8,128)(2,1)} custom-call(bf16[3584,512]{1,0:T(8,128)(2,1)} %weight_ref.1, bf16[3584,128]{1,0:T(8,128)(2,1)S(1)} %copy-done.1, bf16[256,512]{1,0:T(8,128)(2,1)S(1)} %get-tuple-element.15.right_ref), custom_call_target="tpu_custom_call" | custom-call | flops 939524096 | bytes 7340032 | tf_op jit(solution)/shard_map/update/pallas_call | solution.py:167
  149.8 0.7 collective-permute-start.12
  150.5 3.5 %shard_map.89.refs_1_ = f32[768,512]{1,0:T(8,128)S(1)} custom-call(bf16[768,4096]{1,0:T(8,128)(2,1)S(1)} %bitcast.17, bf16[768,256]{1,0:T(8,128)(2,1)S(1)} %get-tuple-element.11.refs_1_, bf16[3584,128]{1,0:T(8,128)(2,1)S(1)} %copy-done.1, bf16[3584,512]{1,0:T(8,128)(2,1)} %weight_ref.1, bf16[3584,512]{1,0:T(8,128)(2,1)} %collective-permute-done.7.refs_4_, ...), custom_call_target="tpu_custom_call" | custom-call | flops 1610612736 | bytes 6029312 | tf_op jit(solution)/shard_map/pallas_call | solution.py:115
  154.0 3.4 %shard_map.87.refs_1_ = f32[768,512]{1,0:T(8,128)S(1)} custom-call(bf16[768,4096]{1,0:T(8,128)(2,1)S(1)} %bitcast.18, bf16[768,256]{1,0:T(8,128)(2,1)S(1)} %get-tuple-element.11.refs_1_, bf16[3584,128]{1,0:T(8,128)(2,1)S(1)} %copy-done.1, bf16[3584,512]{1,0:T(8,128)(2,1)} %weight_ref.1, bf16[3584,512]{1,0:T(8,128)(2,1)} %collective-permute-done.7.refs_4_, ...), custom_call_target="tpu_custom_call" | custom-call | flops 1610612736 | bytes 6029312 | tf_op jit(solution)/shard_map/pallas_call | solution.py:115
  157.4 4.4 %shard_map.92.refs_1_ = f32[768,768]{1,0:T(8,128)S(1)} custom-call(bf16[768,4096]{1,0:T(8,128)(2,1)S(1)} %bitcast.19, bf16[768,256]{1,0:T(8,128)(2,1)S(1)} %get-tuple-element.11.refs_1_, bf16[3584,128]{1,0:T(8,128)(2,1)S(1)} %copy-done.1, bf16[3584,512]{1,0:T(8,128)(2,1)} %weight_ref.1, bf16[3584,512]{1,0:T(8,128)(2,1)} %collective-permute-done.7.refs_4_, ...), custom_call_target="tpu_custom_call" | custom-call | flops 2415919104 | bytes 7471104 | tf_op jit(solution)/shard_map/pallas_call | solution.py:115
  161.8 0.3 collective-permute-start.17
  162.1 0.3 collective-permute-start.13
  162.4 0.2 collective-permute-start.21
  162.6 9.0 %shard_map.94.refs_1_ = f32[768,1792]{1,0:T(8,128)S(1)} custom-call(bf16[768,4096]{1,0:T(8,128)(2,1)S(1)} %bitcast.20, bf16[768,256]{1,0:T(8,128)(2,1)S(1)} %get-tuple-element.11.refs_1_, bf16[3584,128]{1,0:T(8,128)(2,1)S(1)} %copy-done.1, bf16[3584,512]{1,0:T(8,128)(2,1)} %weight_ref.1, bf16[3584,512]{1,0:T(8,128)(2,1)} %collective-permute-done.7.refs_4_, ...), custom_call_target="tpu_custom_call" | custom-call | flops 5637144576 | bytes 13238272 | tf_op jit(solution)/shard_map/pallas_call | solution.py:115
  171.6 3.4 %shard_map.93.refs_1_ = f32[768,768]{1,0:T(8,128)S(1)} custom-call(bf16[768,4096]{1,0:T(8,128)(2,1)S(1)} %bitcast.21, f32[768,768]{1,0:T(8,128)S(1)} %shard_map.92.refs_1_, bf16[3584,512]{1,0:T(8,128)(2,1)} %collective-permute-done.10.refs_2_, bf16[3584,512]{1,0:T(8,128)(2,1)} %collective-permute-done.11.refs_3_), custom_call_target="tpu_custom_call", output_to_operand_aliasing={{}: (1, {})} | custom-call | flops 1207959552 | bytes 4325376 | tf_op jit(solution)/shard_map/pallas_call | solution.py:115
  175.1 6.9 %shard_map.95.refs_1_ = f32[768,1792]{1,0:T(8,128)S(1)} custom-call(bf16[768,4096]{1,0:T(8,128)(2,1)S(1)} %bitcast.22, f32[768,1792]{1,0:T(8,128)S(1)} %shard_map.94.refs_1_, bf16[3584,512]{1,0:T(8,128)(2,1)} %collective-permute-done.10.refs_2_, bf16[3584,512]{1,0:T(8,128)(2,1)} %collective-permute-done.11.refs_3_), custom_call_target="tpu_custom_call", output_to_operand_aliasing={{}: (1, {})} | custom-call | flops 2818572288 | bytes 7995392 | tf_op jit(solution)/shard_map/pallas_call | solution.py:115
  181.9 2.4 %shard_map.90.refs_1_ = f32[768,512]{1,0:T(8,128)S(1)} custom-call(bf16[768,4096]{1,0:T(8,128)(2,1)S(1)} %bitcast.23, f32[768,512]{1,0:T(8,128)S(1)} %shard_map.89.refs_1_, bf16[3584,512]{1,0:T(8,128)(2,1)} %collective-permute-done.10.refs_2_, bf16[3584,512]{1,0:T(8,128)(2,1)} %collective-permute-done.11.refs_3_), custom_call_target="tpu_custom_call", output_to_operand_aliasing={{}: (1, {})} | custom-call | flops 805306368 | bytes 3407872 | tf_op jit(solution)/shard_map/pallas_call | solution.py:115
  184.4 2.4 %shard_map.88.refs_1_ = f32[768,512]{1,0:T(8,128)S(1)} custom-call(bf16[768,4096]{1,0:T(8,128)(2,1)S(1)} %bitcast.24, f32[768,512]{1,0:T(8,128)S(1)} %shard_map.87.refs_1_, bf16[3584,512]{1,0:T(8,128)(2,1)} %collective-permute-done.10.refs_2_, bf16[3584,512]{1,0:T(8,128)(2,1)} %collective-permute-done.11.refs_3_), custom_call_target="tpu_custom_call", output_to_operand_aliasing={{}: (1, {})} | custom-call | flops 805306368 | bytes 3407872 | tf_op jit(solution)/shard_map/pallas_call | solution.py:115
  186.8 7.5 %shard_map.96.refs_4_ = bf16[768,3584]{1,0:T(8,128)(2,1)} custom-call(bf16[768,4096]{1,0:T(8,128)(2,1)S(1)} %bitcast.25, f32[768,1792]{1,0:T(8,128)S(1)} %shard_map.95.refs_1_, bf16[1792,512]{1,0:T(8,128)(2,1)} %collective-permute-done.24.refs_2_, bf16[1792,512]{1,0:T(8,128)(2,1)S(1)} %collective-permute-done.25.refs_3_), custom_call_target="tpu_custom_call" | custom-call | flops 2818572288 | bytes 7995392 | tf_op jit(solution)/shard_map/pallas_call | solution.py:115
  194.2 2.7 %shard_map.97.refs_4_ = bf16[768,3584]{1,0:T(8,128)(2,1)} custom-call(bf16[768,4096]{1,0:T(8,128)(2,1)S(1)} %bitcast.26, f32[768,768]{1,0:T(8,128)S(1)} %shard_map.93.refs_1_, bf16[768,512]{1,0:T(8,128)(2,1)S(1)} %collective-permute-done.20.refs_2_, bf16[768,512]{1,0:T(8,128)(2,1)S(1)} %collective-permute-done.21.refs_3_, ...), custom_call_target="tpu_custom_call", output_to_operand_aliasing={{}: (4, {})} | custom-call | flops 1207959552 | bytes 4325376 | tf_op jit(solution)/shard_map/pallas_call | solution.py:115
  197.0 2.0 shard_map.98.refs_4_
  199.0 2.0 shard_map.99
  (52 shorter events, 0.2 us)
Async XLA Ops:
  0.6 6.5 %copy-start.13 = (s32[48]{0:T(128)S(1)}, s32[48]{0:T(128)}, u32[]{:S(2)}) copy-start(s32[48]{0:T(128)} %param.11) | copy-start | bytes 580
  0.6 6.5 %copy-start.11 = (s32[48,2,8]{0,2,1:T(8,128)S(1)}, s32[48,2,8]{0,2,1:T(8,128)}, u32[]{:S(2)}) copy-start(s32[48,2,8]{0,2,1:T(8,128)} %param.12) | copy-start | bytes 9220
  0.7 7.1 %copy-start.4 = (bf16[1024,128]{1,0:T(8,128)(2,1)S(1)}, bf16[1024,128]{1,0:T(8,128)(2,1)}, u32[]{:S(2)}) copy-start(bf16[1024,128]{1,0:T(8,128)(2,1)} %refs_0_.1) | copy-start | bytes 786436
  0.7 83.6 %collective-permute-start.10 = (bf16[3584,512]{1,0:T(8,128)(2,1)}, bf16[3584,512]{1,0:T(8,128)(2,1)}, u32[]{:S(2)}, u32[]{:S(2)}) collective-permute-start(bf16[3584,512]{1,0:T(8,128)(2,1)} %weight_ref.1), channel_id=1, source_target_pairs={{0,16},{4,12},{8,24},{12,4},{16,0},{20,28},{24,8},{28,20},{1,17},{... | collective-permute-start | bytes 11010056 | tf_op jit(solution)/shard_map/ppermute | solution.py:272
  5.6 94.3 %collective-permute-start.22 = (bf16[1792,512]{1,0:T(8,128)(2,1)S(1)}, bf16[1792,512]{1,0:T(8,128)(2,1)S(1)}, u32[]{:S(2)}, u32[]{:S(2)}) collective-permute-start(bf16[1792,512]{1,0:T(8,128)(2,1)S(1)} %get-tuple-element.14), channel_id=1, source_target_pairs={{0,8},{4,20},{8,0},{12,28},{16,24},{20,4},{24,16},{28,12},{1,9},{5... | collective-permute-start | bytes 5505032 | tf_op jit(solution)/shard_map/ppermute | solution.py:272
  7.1 142.7 %collective-permute-start.7 = (bf16[3584,512]{1,0:T(8,128)(2,1)}, bf16[3584,512]{1,0:T(8,128)(2,1)}, u32[]{:S(2)}, u32[]{:S(2)}) collective-permute-start(bf16[3584,512]{1,0:T(8,128)(2,1)} %weight_ref.1), channel_id=1, source_target_pairs={{0,4},{4,0},{8,12},{12,8},{16,20},{20,16},{24,28},{28,24},{1,5},{5... | collective-permute-start | bytes 11010056 | tf_op jit(solution)/shard_map/ppermute | solution.py:267
  7.1 6.7 %collective-permute-start.3 = (s32[48,17]{0,1:T(8,128)S(1)}, s32[48,17]{0,1:T(8,128)S(1)}, u32[]{:S(2)}, u32[]{:S(2)}) collective-permute-start(s32[48,17]{0,1:T(8,128)S(1)} %pad_add_fusion.1), channel_id=1, source_target_pairs={{0,4},{4,0},{8,12},{12,8},{16,20},{20,16},{24,28},{28,24},{1,5},{5... | collective-permute-start | bytes 9800 | tf_op jit(solution)/shard_map/ppermute | solution.py:267
  7.7 51.5 %collective-permute-start = (bf16[1024,128]{1,0:T(8,128)(2,1)S(1)}, bf16[1024,128]{1,0:T(8,128)(2,1)S(1)}, u32[]{:S(2)}, u32[]{:S(2)}) collective-permute-start(bf16[1024,128]{1,0:T(8,128)(2,1)S(1)} %copy-done.4), channel_id=1, source_target_pairs={{0,3},{1,0},{2,1},{3,2},{4,7},{5,4},{6,5},{7,6},{8,11},{9,8},{10,9... | collective-permute-start | bytes 786440 | tf_op jit(solution)/shard_map/ppermute | solution.py:316
  13.9 34.8 %collective-permute-start.4 = (s32[96,17]{0,1:T(8,128)S(1)}, s32[96,17]{0,1:T(8,128)S(1)}, u32[]{:S(2)}, u32[]{:S(2)}) collective-permute-start(s32[96,17]{0,1:T(8,128)S(1)} %pad_add_fusion.2), channel_id=1, source_target_pairs={{0,8},{4,20},{8,0},{12,28},{16,24},{20,4},{24,16},{28,12},{1,9},{5... | collective-permute-start | bytes 19592 | tf_op jit(solution)/shard_map/ppermute | solution.py:272
  48.8 6.6 %collective-permute-start.5 = (s32[96,17]{0,1:T(8,128)S(1)}, s32[96,17]{0,1:T(8,128)S(1)}, u32[]{:S(2)}, u32[]{:S(2)}) collective-permute-start(s32[96,17]{0,1:T(8,128)S(1)} %pad_add_fusion.2), channel_id=1, source_target_pairs={{0,24},{8,16},{16,8},{24,0},{1,25},{9,17},{17,9},{25,1},{2,26},{10... | collective-permute-start | bytes 19592 | tf_op jit(solution)/shard_map/ppermute | solution.py:291
  55.5 1.2 collective-permute-start.6
  56.7 14.9 %collective-permute-start.1 = (bf16[1024,128]{1,0:T(8,128)(2,1)S(1)}, bf16[1024,128]{1,0:T(8,128)(2,1)S(1)}, u32[]{:S(2)}, u32[]{:S(2)}) collective-permute-start(bf16[1024,128]{1,0:T(8,128)(2,1)S(1)} %copy-done.4), channel_id=1, source_target_pairs={{0,2},{1,3},{2,0},{3,1},{4,6},{5,7},{6,4},{7,5},{8,10},{9,11},{10,... | collective-permute-start | bytes 786440 | tf_op jit(solution)/shard_map/ppermute | solution.py:316
  59.3 14.1 %copy-start.5 = (bf16[1024,128]{1,0:T(8,128)(2,1)}, bf16[1024,128]{1,0:T(8,128)(2,1)S(1)}, u32[]{:S(2)}) copy-start(bf16[1024,128]{1,0:T(8,128)(2,1)S(1)} %collective-permute-done.refs_1_) | copy-start | bytes 786436
  59.3 42.7 %copy-start.12 = (s32[48,2,8]{0,2,1:T(8,128)S(1)}, s32[48,2,8]{0,2,1:T(8,128)}, u32[]{:S(2)}) copy-start(s32[48,2,8]{0,2,1:T(8,128)} %param.13) | copy-start | bytes 9220
  59.3 24.5 %collective-permute-start.14 = (bf16[512,512]{1,0:T(8,128)(2,1)S(1)}, bf16[512,512]{1,0:T(8,128)(2,1)}, u32[]{:S(2)}, u32[]{:S(2)}) collective-permute-start(bf16[512,512]{1,0:T(8,128)(2,1)S(1)} %get-tuple-element.13), channel_id=1, source_target_pairs={{0,8},{4,20},{8,0},{12,28},{16,24},{20,4},{24,16},{28,12},{1,9},{5... | collective-permute-start | bytes 1572872 | tf_op jit(solution)/shard_map/ppermute | solution.py:272
  71.5 1.8 copy-start.7
  71.5 10.0 %collective-permute-start.2 = (bf16[1024,128]{1,0:T(8,128)(2,1)S(1)}, bf16[1024,128]{1,0:T(8,128)(2,1)S(1)}, u32[]{:S(2)}, u32[]{:S(2)}) collective-permute-start(bf16[1024,128]{1,0:T(8,128)(2,1)S(1)} %copy-done.4), channel_id=1, source_target_pairs={{0,1},{1,2},{2,3},{3,0},{4,5},{5,6},{6,7},{7,4},{8,9},{9,10},{10,1... | collective-permute-start | bytes 786440 | tf_op jit(solution)/shard_map/ppermute | solution.py:316
  81.5 0.7 copy-start.9
  82.3 18.4 %collective-permute-start.18 = (bf16[768,512]{1,0:T(8,128)(2,1)S(1)}, bf16[768,512]{1,0:T(8,128)(2,1)S(1)}, u32[]{:S(2)}, u32[]{:S(2)}) collective-permute-start(bf16[768,512]{1,0:T(8,128)(2,1)S(1)} %shard_map.91), channel_id=1, source_target_pairs={{0,8},{4,20},{8,0},{12,28},{16,24},{20,4},{24,16},{28,12},{1,9},{5... | collective-permute-start | bytes 2359304 | tf_op jit(solution)/shard_map/ppermute | solution.py:272
  83.8 16.1 %collective-permute-start.8 = (bf16[512,512]{1,0:T(8,128)(2,1)S(1)}, bf16[512,512]{1,0:T(8,128)(2,1)S(1)}, u32[]{:S(2)}, u32[]{:S(2)}) collective-permute-start(bf16[512,512]{1,0:T(8,128)(2,1)S(1)} %get-tuple-element.12), channel_id=1, source_target_pairs={{0,8},{4,20},{8,0},{12,28},{16,24},{20,4},{24,16},{28,12},{1,9},{5... | collective-permute-start | bytes 1572872 | tf_op jit(solution)/shard_map/ppermute | solution.py:272
  84.3 87.3 %collective-permute-start.11 = (bf16[3584,512]{1,0:T(8,128)(2,1)}, bf16[3584,512]{1,0:T(8,128)(2,1)}, u32[]{:S(2)}, u32[]{:S(2)}) collective-permute-start(bf16[3584,512]{1,0:T(8,128)(2,1)} %collective-permute-done.10.refs_2_), channel_id=1, source_target_pairs={{0,4},{4,0},{8,12},{12,8},{16,20},{20,16},{24,28},{28,24},{1,5},{5... | collective-permute-start | bytes 11010056 | tf_op jit(solution)/shard_map/ppermute | solution.py:267
  99.9 0.8 copy-start.2
  99.9 2.3 %collective-permute-start.15 = (bf16[512,512]{1,0:T(8,128)(2,1)}, bf16[512,512]{1,0:T(8,128)(2,1)}, u32[]{:S(2)}, u32[]{:S(2)}) collective-permute-start(bf16[512,512]{1,0:T(8,128)(2,1)} %collective-permute-done.14.refs_5_), channel_id=1, source_target_pairs={{0,4},{4,0},{8,12},{12,8},{16,20},{20,16},{24,28},{28,24},{1,5},{5... | collective-permute-start | bytes 1572872 | tf_op jit(solution)/shard_map/ppermute | solution.py:267
  99.9 34.3 %collective-permute-start.24 = (bf16[1792,512]{1,0:T(8,128)(2,1)S(1)}, bf16[1792,512]{1,0:T(8,128)(2,1)}, u32[]{:S(2)}, u32[]{:S(2)}) collective-permute-start(bf16[1792,512]{1,0:T(8,128)(2,1)S(1)} %collective-permute-done.22.refs_5_), channel_id=1, source_target_pairs={{0,16},{4,12},{8,24},{12,4},{16,0},{20,28},{24,8},{28,20},{1,17},{... | collective-permute-start | bytes 5505032 | tf_op jit(solution)/shard_map/ppermute | solution.py:272
  100.7 28.1 %collective-permute-start.16 = (bf16[512,512]{1,0:T(8,128)(2,1)}, bf16[512,512]{1,0:T(8,128)(2,1)S(1)}, u32[]{:S(2)}, u32[]{:S(2)}) collective-permute-start(bf16[512,512]{1,0:T(8,128)(2,1)} %collective-permute-done.14.refs_5_), channel_id=1, source_target_pairs={{0,16},{4,12},{8,24},{12,4},{16,0},{20,28},{24,8},{28,20},{1,17},{... | collective-permute-start | bytes 1572872 | tf_op jit(solution)/shard_map/ppermute | solution.py:272
  102.1 28.1 %collective-permute-start.9 = (bf16[512,512]{1,0:T(8,128)(2,1)}, bf16[512,512]{1,0:T(8,128)(2,1)}, u32[]{:S(2)}, u32[]{:S(2)}) collective-permute-start(bf16[512,512]{1,0:T(8,128)(2,1)} %copy-done.2), channel_id=1, source_target_pairs={{0,4},{4,0},{8,12},{12,8},{16,20},{20,16},{24,28},{28,24},{1,5},{5... | collective-permute-start | bytes 1572872 | tf_op jit(solution)/shard_map/ppermute | solution.py:267
  128.8 33.6 %collective-permute-start.23 = (bf16[1792,512]{1,0:T(8,128)(2,1)S(1)}, bf16[1792,512]{1,0:T(8,128)(2,1)}, u32[]{:S(2)}, u32[]{:S(2)}) collective-permute-start(bf16[1792,512]{1,0:T(8,128)(2,1)S(1)} %collective-permute-done.22.refs_5_), channel_id=1, source_target_pairs={{0,4},{4,0},{8,12},{12,8},{16,20},{20,16},{24,28},{28,24},{1,5},{5... | collective-permute-start | bytes 5505032 | tf_op jit(solution)/shard_map/ppermute | solution.py:267
  130.2 6.2 %copy-start.6 = (bf16[1024,128]{1,0:T(8,128)(2,1)S(1)}, bf16[1024,128]{1,0:T(8,128)(2,1)}, u32[]{:S(2)}) copy-start(bf16[1024,128]{1,0:T(8,128)(2,1)} %copy-done.5) | copy-start | bytes 786436
  130.2 6.2 %copy-start.8 = (bf16[1024,128]{1,0:T(8,128)(2,1)S(1)}, bf16[1024,128]{1,0:T(8,128)(2,1)}, u32[]{:S(2)}) copy-start(bf16[1024,128]{1,0:T(8,128)(2,1)} %copy-done.7) | copy-start | bytes 786436
  130.2 6.2 %copy-start.10 = (bf16[1024,128]{1,0:T(8,128)(2,1)S(1)}, bf16[1024,128]{1,0:T(8,128)(2,1)}, u32[]{:S(2)}) copy-start(bf16[1024,128]{1,0:T(8,128)(2,1)} %copy-done.9) | copy-start | bytes 786436
  130.3 3.5 %collective-permute-start.19 = (bf16[768,512]{1,0:T(8,128)(2,1)S(1)}, bf16[768,512]{1,0:T(8,128)(2,1)S(1)}, u32[]{:S(2)}, u32[]{:S(2)}) collective-permute-start(bf16[768,512]{1,0:T(8,128)(2,1)S(1)} %collective-permute-done.18.refs_5_), channel_id=1, source_target_pairs={{0,4},{4,0},{8,12},{12,8},{16,20},{20,16},{24,28},{28,24},{1,5},{5... | collective-permute-start | bytes 2359304 | tf_op jit(solution)/shard_map/ppermute | solution.py:267
  133.7 28.4 %collective-permute-start.20 = (bf16[768,512]{1,0:T(8,128)(2,1)S(1)}, bf16[768,512]{1,0:T(8,128)(2,1)S(1)}, u32[]{:S(2)}, u32[]{:S(2)}) collective-permute-start(bf16[768,512]{1,0:T(8,128)(2,1)S(1)} %collective-permute-done.18.refs_5_), channel_id=1, source_target_pairs={{0,16},{4,12},{8,24},{12,4},{16,0},{20,28},{24,8},{28,20},{1,17},{... | collective-permute-start | bytes 2359304 | tf_op jit(solution)/shard_map/ppermute | solution.py:272
  134.2 52.5 %collective-permute-start.25 = (bf16[1792,512]{1,0:T(8,128)(2,1)}, bf16[1792,512]{1,0:T(8,128)(2,1)S(1)}, u32[]{:S(2)}, u32[]{:S(2)}) collective-permute-start(bf16[1792,512]{1,0:T(8,128)(2,1)} %collective-permute-done.24.refs_2_), channel_id=1, source_target_pairs={{0,4},{4,0},{8,12},{12,8},{16,20},{20,16},{24,28},{28,24},{1,5},{5... | collective-permute-start | bytes 5505032 | tf_op jit(solution)/shard_map/ppermute | solution.py:267
  136.4 2.8 %copy-start = (bf16[48,16,4096]{2,1,0:T(8,128)(2,1)S(1)}, bf16[48,16,4096]{2,1,0:T(8,128)(2,1)}, u32[]{:S(2)}) copy-start(bf16[48,16,4096]{2,1,0:T(8,128)(2,1)} %param.7) | copy-start | bytes 18874372
  139.2 5.3 %copy-start.1 = (bf16[3584,128]{1,0:T(8,128)(2,1)S(1)}, bf16[3584,128]{1,0:T(8,128)(2,1)}, u32[]{:S(2)}) copy-start(bf16[3584,128]{1,0:T(8,128)(2,1)} %bank_ref.1) | copy-start | bytes 2752516
  139.2 11.3 %slice-start = ((s8[6291456]{0:T(1024)(128)(4,1)}), s8[4194304]{0:T(1024)(128)(4,1)S(1)}, s32[]{:S(2)}) async-start(s8[6291456]{0:T(1024)(128)(4,1)} %bitcast.15), calls=%async_computation | async-start | bytes 8388608
  144.4 5.4 %copy-start.3 = (bf16[512,512]{1,0:T(8,128)(2,1)S(1)}, bf16[512,512]{1,0:T(8,128)(2,1)}, u32[]{:S(2)}) copy-start(bf16[512,512]{1,0:T(8,128)(2,1)} %copy-done.2) | copy-start | bytes 1572868
  144.4 6.0 %slice-start.1 = ((s8[6291456]{0:T(1024)(128)(4,1)}), s8[2097152]{0:T(1024)(128)(4,1)S(1)}, s32[]{:S(2)}) async-start(s8[6291456]{0:T(1024)(128)(4,1)} %bitcast.15), calls=%async_computation.1 | async-start | bytes 4194304
  149.8 12.0 %collective-permute-start.12 = (bf16[512,512]{1,0:T(8,128)(2,1)S(1)}, bf16[512,512]{1,0:T(8,128)(2,1)S(1)}, u32[]{:S(2)}, u32[]{:S(2)}) collective-permute-start(bf16[512,512]{1,0:T(8,128)(2,1)S(1)} %copy-done.3), channel_id=1, source_target_pairs={{0,16},{4,12},{8,24},{12,4},{16,0},{20,28},{24,8},{28,20},{1,17},{... | collective-permute-start | bytes 1572872 | tf_op jit(solution)/shard_map/ppermute | solution.py:272
  161.8 35.1 %collective-permute-start.17 = (bf16[512,512]{1,0:T(8,128)(2,1)S(1)}, bf16[512,512]{1,0:T(8,128)(2,1)S(1)}, u32[]{:S(2)}, u32[]{:S(2)}) collective-permute-start(bf16[512,512]{1,0:T(8,128)(2,1)S(1)} %collective-permute-done.16.refs_2_), channel_id=1, source_target_pairs={{0,4},{4,0},{8,12},{12,8},{16,20},{20,16},{24,28},{28,24},{1,5},{5... | collective-permute-start | bytes 1572872 | tf_op jit(solution)/shard_map/ppermute | solution.py:267
  162.1 36.9 %collective-permute-start.13 = (bf16[512,512]{1,0:T(8,128)(2,1)S(1)}, bf16[512,512]{1,0:T(8,128)(2,1)S(1)}, u32[]{:S(2)}, u32[]{:S(2)}) collective-permute-start(bf16[512,512]{1,0:T(8,128)(2,1)S(1)} %collective-permute-done.12.refs_2_), channel_id=1, source_target_pairs={{0,4},{4,0},{8,12},{12,8},{16,20},{20,16},{24,28},{28,24},{1,5},{5... | collective-permute-start | bytes 1572872 | tf_op jit(solution)/shard_map/ppermute | solution.py:267
  162.4 31.8 %collective-permute-start.21 = (bf16[768,512]{1,0:T(8,128)(2,1)S(1)}, bf16[768,512]{1,0:T(8,128)(2,1)S(1)}, u32[]{:S(2)}, u32[]{:S(2)}) collective-permute-start(bf16[768,512]{1,0:T(8,128)(2,1)S(1)} %collective-permute-done.20.refs_2_), channel_id=1, source_target_pairs={{0,4},{4,0},{8,12},{12,8},{16,20},{20,16},{24,28},{28,24},{1,5},{5... | collective-permute-start | bytes 2359304 | tf_op jit(solution)/shard_map/ppermute | solution.py:267

commit v4 on v3

--- a/solution.py
+++ b/solution.py
@@ -336,7 +336,10 @@
             partial.append(product(flat_tokens, start, length, tile, rows, side, partial=part))
         for c, (start, length) in enumerate(chunks):
             far = [(m, held[c, m], 0) for m in (6, 7)]
-            hidden = product(flat_tokens, start, length, tile, rows, far, partial=partial[c], final=True, hidden=hidden, resident=c > 1)
+            if c + 1 == len(chunks):
+                partial[c] = product(flat_tokens, start, length, tile, rows, far[:1], partial=partial[c], resident=True)
+                far = far[1:]
+            hidden = product(flat_tokens, start, length, length if c > 1 and start % length == 0 else tile, rows, far, partial=partial[c], final=True, hidden=hidden, resident=c > 1)
     else:
         blocks = {0: weight}
         for bit in range((pops - 1).bit_length()):

time: 202 us -> 202 us (level)
    pallas_call x12 -> x13, Pallas kernels: 49.6 us -> 49.9 us  [product(): pl.pallas_call(kernel, grid=(length // tile,), in_specs=specs, out_specs=...]
  transfers between devices with their start and end apart: 26 -> 26, of which waited for: 9 -> 9; matrix products, arithmetic and copies ran while one was open for 2% -> 2% of each run, Pallas kernels for 30% -> 31%
where the time goes in v4:
time: 202 us; the launch traced here: 201 us
  waiting for transfers between devices  105 us (52%)
  Pallas kernels  63.4 us (31%)
  starting transfers between devices  24.9 us (12%)
  local copies, waits for them, and re-layouts  4.67 us (2%)
    ppermute x10, waiting for transfers between devices, send(): lax.ppermute(block, 'pop', [(i, i ^ (axis ^ (one | two) if i & core else...  76.3 us
    pallas_call x13, Pallas kernels, product(): pl.pallas_call(kernel, grid=(length // tile,), in_specs=specs, out_specs=...  49.9 us
    ppermute x3, waiting for transfers between devices, shards(): lax.ppermute(bank_in, 'row', [(i, (i - step) % lanes) for i in range(lane...  19 us
    ppermute x10, starting transfers between devices, send(): lax.ppermute(block, 'pop', [(i, i ^ (axis ^ (one | two) if i & core else...  11.8 us
    ppermute x3, starting transfers between devices, shards(): lax.ppermute(bank_in, 'row', [(i, (i - step) % lanes) for i in range(lane...  6.88 us
    ppermute x12, waiting for transfers between devices, flip(): return lax.ppermute(block, 'pop', [(i, i ^ mask) for i in range(pops)])  6.37 us
    pallas_call x1, Pallas kernels, updated(): pl.pallas_call(update_kernel, grid=(rows // tile,), in_specs=[pl.BlockSpe...  5.33 us
  transfers between devices with their start and end apart: 26, of which 9 were waited for; matrix products, arithmetic and copies ran while one was open for 2% of the time, Pallas kernels for 31%

profile of v4, /device:TPU:0, one launch (start us, length us, event | category | flops | bytes accessed | tf_op | source)
XLA Modules:
  0.0 201.3 jit_solution(17534398760237666314)
XLA Ops:
  0.7 3.1 %collective-permute-start.10 = (bf16[3584,512]{1,0:T(8,128)(2,1)}, bf16[3584,512]{1,0:T(8,128)(2,1)}, u32[]{:S(2)}, u32[]{:S(2)}) collective-permute-start(bf16[3584,512]{1,0:T(8,128)(2,1)} %weight_ref.1), channel_id=1, source_target_pairs={{0,16},{4,12},{8,24},{12,4},{16,0},{20,28},{24,8},{28,20},{1,17},{... | collective-permute-start | bytes 11010056 | tf_op jit(solution)/shard_map/ppermute | solution.py:272
  3.7 1.8 shard_map.86
  5.6 1.6 collective-permute-start.22
  7.1 0.6 collective-permute-start.3
  7.7 3.6 %collective-permute-start = (bf16[1024,128]{1,0:T(8,128)(2,1)S(1)}, bf16[1024,128]{1,0:T(8,128)(2,1)S(1)}, u32[]{:S(2)}, u32[]{:S(2)}) collective-permute-start(bf16[1024,128]{1,0:T(8,128)(2,1)S(1)} %copy-done.4), channel_id=1, source_target_pairs={{0,3},{1,0},{2,1},{3,2},{4,7},{5,4},{6,5},{7,6},{8,11},{9,8},{10,9... | collective-permute-start | bytes 786440 | tf_op jit(solution)/shard_map/ppermute | solution.py:316
  11.3 2.6 %collective-permute-done.3 = s32[48,17]{0,1:T(8,128)S(1)} collective-permute-done((s32[48,17]{0,1:T(8,128)S(1)}, s32[48,17]{0,1:T(8,128)S(1)}, u32[]{:S(2)}, u32[]{:S(2)}) %collective-permute-start.3) | collective-permute-done | bytes 3296 | tf_op jit(solution)/shard_map/ppermute | solution.py:267
  13.9 0.1 pad_add_fusion.2
  13.9 0.5 collective-permute-start.4
  14.5 34.3 %collective-permute-done.4 = s32[96,17]{0,1:T(8,128)S(1)} collective-permute-done((s32[96,17]{0,1:T(8,128)S(1)}, s32[96,17]{0,1:T(8,128)S(1)}, u32[]{:S(2)}, u32[]{:S(2)}) %collective-permute-start.4) | collective-permute-done | bytes 6560 | tf_op jit(solution)/shard_map/ppermute | solution.py:272
  48.8 3.3 %collective-permute-start.5 = (s32[96,17]{0,1:T(8,128)S(1)}, s32[96,17]{0,1:T(8,128)S(1)}, u32[]{:S(2)}, u32[]{:S(2)}) collective-permute-start(s32[96,17]{0,1:T(8,128)S(1)} %pad_add_fusion.2), channel_id=1, source_target_pairs={{0,24},{8,16},{16,8},{24,0},{1,25},{9,17},{17,9},{25,1},{2,26},{10... | collective-permute-start | bytes 19592 | tf_op jit(solution)/shard_map/ppermute | solution.py:291
  52.1 3.3 %collective-permute-done.5 = s32[96,17]{0,1:T(8,128)S(1)} collective-permute-done((s32[96,17]{0,1:T(8,128)S(1)}, s32[96,17]{0,1:T(8,128)S(1)}, u32[]{:S(2)}, u32[]{:S(2)}) %collective-permute-start.5) | collective-permute-done | bytes 6560 | tf_op jit(solution)/shard_map/ppermute | solution.py:291
  55.4 0.1 pad_add_fusion
  55.5 0.0 collective-permute-start.6
  55.5 1.2 collective-permute-done.6
  56.7 2.6 %collective-permute-start.1 = (bf16[1024,128]{1,0:T(8,128)(2,1)S(1)}, bf16[1024,128]{1,0:T(8,128)(2,1)S(1)}, u32[]{:S(2)}, u32[]{:S(2)}) collective-permute-start(bf16[1024,128]{1,0:T(8,128)(2,1)S(1)} %copy-done.4), channel_id=1, source_target_pairs={{0,2},{1,3},{2,0},{3,1},{4,6},{5,7},{6,4},{7,5},{8,10},{9,11},{10,... | collective-permute-start | bytes 786440 | tf_op jit(solution)/shard_map/ppermute | solution.py:316
  59.3 1.5 collective-permute-start.14
  60.7 10.8 %collective-permute-done.1.refs_2_ = bf16[1024,128]{1,0:T(8,128)(2,1)S(1)} collective-permute-done((bf16[1024,128]{1,0:T(8,128)(2,1)S(1)}, bf16[1024,128]{1,0:T(8,128)(2,1)S(1)}, u32[]{:S(2)}, u32[]{:S(2)}) %collective-permute-start.1) | collective-permute-done | bytes 262176 | tf_op jit(solution)/shard_map/ppermute | solution.py:316
  71.5 0.7 collective-permute-start.2
  72.2 1.1 shard_map.92
  73.4 8.1 %collective-permute-done.2.refs_3_ = bf16[1024,128]{1,0:T(8,128)(2,1)S(1)} collective-permute-done((bf16[1024,128]{1,0:T(8,128)(2,1)S(1)}, bf16[1024,128]{1,0:T(8,128)(2,1)S(1)}, u32[]{:S(2)}, u32[]{:S(2)}) %collective-permute-start.2) | collective-permute-done | bytes 262176 | tf_op jit(solution)/shard_map/ppermute | solution.py:316
  81.6 0.7 copy-done.9
  82.3 1.5 collective-permute-start.18
  83.8 0.5 collective-permute-start.8
  84.3 15.6 %collective-permute-done.8.refs_5_ = bf16[512,512]{1,0:T(8,128)(2,1)S(1)} collective-permute-done((bf16[512,512]{1,0:T(8,128)(2,1)S(1)}, bf16[512,512]{1,0:T(8,128)(2,1)S(1)}, u32[]{:S(2)}, u32[]{:S(2)}) %collective-permute-start.8) | collective-permute-done | bytes 524320 | tf_op jit(solution)/shard_map/ppermute | solution.py:272
  99.9 0.6 collective-permute-start.24
  100.5 0.2 copy-done.2
  100.7 1.3 collective-permute-start.16
  102.0 0.1 copy.18.seeds_ref
  102.1 0.0 collective-permute-done.15.refs_6_
  102.1 0.1 collective-permute-start.9
  102.3 0.1 pad_add_fusion.3.pick_ref
  102.4 26.4 %collective-permute-done.16.refs_2_ = bf16[512,512]{1,0:T(8,128)(2,1)S(1)} collective-permute-done((bf16[512,512]{1,0:T(8,128)(2,1)}, bf16[512,512]{1,0:T(8,128)(2,1)S(1)}, u32[]{:S(2)}, u32[]{:S(2)}) %collective-permute-start.16) | collective-permute-done | bytes 524320 | tf_op jit(solution)/shard_map/ppermute | solution.py:272
  128.8 0.6 slice_add_fusion
  129.4 0.8 concatenate.20
  130.3 0.6 collective-permute-start.19
  130.8 0.3 convert_reduce_fusion
  131.1 2.6 %collective-permute-done.19.refs_6_ = bf16[768,512]{1,0:T(8,128)(2,1)S(1)} collective-permute-done((bf16[768,512]{1,0:T(8,128)(2,1)S(1)}, bf16[768,512]{1,0:T(8,128)(2,1)S(1)}, u32[]{:S(2)}, u32[]{:S(2)}) %collective-permute-start.19) | collective-permute-done | bytes 786464 | tf_op jit(solution)/shard_map/ppermute | solution.py:267
  133.7 0.5 collective-permute-start.20
  134.2 0.8 collective-permute-start.25
  135.1 1.3 fusion.2.coupling_ref
  136.4 0.0 copy-start
  136.4 2.8 %copy-done = bf16[48,16,4096]{2,1,0:T(8,128)(2,1)S(1)} copy-done((bf16[48,16,4096]{2,1,0:T(8,128)(2,1)S(1)}, bf16[48,16,4096]{2,1,0:T(8,128)(2,1)}, u32[]{:S(2)}) %copy-start) | copy-done | bytes 6291480
  139.2 2.9 %project.1 = (f32[768,128]{1,0:T(8,128)S(1)}, bf16[512,128]{1,0:T(8,128)(2,1)S(1)}) custom-call(s32[6]{0:T(128)S(1)} %pad_add_fusion.3.pick_ref, bf16[768,4096]{1,0:T(8,128)(2,1)S(1)} %bitcast.14, bf16[1024,128]{1,0:T(8,128)(2,1)S(1)} %copy-done.4, bf16[1024,128]{1,0:T(8,128)(2,1)S(1)} %copy-done.6, bf16[1024,128]{1,0:T(8,128)(2,1)S(1)} %copy-done.8, ...), custom_call_target="tpu_custom_call" | custom-call | flops 805306368 | bytes 6291456 | tf_op jit(solution)/shard_map/project/pallas_call | solution.py:204
  142.1 2.3 %lowrank.1 = (bf16[768,256]{1,0:T(8,128)(2,1)S(1)}, bf16[256,512]{1,0:T(8,128)(2,1)S(1)}) custom-call(f32[768,128]{1,0:T(8,128)S(1)} %get-tuple-element.9.projected_ref, f32[128,128]{1,0:T(8,128)S(1)} %fusion.2.coupling_ref, s32[48,2,8]{2,1,0:T(2,128)S(1)} %copy.18.seeds_ref, bf16[512,128]{1,0:T(8,128)(2,1)S(1)} %get-tuple-element.10.columns_ref), custom_call_target="tpu_custom_call" | custom-call | flops 251658240 | bytes 786432 | tf_op jit(solution)/shard_map/lowrank/pallas_call | solution.py:244
  144.4 0.0 copy-start.3
  144.4 0.0 slice-start.1
  144.4 5.3 %update.1 = bf16[3584,512]{1,0:T(8,128)(2,1)} custom-call(bf16[3584,512]{1,0:T(8,128)(2,1)} %weight_ref.1, bf16[3584,128]{1,0:T(8,128)(2,1)S(1)} %copy-done.1, bf16[256,512]{1,0:T(8,128)(2,1)S(1)} %get-tuple-element.15.right_ref), custom_call_target="tpu_custom_call" | custom-call | flops 939524096 | bytes 7340032 | tf_op jit(solution)/shard_map/update/pallas_call | solution.py:167
  149.8 0.7 collective-permute-start.12
  150.5 3.5 %shard_map.90.refs_1_ = f32[768,512]{1,0:T(8,128)S(1)} custom-call(bf16[768,4096]{1,0:T(8,128)(2,1)S(1)} %bitcast.17, bf16[768,256]{1,0:T(8,128)(2,1)S(1)} %get-tuple-element.11.refs_1_, bf16[3584,128]{1,0:T(8,128)(2,1)S(1)} %copy-done.1, bf16[3584,512]{1,0:T(8,128)(2,1)} %weight_ref.1, bf16[3584,512]{1,0:T(8,128)(2,1)} %collective-permute-done.7.refs_4_, ...), custom_call_target="tpu_custom_call" | custom-call | flops 1610612736 | bytes 6029312 | tf_op jit(solution)/shard_map/pallas_call | solution.py:115
  154.0 3.4 %shard_map.87.refs_1_ = f32[768,512]{1,0:T(8,128)S(1)} custom-call(bf16[768,4096]{1,0:T(8,128)(2,1)S(1)} %bitcast.18, bf16[768,256]{1,0:T(8,128)(2,1)S(1)} %get-tuple-element.11.refs_1_, bf16[3584,128]{1,0:T(8,128)(2,1)S(1)} %copy-done.1, bf16[3584,512]{1,0:T(8,128)(2,1)} %weight_ref.1, bf16[3584,512]{1,0:T(8,128)(2,1)} %collective-permute-done.7.refs_4_, ...), custom_call_target="tpu_custom_call" | custom-call | flops 1610612736 | bytes 6029312 | tf_op jit(solution)/shard_map/pallas_call | solution.py:115
  157.4 4.4 %shard_map.93.refs_1_ = f32[768,768]{1,0:T(8,128)S(1)} custom-call(bf16[768,4096]{1,0:T(8,128)(2,1)S(1)} %bitcast.19, bf16[768,256]{1,0:T(8,128)(2,1)S(1)} %get-tuple-element.11.refs_1_, bf16[3584,128]{1,0:T(8,128)(2,1)S(1)} %copy-done.1, bf16[3584,512]{1,0:T(8,128)(2,1)} %weight_ref.1, bf16[3584,512]{1,0:T(8,128)(2,1)} %collective-permute-done.7.refs_4_, ...), custom_call_target="tpu_custom_call" | custom-call | flops 2415919104 | bytes 7471104 | tf_op jit(solution)/shard_map/pallas_call | solution.py:115
  161.8 0.3 collective-permute-start.17
  162.1 0.3 collective-permute-start.13
  162.4 0.2 collective-permute-start.21
  162.6 9.0 %shard_map.95.refs_1_ = f32[768,1792]{1,0:T(8,128)S(1)} custom-call(bf16[768,4096]{1,0:T(8,128)(2,1)S(1)} %bitcast.20, bf16[768,256]{1,0:T(8,128)(2,1)S(1)} %get-tuple-element.11.refs_1_, bf16[3584,128]{1,0:T(8,128)(2,1)S(1)} %copy-done.1, bf16[3584,512]{1,0:T(8,128)(2,1)} %weight_ref.1, bf16[3584,512]{1,0:T(8,128)(2,1)} %collective-permute-done.7.refs_4_, ...), custom_call_target="tpu_custom_call" | custom-call | flops 5637144576 | bytes 13238272 | tf_op jit(solution)/shard_map/pallas_call | solution.py:115
  171.6 3.4 %shard_map.94.refs_1_ = f32[768,768]{1,0:T(8,128)S(1)} custom-call(bf16[768,4096]{1,0:T(8,128)(2,1)S(1)} %bitcast.21, f32[768,768]{1,0:T(8,128)S(1)} %shard_map.93.refs_1_, bf16[3584,512]{1,0:T(8,128)(2,1)} %collective-permute-done.10.refs_2_, bf16[3584,512]{1,0:T(8,128)(2,1)} %collective-permute-done.11.refs_3_), custom_call_target="tpu_custom_call", output_to_operand_aliasing={{}: (1, {})} | custom-call | flops 1207959552 | bytes 4325376 | tf_op jit(solution)/shard_map/pallas_call | solution.py:115
  175.1 6.9 %shard_map.96.refs_1_ = f32[768,1792]{1,0:T(8,128)S(1)} custom-call(bf16[768,4096]{1,0:T(8,128)(2,1)S(1)} %bitcast.22, f32[768,1792]{1,0:T(8,128)S(1)} %shard_map.95.refs_1_, bf16[3584,512]{1,0:T(8,128)(2,1)} %collective-permute-done.10.refs_2_, bf16[3584,512]{1,0:T(8,128)(2,1)} %collective-permute-done.11.refs_3_), custom_call_target="tpu_custom_call", output_to_operand_aliasing={{}: (1, {})} | custom-call | flops 2818572288 | bytes 7995392 | tf_op jit(solution)/shard_map/pallas_call | solution.py:115
  181.9 2.4 %shard_map.88.refs_1_ = f32[768,512]{1,0:T(8,128)S(1)} custom-call(bf16[768,4096]{1,0:T(8,128)(2,1)S(1)} %bitcast.23, f32[768,512]{1,0:T(8,128)S(1)} %shard_map.87.refs_1_, bf16[3584,512]{1,0:T(8,128)(2,1)} %collective-permute-done.10.refs_2_, bf16[3584,512]{1,0:T(8,128)(2,1)} %collective-permute-done.11.refs_3_), custom_call_target="tpu_custom_call", output_to_operand_aliasing={{}: (1, {})} | custom-call | flops 805306368 | bytes 3407872 | tf_op jit(solution)/shard_map/pallas_call | solution.py:115
  184.4 0.9 shard_map.89.refs_1_
  185.3 2.4 %shard_map.91.refs_1_ = f32[768,512]{1,0:T(8,128)S(1)} custom-call(bf16[768,4096]{1,0:T(8,128)(2,1)S(1)} %bitcast.25, f32[768,512]{1,0:T(8,128)S(1)} %shard_map.90.refs_1_, bf16[3584,512]{1,0:T(8,128)(2,1)} %collective-permute-done.10.refs_2_, bf16[3584,512]{1,0:T(8,128)(2,1)} %collective-permute-done.11.refs_3_), custom_call_target="tpu_custom_call", output_to_operand_aliasing={{}: (1, {})} | custom-call | flops 805306368 | bytes 3407872 | tf_op jit(solution)/shard_map/pallas_call | solution.py:115
  187.7 7.5 %shard_map.97.refs_4_ = bf16[768,3584]{1,0:T(8,128)(2,1)} custom-call(bf16[768,4096]{1,0:T(8,128)(2,1)S(1)} %bitcast.26, f32[768,1792]{1,0:T(8,128)S(1)} %shard_map.96.refs_1_, bf16[1792,512]{1,0:T(8,128)(2,1)} %collective-permute-done.24.refs_2_, bf16[1792,512]{1,0:T(8,128)(2,1)S(1)} %collective-permute-done.25.refs_3_), custom_call_target="tpu_custom_call" | custom-call | flops 2818572288 | bytes 7995392 | tf_op jit(solution)/shard_map/pallas_call | solution.py:115
  195.2 2.7 %shard_map.98.refs_4_ = bf16[768,3584]{1,0:T(8,128)(2,1)} custom-call(bf16[768,4096]{1,0:T(8,128)(2,1)S(1)} %bitcast.27, f32[768,768]{1,0:T(8,128)S(1)} %shard_map.94.refs_1_, bf16[768,512]{1,0:T(8,128)(2,1)S(1)} %collective-permute-done.20.refs_2_, bf16[768,512]{1,0:T(8,128)(2,1)S(1)} %collective-permute-done.21.refs_3_, ...), custom_call_target="tpu_custom_call", output_to_operand_aliasing={{}: (4, {})} | custom-call | flops 1207959552 | bytes 4325376 | tf_op jit(solution)/shard_map/pallas_call | solution.py:115
  197.9 1.9 shard_map.99.refs_3_
  199.8 1.5 shard_map.100
  (53 shorter events, 0.2 us)
Async XLA Ops:
  0.6 6.5 %copy-start.13 = (s32[48]{0:T(128)S(1)}, s32[48]{0:T(128)}, u32[]{:S(2)}) copy-start(s32[48]{0:T(128)} %param.11) | copy-start | bytes 580
  0.6 6.5 %copy-start.11 = (s32[48,2,8]{0,2,1:T(8,128)S(1)}, s32[48,2,8]{0,2,1:T(8,128)}, u32[]{:S(2)}) copy-start(s32[48,2,8]{0,2,1:T(8,128)} %param.12) | copy-start | bytes 9220
  0.7 7.1 %copy-start.4 = (bf16[1024,128]{1,0:T(8,128)(2,1)S(1)}, bf16[1024,128]{1,0:T(8,128)(2,1)}, u32[]{:S(2)}) copy-start(bf16[1024,128]{1,0:T(8,128)(2,1)} %refs_0_.1) | copy-start | bytes 786436
  0.7 83.6 %collective-permute-start.10 = (bf16[3584,512]{1,0:T(8,128)(2,1)}, bf16[3584,512]{1,0:T(8,128)(2,1)}, u32[]{:S(2)}, u32[]{:S(2)}) collective-permute-start(bf16[3584,512]{1,0:T(8,128)(2,1)} %weight_ref.1), channel_id=1, source_target_pairs={{0,16},{4,12},{8,24},{12,4},{16,0},{20,28},{24,8},{28,20},{1,17},{... | collective-permute-start | bytes 11010056 | tf_op jit(solution)/shard_map/ppermute | solution.py:272
  5.6 94.3 %collective-permute-start.22 = (bf16[1792,512]{1,0:T(8,128)(2,1)S(1)}, bf16[1792,512]{1,0:T(8,128)(2,1)S(1)}, u32[]{:S(2)}, u32[]{:S(2)}) collective-permute-start(bf16[1792,512]{1,0:T(8,128)(2,1)S(1)} %get-tuple-element.14), channel_id=1, source_target_pairs={{0,8},{4,20},{8,0},{12,28},{16,24},{20,4},{24,16},{28,12},{1,9},{5... | collective-permute-start | bytes 5505032 | tf_op jit(solution)/shard_map/ppermute | solution.py:272
  7.1 142.7 %collective-permute-start.7 = (bf16[3584,512]{1,0:T(8,128)(2,1)}, bf16[3584,512]{1,0:T(8,128)(2,1)}, u32[]{:S(2)}, u32[]{:S(2)}) collective-permute-start(bf16[3584,512]{1,0:T(8,128)(2,1)} %weight_ref.1), channel_id=1, source_target_pairs={{0,4},{4,0},{8,12},{12,8},{16,20},{20,16},{24,28},{28,24},{1,5},{5... | collective-permute-start | bytes 11010056 | tf_op jit(solution)/shard_map/ppermute | solution.py:267
  7.1 6.7 %collective-permute-start.3 = (s32[48,17]{0,1:T(8,128)S(1)}, s32[48,17]{0,1:T(8,128)S(1)}, u32[]{:S(2)}, u32[]{:S(2)}) collective-permute-start(s32[48,17]{0,1:T(8,128)S(1)} %pad_add_fusion.1), channel_id=1, source_target_pairs={{0,4},{4,0},{8,12},{12,8},{16,20},{20,16},{24,28},{28,24},{1,5},{5... | collective-permute-start | bytes 9800 | tf_op jit(solution)/shard_map/ppermute | solution.py:267
  7.7 51.5 %collective-permute-start = (bf16[1024,128]{1,0:T(8,128)(2,1)S(1)}, bf16[1024,128]{1,0:T(8,128)(2,1)S(1)}, u32[]{:S(2)}, u32[]{:S(2)}) collective-permute-start(bf16[1024,128]{1,0:T(8,128)(2,1)S(1)} %copy-done.4), channel_id=1, source_target_pairs={{0,3},{1,0},{2,1},{3,2},{4,7},{5,4},{6,5},{7,6},{8,11},{9,8},{10,9... | collective-permute-start | bytes 786440 | tf_op jit(solution)/shard_map/ppermute | solution.py:316
  13.9 34.8 %collective-permute-start.4 = (s32[96,17]{0,1:T(8,128)S(1)}, s32[96,17]{0,1:T(8,128)S(1)}, u32[]{:S(2)}, u32[]{:S(2)}) collective-permute-start(s32[96,17]{0,1:T(8,128)S(1)} %pad_add_fusion.2), channel_id=1, source_target_pairs={{0,8},{4,20},{8,0},{12,28},{16,24},{20,4},{24,16},{28,12},{1,9},{5... | collective-permute-start | bytes 19592 | tf_op jit(solution)/shard_map/ppermute | solution.py:272
  48.8 6.6 %collective-permute-start.5 = (s32[96,17]{0,1:T(8,128)S(1)}, s32[96,17]{0,1:T(8,128)S(1)}, u32[]{:S(2)}, u32[]{:S(2)}) collective-permute-start(s32[96,17]{0,1:T(8,128)S(1)} %pad_add_fusion.2), channel_id=1, source_target_pairs={{0,24},{8,16},{16,8},{24,0},{1,25},{9,17},{17,9},{25,1},{2,26},{10... | collective-permute-start | bytes 19592 | tf_op jit(solution)/shard_map/ppermute | solution.py:291
  55.5 1.2 collective-permute-start.6
  56.7 14.9 %collective-permute-start.1 = (bf16[1024,128]{1,0:T(8,128)(2,1)S(1)}, bf16[1024,128]{1,0:T(8,128)(2,1)S(1)}, u32[]{:S(2)}, u32[]{:S(2)}) collective-permute-start(bf16[1024,128]{1,0:T(8,128)(2,1)S(1)} %copy-done.4), channel_id=1, source_target_pairs={{0,2},{1,3},{2,0},{3,1},{4,6},{5,7},{6,4},{7,5},{8,10},{9,11},{10,... | collective-permute-start | bytes 786440 | tf_op jit(solution)/shard_map/ppermute | solution.py:316
  59.3 14.1 %copy-start.5 = (bf16[1024,128]{1,0:T(8,128)(2,1)}, bf16[1024,128]{1,0:T(8,128)(2,1)S(1)}, u32[]{:S(2)}) copy-start(bf16[1024,128]{1,0:T(8,128)(2,1)S(1)} %collective-permute-done.refs_1_) | copy-start | bytes 786436
  59.3 42.7 %copy-start.12 = (s32[48,2,8]{0,2,1:T(8,128)S(1)}, s32[48,2,8]{0,2,1:T(8,128)}, u32[]{:S(2)}) copy-start(s32[48,2,8]{0,2,1:T(8,128)} %param.13) | copy-start | bytes 9220
  59.3 24.5 %collective-permute-start.14 = (bf16[512,512]{1,0:T(8,128)(2,1)S(1)}, bf16[512,512]{1,0:T(8,128)(2,1)}, u32[]{:S(2)}, u32[]{:S(2)}) collective-permute-start(bf16[512,512]{1,0:T(8,128)(2,1)S(1)} %get-tuple-element.13), channel_id=1, source_target_pairs={{0,8},{4,20},{8,0},{12,28},{16,24},{20,4},{24,16},{28,12},{1,9},{5... | collective-permute-start | bytes 1572872 | tf_op jit(solution)/shard_map/ppermute | solution.py:272
  71.5 1.8 copy-start.7
  71.5 10.0 %collective-permute-start.2 = (bf16[1024,128]{1,0:T(8,128)(2,1)S(1)}, bf16[1024,128]{1,0:T(8,128)(2,1)S(1)}, u32[]{:S(2)}, u32[]{:S(2)}) collective-permute-start(bf16[1024,128]{1,0:T(8,128)(2,1)S(1)} %copy-done.4), channel_id=1, source_target_pairs={{0,1},{1,2},{2,3},{3,0},{4,5},{5,6},{6,7},{7,4},{8,9},{9,10},{10,1... | collective-permute-start | bytes 786440 | tf_op jit(solution)/shard_map/ppermute | solution.py:316
  81.5 0.7 copy-start.9
  82.3 18.4 %collective-permute-start.18 = (bf16[768,512]{1,0:T(8,128)(2,1)S(1)}, bf16[768,512]{1,0:T(8,128)(2,1)S(1)}, u32[]{:S(2)}, u32[]{:S(2)}) collective-permute-start(bf16[768,512]{1,0:T(8,128)(2,1)S(1)} %shard_map.92), channel_id=1, source_target_pairs={{0,8},{4,20},{8,0},{12,28},{16,24},{20,4},{24,16},{28,12},{1,9},{5... | collective-permute-start | bytes 2359304 | tf_op jit(solution)/shard_map/ppermute | solution.py:272
  83.8 16.1 %collective-permute-start.8 = (bf16[512,512]{1,0:T(8,128)(2,1)S(1)}, bf16[512,512]{1,0:T(8,128)(2,1)S(1)}, u32[]{:S(2)}, u32[]{:S(2)}) collective-permute-start(bf16[512,512]{1,0:T(8,128)(2,1)S(1)} %get-tuple-element.12), channel_id=1, source_target_pairs={{0,8},{4,20},{8,0},{12,28},{16,24},{20,4},{24,16},{28,12},{1,9},{5... | collective-permute-start | bytes 1572872 | tf_op jit(solution)/shard_map/ppermute | solution.py:272
  84.3 87.3 %collective-permute-start.11 = (bf16[3584,512]{1,0:T(8,128)(2,1)}, bf16[3584,512]{1,0:T(8,128)(2,1)}, u32[]{:S(2)}, u32[]{:S(2)}) collective-permute-start(bf16[3584,512]{1,0:T(8,128)(2,1)} %collective-permute-done.10.refs_2_), channel_id=1, source_target_pairs={{0,4},{4,0},{8,12},{12,8},{16,20},{20,16},{24,28},{28,24},{1,5},{5... | collective-permute-start | bytes 11010056 | tf_op jit(solution)/shard_map/ppermute | solution.py:267
  99.9 0.8 copy-start.2
  99.9 2.3 %collective-permute-start.15 = (bf16[512,512]{1,0:T(8,128)(2,1)}, bf16[512,512]{1,0:T(8,128)(2,1)}, u32[]{:S(2)}, u32[]{:S(2)}) collective-permute-start(bf16[512,512]{1,0:T(8,128)(2,1)} %collective-permute-done.14.refs_5_), channel_id=1, source_target_pairs={{0,4},{4,0},{8,12},{12,8},{16,20},{20,16},{24,28},{28,24},{1,5},{5... | collective-permute-start | bytes 1572872 | tf_op jit(solution)/shard_map/ppermute | solution.py:267
  99.9 34.3 %collective-permute-start.24 = (bf16[1792,512]{1,0:T(8,128)(2,1)S(1)}, bf16[1792,512]{1,0:T(8,128)(2,1)}, u32[]{:S(2)}, u32[]{:S(2)}) collective-permute-start(bf16[1792,512]{1,0:T(8,128)(2,1)S(1)} %collective-permute-done.22.refs_5_), channel_id=1, source_target_pairs={{0,16},{4,12},{8,24},{12,4},{16,0},{20,28},{24,8},{28,20},{1,17},{... | collective-permute-start | bytes 5505032 | tf_op jit(solution)/shard_map/ppermute | solution.py:272
  100.7 28.1 %collective-permute-start.16 = (bf16[512,512]{1,0:T(8,128)(2,1)}, bf16[512,512]{1,0:T(8,128)(2,1)S(1)}, u32[]{:S(2)}, u32[]{:S(2)}) collective-permute-start(bf16[512,512]{1,0:T(8,128)(2,1)} %collective-permute-done.14.refs_5_), channel_id=1, source_target_pairs={{0,16},{4,12},{8,24},{12,4},{16,0},{20,28},{24,8},{28,20},{1,17},{... | collective-permute-start | bytes 1572872 | tf_op jit(solution)/shard_map/ppermute | solution.py:272
  102.1 28.1 %collective-permute-start.9 = (bf16[512,512]{1,0:T(8,128)(2,1)}, bf16[512,512]{1,0:T(8,128)(2,1)}, u32[]{:S(2)}, u32[]{:S(2)}) collective-permute-start(bf16[512,512]{1,0:T(8,128)(2,1)} %copy-done.2), channel_id=1, source_target_pairs={{0,4},{4,0},{8,12},{12,8},{16,20},{20,16},{24,28},{28,24},{1,5},{5... | collective-permute-start | bytes 1572872 | tf_op jit(solution)/shard_map/ppermute | solution.py:267
  128.8 33.6 %collective-permute-start.23 = (bf16[1792,512]{1,0:T(8,128)(2,1)S(1)}, bf16[1792,512]{1,0:T(8,128)(2,1)}, u32[]{:S(2)}, u32[]{:S(2)}) collective-permute-start(bf16[1792,512]{1,0:T(8,128)(2,1)S(1)} %collective-permute-done.22.refs_5_), channel_id=1, source_target_pairs={{0,4},{4,0},{8,12},{12,8},{16,20},{20,16},{24,28},{28,24},{1,5},{5... | collective-permute-start | bytes 5505032 | tf_op jit(solution)/shard_map/ppermute | solution.py:267
  130.2 6.2 %copy-start.6 = (bf16[1024,128]{1,0:T(8,128)(2,1)S(1)}, bf16[1024,128]{1,0:T(8,128)(2,1)}, u32[]{:S(2)}) copy-start(bf16[1024,128]{1,0:T(8,128)(2,1)} %copy-done.5) | copy-start | bytes 786436
  130.2 6.2 %copy-start.8 = (bf16[1024,128]{1,0:T(8,128)(2,1)S(1)}, bf16[1024,128]{1,0:T(8,128)(2,1)}, u32[]{:S(2)}) copy-start(bf16[1024,128]{1,0:T(8,128)(2,1)} %copy-done.7) | copy-start | bytes 786436
  130.2 6.2 %copy-start.10 = (bf16[1024,128]{1,0:T(8,128)(2,1)S(1)}, bf16[1024,128]{1,0:T(8,128)(2,1)}, u32[]{:S(2)}) copy-start(bf16[1024,128]{1,0:T(8,128)(2,1)} %copy-done.9) | copy-start | bytes 786436
  130.3 3.5 %collective-permute-start.19 = (bf16[768,512]{1,0:T(8,128)(2,1)S(1)}, bf16[768,512]{1,0:T(8,128)(2,1)S(1)}, u32[]{:S(2)}, u32[]{:S(2)}) collective-permute-start(bf16[768,512]{1,0:T(8,128)(2,1)S(1)} %collective-permute-done.18.refs_5_), channel_id=1, source_target_pairs={{0,4},{4,0},{8,12},{12,8},{16,20},{20,16},{24,28},{28,24},{1,5},{5... | collective-permute-start | bytes 2359304 | tf_op jit(solution)/shard_map/ppermute | solution.py:267
  133.7 28.4 %collective-permute-start.20 = (bf16[768,512]{1,0:T(8,128)(2,1)S(1)}, bf16[768,512]{1,0:T(8,128)(2,1)S(1)}, u32[]{:S(2)}, u32[]{:S(2)}) collective-permute-start(bf16[768,512]{1,0:T(8,128)(2,1)S(1)} %collective-permute-done.18.refs_5_), channel_id=1, source_target_pairs={{0,16},{4,12},{8,24},{12,4},{16,0},{20,28},{24,8},{28,20},{1,17},{... | collective-permute-start | bytes 2359304 | tf_op jit(solution)/shard_map/ppermute | solution.py:272
  134.2 53.5 %collective-permute-start.25 = (bf16[1792,512]{1,0:T(8,128)(2,1)}, bf16[1792,512]{1,0:T(8,128)(2,1)S(1)}, u32[]{:S(2)}, u32[]{:S(2)}) collective-permute-start(bf16[1792,512]{1,0:T(8,128)(2,1)} %collective-permute-done.24.refs_2_), channel_id=1, source_target_pairs={{0,4},{4,0},{8,12},{12,8},{16,20},{20,16},{24,28},{28,24},{1,5},{5... | collective-permute-start | bytes 5505032 | tf_op jit(solution)/shard_map/ppermute | solution.py:267
  136.4 2.8 %copy-start = (bf16[48,16,4096]{2,1,0:T(8,128)(2,1)S(1)}, bf16[48,16,4096]{2,1,0:T(8,128)(2,1)}, u32[]{:S(2)}) copy-start(bf16[48,16,4096]{2,1,0:T(8,128)(2,1)} %param.7) | copy-start | bytes 18874372
  139.2 5.3 %copy-start.1 = (bf16[3584,128]{1,0:T(8,128)(2,1)S(1)}, bf16[3584,128]{1,0:T(8,128)(2,1)}, u32[]{:S(2)}) copy-start(bf16[3584,128]{1,0:T(8,128)(2,1)} %bank_ref.1) | copy-start | bytes 2752516
  139.2 11.3 %slice-start = ((s8[6291456]{0:T(1024)(128)(4,1)}), s8[4194304]{0:T(1024)(128)(4,1)S(1)}, s32[]{:S(2)}) async-start(s8[6291456]{0:T(1024)(128)(4,1)} %bitcast.15), calls=%async_computation | async-start | bytes 8388608
  144.4 5.4 %copy-start.3 = (bf16[512,512]{1,0:T(8,128)(2,1)S(1)}, bf16[512,512]{1,0:T(8,128)(2,1)}, u32[]{:S(2)}) copy-start(bf16[512,512]{1,0:T(8,128)(2,1)} %copy-done.2) | copy-start | bytes 1572868
  144.4 6.0 %slice-start.1 = ((s8[6291456]{0:T(1024)(128)(4,1)}), s8[2097152]{0:T(1024)(128)(4,1)S(1)}, s32[]{:S(2)}) async-start(s8[6291456]{0:T(1024)(128)(4,1)} %bitcast.15), calls=%async_computation.1 | async-start | bytes 4194304
  149.8 12.0 %collective-permute-start.12 = (bf16[512,512]{1,0:T(8,128)(2,1)S(1)}, bf16[512,512]{1,0:T(8,128)(2,1)S(1)}, u32[]{:S(2)}, u32[]{:S(2)}) collective-permute-start(bf16[512,512]{1,0:T(8,128)(2,1)S(1)} %copy-done.3), channel_id=1, source_target_pairs={{0,16},{4,12},{8,24},{12,4},{16,0},{20,28},{24,8},{28,20},{1,17},{... | collective-permute-start | bytes 1572872 | tf_op jit(solution)/shard_map/ppermute | solution.py:272
  161.8 36.1 %collective-permute-start.17 = (bf16[512,512]{1,0:T(8,128)(2,1)S(1)}, bf16[512,512]{1,0:T(8,128)(2,1)S(1)}, u32[]{:S(2)}, u32[]{:S(2)}) collective-permute-start(bf16[512,512]{1,0:T(8,128)(2,1)S(1)} %collective-permute-done.16.refs_2_), channel_id=1, source_target_pairs={{0,4},{4,0},{8,12},{12,8},{16,20},{20,16},{24,28},{28,24},{1,5},{5... | collective-permute-start | bytes 1572872 | tf_op jit(solution)/shard_map/ppermute | solution.py:267
  162.1 37.7 %collective-permute-start.13 = (bf16[512,512]{1,0:T(8,128)(2,1)S(1)}, bf16[512,512]{1,0:T(8,128)(2,1)S(1)}, u32[]{:S(2)}, u32[]{:S(2)}) collective-permute-start(bf16[512,512]{1,0:T(8,128)(2,1)S(1)} %collective-permute-done.12.refs_2_), channel_id=1, source_target_pairs={{0,4},{4,0},{8,12},{12,8},{16,20},{20,16},{24,28},{28,24},{1,5},{5... | collective-permute-start | bytes 1572872 | tf_op jit(solution)/shard_map/ppermute | solution.py:267
  162.4 32.8 %collective-permute-start.21 = (bf16[768,512]{1,0:T(8,128)(2,1)S(1)}, bf16[768,512]{1,0:T(8,128)(2,1)S(1)}, u32[]{:S(2)}, u32[]{:S(2)}) collective-permute-start(bf16[768,512]{1,0:T(8,128)(2,1)S(1)} %collective-permute-done.20.refs_2_), channel_id=1, source_target_pairs={{0,4},{4,0},{8,12},{12,8},{16,20},{20,16},{24,28},{28,24},{1,5},{5... | collective-permute-start | bytes 2359304 | tf_op jit(solution)/shard_map/ppermute | solution.py:267

commit v5 on v4

--- a/solution.py
+++ b/solution.py
@@ -29,8 +29,8 @@
     tiles = rows // tile
     if rows % tile or tiles < 8:
         return None
-    second = (tiles - 4) * 3 // 10
-    lengths = [tiles - 4 - second, second, 2, 2]
+    second = (tiles - 3) * 2 // 5
+    lengths = [tiles - 3 - second, second, 2, 1]
     pieces, start = [], 0
     for length in lengths:
         pieces.append((start * tile, length * tile))
@@ -336,7 +336,7 @@
             partial.append(product(flat_tokens, start, length, tile, rows, side, partial=part))
         for c, (start, length) in enumerate(chunks):
             far = [(m, held[c, m], 0) for m in (6, 7)]
-            if c + 1 == len(chunks):
+            if c > 1:
                 partial[c] = product(flat_tokens, start, length, tile, rows, far[:1], partial=partial[c], resident=True)
                 far = far[1:]
             hidden = product(flat_tokens, start, length, length if c > 1 and start % length == 0 else tile, rows, far, partial=partial[c], final=True, hidden=hidden, resident=c > 1)

time: 202 us -> 196 us (0.970)
  waiting for transfers between devices: 105 us -> 95.9 us
    ppermute x10, waiting for transfers between devices: 76.3 us -> 68.4 us  [send(): lax.ppermute(block, 'pop', [(i, i ^ (axis ^ (one | two) if i & core else...]
    ppermute x3, waiting for transfers between devices: 19 us -> 15.6 us  [shards(): lax.ppermute(bank_in, 'row', [(i, (i - step) % lanes) for i in range(lane...]
    ppermute x12, waiting for transfers between devices: 6.37 us -> 8.51 us  [flip(): return lax.ppermute(block, 'pop', [(i, i ^ mask) for i in range(pops)])]
    unnamed x33 -> x31, local copies, waits for them, and re-layouts: 3.85 us -> 5.04 us
    pallas_call x13 -> x14, Pallas kernels: 49.9 us -> 50.3 us  [product(): pl.pallas_call(kernel, grid=(length // tile,), in_specs=specs, out_specs=...]
  transfers between devices with their start and end apart: 26 -> 26, of which waited for: 9 -> 9; matrix products, arithmetic and copies ran while one was open for 2% -> 2% of each run, Pallas kernels for 31% -> 33%
where the time goes in v5:
time: 196 us; the launch traced here: 195 us
  waiting for transfers between devices  95.9 us (49%)
  Pallas kernels  64.8 us (33%)
  starting transfers between devices  25.1 us (13%)
  local copies, waits for them, and re-layouts  5.86 us (3%)
    ppermute x10, waiting for transfers between devices, send(): lax.ppermute(block, 'pop', [(i, i ^ (axis ^ (one | two) if i & core else...  68.4 us
    pallas_call x14, Pallas kernels, product(): pl.pallas_call(kernel, grid=(length // tile,), in_specs=specs, out_specs=...  50.3 us
    ppermute x3, waiting for transfers between devices, shards(): lax.ppermute(bank_in, 'row', [(i, (i - step) % lanes) for i in range(lane...  15.6 us
    ppermute x10, starting transfers between devices, send(): lax.ppermute(block, 'pop', [(i, i ^ (axis ^ (one | two) if i & core else...  12 us
    ppermute x12, waiting for transfers between devices, flip(): return lax.ppermute(block, 'pop', [(i, i ^ mask) for i in range(pops)])  8.51 us
    ppermute x3, starting transfers between devices, shards(): lax.ppermute(bank_in, 'row', [(i, (i - step) % lanes) for i in range(lane...  7.77 us
    pallas_call x1, Pallas kernels, updated(): pl.pallas_call(update_kernel, grid=(rows // tile,), in_specs=[pl.BlockSpe...  5.33 us
    unnamed x31, local copies, waits for them, and re-layouts  5.04 us
  transfers between devices with their start and end apart: 26, of which 9 were waited for; matrix products, arithmetic and copies ran while one was open for 2% of the time, Pallas kernels for 33%

profile of v5, /device:TPU:0, one launch (start us, length us, event | category | flops | bytes accessed | tf_op | source)
XLA Modules:
  0.0 195.0 jit_solution(8429000070132623798)
XLA Ops:
  0.7 3.1 %collective-permute-start.10 = (bf16[3584,512]{1,0:T(8,128)(2,1)}, bf16[3584,512]{1,0:T(8,128)(2,1)}, u32[]{:S(2)}, u32[]{:S(2)}) collective-permute-start(bf16[3584,512]{1,0:T(8,128)(2,1)} %weight_ref.1), channel_id=1, source_target_pairs={{0,16},{4,12},{8,24},{12,4},{16,0},{20,28},{24,8},{28,20},{1,17},{... | collective-permute-start | bytes 11010056 | tf_op jit(solution)/shard_map/ppermute | solution.py:272
  3.7 1.7 shard_map.86
  5.5 1.6 collective-permute-start.22
  7.1 0.6 collective-permute-start.3
  7.6 3.6 %collective-permute-start = (bf16[1024,128]{1,0:T(8,128)(2,1)S(1)}, bf16[1024,128]{1,0:T(8,128)(2,1)S(1)}, u32[]{:S(2)}, u32[]{:S(2)}) collective-permute-start(bf16[1024,128]{1,0:T(8,128)(2,1)S(1)} %copy-done.2), channel_id=1, source_target_pairs={{0,3},{1,0},{2,1},{3,2},{4,7},{5,4},{6,5},{7,6},{8,11},{9,8},{10,9... | collective-permute-start | bytes 786440 | tf_op jit(solution)/shard_map/ppermute | solution.py:316
  11.2 2.6 %collective-permute-done.3 = s32[48,17]{0,1:T(8,128)S(1)} collective-permute-done((s32[48,17]{0,1:T(8,128)S(1)}, s32[48,17]{0,1:T(8,128)S(1)}, u32[]{:S(2)}, u32[]{:S(2)}) %collective-permute-start.3) | collective-permute-done | bytes 3296 | tf_op jit(solution)/shard_map/ppermute | solution.py:267
  13.8 0.1 pad_add_fusion.2
  13.9 0.5 collective-permute-start.4
  14.4 34.3 %collective-permute-done.4 = s32[96,17]{0,1:T(8,128)S(1)} collective-permute-done((s32[96,17]{0,1:T(8,128)S(1)}, s32[96,17]{0,1:T(8,128)S(1)}, u32[]{:S(2)}, u32[]{:S(2)}) %collective-permute-start.4) | collective-permute-done | bytes 6560 | tf_op jit(solution)/shard_map/ppermute | solution.py:272
  48.7 3.3 %collective-permute-start.5 = (s32[96,17]{0,1:T(8,128)S(1)}, s32[96,17]{0,1:T(8,128)S(1)}, u32[]{:S(2)}, u32[]{:S(2)}) collective-permute-start(s32[96,17]{0,1:T(8,128)S(1)} %pad_add_fusion.2), channel_id=1, source_target_pairs={{0,24},{8,16},{16,8},{24,0},{1,25},{9,17},{17,9},{25,1},{2,26},{10... | collective-permute-start | bytes 19592 | tf_op jit(solution)/shard_map/ppermute | solution.py:291
  52.0 3.3 %collective-permute-done.5 = s32[96,17]{0,1:T(8,128)S(1)} collective-permute-done((s32[96,17]{0,1:T(8,128)S(1)}, s32[96,17]{0,1:T(8,128)S(1)}, u32[]{:S(2)}, u32[]{:S(2)}) %collective-permute-start.5) | collective-permute-done | bytes 6560 | tf_op jit(solution)/shard_map/ppermute | solution.py:291
  55.3 0.1 pad_add_fusion
  55.4 0.0 collective-permute-start.6
  55.4 1.2 collective-permute-done.6
  56.6 2.6 %collective-permute-start.1 = (bf16[1024,128]{1,0:T(8,128)(2,1)S(1)}, bf16[1024,128]{1,0:T(8,128)(2,1)S(1)}, u32[]{:S(2)}, u32[]{:S(2)}) collective-permute-start(bf16[1024,128]{1,0:T(8,128)(2,1)S(1)} %copy-done.2), channel_id=1, source_target_pairs={{0,2},{1,3},{2,0},{3,1},{4,6},{5,7},{6,4},{7,5},{8,10},{9,11},{10,... | collective-permute-start | bytes 786440 | tf_op jit(solution)/shard_map/ppermute | solution.py:316
  59.2 0.7 copy-done.4
  59.9 1.6 collective-permute-start.2
  61.4 15.6 %collective-permute-done.1.refs_2_ = bf16[1024,128]{1,0:T(8,128)(2,1)S(1)} collective-permute-done((bf16[1024,128]{1,0:T(8,128)(2,1)S(1)}, bf16[1024,128]{1,0:T(8,128)(2,1)S(1)}, u32[]{:S(2)}, u32[]{:S(2)}) %collective-permute-start.1) | collective-permute-done | bytes 262176 | tf_op jit(solution)/shard_map/ppermute | solution.py:316
  77.1 0.7 copy-done.6
  77.8 1.5 collective-permute-start.8
  79.3 2.2 %shard_map.93 = bf16[1024,512]{1,0:T(8,128)(2,1)} custom-call(bf16[3584,512]{1,0:T(8,128)(2,1)} %weight_ref.1), custom_call_target="tpu_custom_call" | custom-call | flops 1048576 | bytes 2097152 | tf_op jit(solution)/shard_map/pallas_call | solution.py:146
  81.5 0.7 copy-done.8
  82.2 0.5 collective-permute-start.18
  82.7 1.5 collective-permute-done.8.refs_5_
  84.3 1.5 collective-permute-start.14
  85.8 0.5 collective-permute-start.24
  86.3 32.6 %collective-permute-done.14.refs_5_ = bf16[512,512]{1,0:T(8,128)(2,1)S(1)} collective-permute-done((bf16[512,512]{1,0:T(8,128)(2,1)S(1)}, bf16[512,512]{1,0:T(8,128)(2,1)S(1)}, u32[]{:S(2)}, u32[]{:S(2)}) %collective-permute-start.14) | collective-permute-done | bytes 524320 | tf_op jit(solution)/shard_map/ppermute | solution.py:272
  118.9 1.9 collective-permute-done.9.refs_6_
  120.8 0.1 collective-permute-start.23
  120.9 0.1 pad_add_fusion.3.pick_ref
  121.0 0.1 copy.19.seeds_ref
  121.1 0.4 collective-permute-start.19
  121.5 0.6 slice_add_fusion
  122.1 0.8 concatenate.20
  122.9 0.0 copy-start.5
  123.0 0.3 convert_reduce_fusion
  123.3 2.9 %collective-permute-done.19.refs_6_ = bf16[1024,512]{1,0:T(8,128)(2,1)} collective-permute-done((bf16[1024,512]{1,0:T(8,128)(2,1)S(1)}, bf16[1024,512]{1,0:T(8,128)(2,1)}, u32[]{:S(2)}, u32[]{:S(2)}) %collective-permute-start.19) | collective-permute-done | bytes 1048608 | tf_op jit(solution)/shard_map/ppermute | solution.py:267
  126.2 0.5 collective-permute-start.20
  126.7 1.3 fusion.2.coupling_ref
  128.0 2.8 %copy-done = bf16[48,16,4096]{2,1,0:T(8,128)(2,1)S(1)} copy-done((bf16[48,16,4096]{2,1,0:T(8,128)(2,1)S(1)}, bf16[48,16,4096]{2,1,0:T(8,128)(2,1)}, u32[]{:S(2)}) %copy-start) | copy-done | bytes 6291480
  130.8 2.9 %project.1 = (f32[768,128]{1,0:T(8,128)S(1)}, bf16[512,128]{1,0:T(8,128)(2,1)S(1)}) custom-call(s32[6]{0:T(128)S(1)} %pad_add_fusion.3.pick_ref, bf16[768,4096]{1,0:T(8,128)(2,1)S(1)} %bitcast.14, bf16[1024,128]{1,0:T(8,128)(2,1)S(1)} %copy-done.3, bf16[1024,128]{1,0:T(8,128)(2,1)S(1)} %copy-done.5, bf16[1024,128]{1,0:T(8,128)(2,1)S(1)} %copy-done.7, ...), custom_call_target="tpu_custom_call" | custom-call | flops 805306368 | bytes 6291456 | tf_op jit(solution)/shard_map/project/pallas_call | solution.py:204
  133.8 2.3 %lowrank.1 = (bf16[768,256]{1,0:T(8,128)(2,1)S(1)}, bf16[256,512]{1,0:T(8,128)(2,1)S(1)}) custom-call(f32[768,128]{1,0:T(8,128)S(1)} %get-tuple-element.9.projected_ref, f32[128,128]{1,0:T(8,128)S(1)} %fusion.2.coupling_ref, s32[48,2,8]{2,1,0:T(2,128)S(1)} %copy.19.seeds_ref, bf16[512,128]{1,0:T(8,128)(2,1)S(1)} %get-tuple-element.10.columns_ref), custom_call_target="tpu_custom_call" | custom-call | flops 251658240 | bytes 786432 | tf_op jit(solution)/shard_map/lowrank/pallas_call | solution.py:244
  136.1 0.0 slice-start.1
  136.1 5.3 %update.1 = bf16[3584,512]{1,0:T(8,128)(2,1)} custom-call(bf16[3584,512]{1,0:T(8,128)(2,1)} %weight_ref.1, bf16[3584,128]{1,0:T(8,128)(2,1)S(1)} %copy-done.1, bf16[256,512]{1,0:T(8,128)(2,1)S(1)} %get-tuple-element.15.right_ref), custom_call_target="tpu_custom_call" | custom-call | flops 939524096 | bytes 7340032 | tf_op jit(solution)/shard_map/update/pallas_call | solution.py:167
  141.4 1.5 collective-permute-start.12
  143.0 5.7 %shard_map.94.refs_1_ = f32[768,1024]{1,0:T(8,128)S(1)} custom-call(bf16[768,4096]{1,0:T(8,128)(2,1)S(1)} %bitcast.17, bf16[768,256]{1,0:T(8,128)(2,1)S(1)} %get-tuple-element.11.refs_1_, bf16[3584,128]{1,0:T(8,128)(2,1)S(1)} %copy-done.1, bf16[3584,512]{1,0:T(8,128)(2,1)} %weight_ref.1, bf16[3584,512]{1,0:T(8,128)(2,1)} %collective-permute-done.7.refs_4_, ...), custom_call_target="tpu_custom_call" | custom-call | flops 3221225472 | bytes 8912896 | tf_op jit(solution)/shard_map/pallas_call | solution.py:115
  148.6 0.1 collective-permute-start.15
  148.7 0.8 collective-permute-start.16
  149.5 9.0 %shard_map.96.refs_1_ = f32[768,1792]{1,0:T(8,128)S(1)} custom-call(bf16[768,4096]{1,0:T(8,128)(2,1)S(1)} %bitcast.18, bf16[768,256]{1,0:T(8,128)(2,1)S(1)} %get-tuple-element.11.refs_1_, bf16[3584,128]{1,0:T(8,128)(2,1)S(1)} %copy-done.1, bf16[3584,512]{1,0:T(8,128)(2,1)} %weight_ref.1, bf16[3584,512]{1,0:T(8,128)(2,1)} %collective-permute-done.7.refs_4_, ...), custom_call_target="tpu_custom_call" | custom-call | flops 5637144576 | bytes 13238272 | tf_op jit(solution)/shard_map/pallas_call | solution.py:115
  158.6 0.1 collective-permute-start.21
  158.7 2.3 %shard_map.87.refs_1_ = f32[768,256]{1,0:T(8,128)S(1)} custom-call(bf16[768,4096]{1,0:T(8,128)(2,1)S(1)} %bitcast.19, bf16[768,256]{1,0:T(8,128)(2,1)S(1)} %get-tuple-element.11.refs_1_, bf16[3584,128]{1,0:T(8,128)(2,1)S(1)} %copy-done.1, bf16[3584,512]{1,0:T(8,128)(2,1)} %weight_ref.1, bf16[3584,512]{1,0:T(8,128)(2,1)} %collective-permute-done.7.refs_4_, ...), custom_call_target="tpu_custom_call" | custom-call | flops 805306368 | bytes 4587520 | tf_op jit(solution)/shard_map/pallas_call | solution.py:115
  161.0 0.5 collective-permute-start.13
  161.5 0.1 collective-permute-start.17
  161.6 3.3 %shard_map.90.refs_1_ = f32[768,512]{1,0:T(8,128)S(1)} custom-call(bf16[768,4096]{1,0:T(8,128)(2,1)S(1)} %bitcast.20, bf16[768,256]{1,0:T(8,128)(2,1)S(1)} %get-tuple-element.11.refs_1_, bf16[3584,128]{1,0:T(8,128)(2,1)S(1)} %copy-done.1, bf16[3584,512]{1,0:T(8,128)(2,1)} %weight_ref.1, bf16[3584,512]{1,0:T(8,128)(2,1)} %collective-permute-done.7.refs_4_, ...), custom_call_target="tpu_custom_call" | custom-call | flops 1610612736 | bytes 6029312 | tf_op jit(solution)/shard_map/pallas_call | solution.py:115
  164.9 4.2 %shard_map.95.refs_1_ = f32[768,1024]{1,0:T(8,128)S(1)} custom-call(bf16[768,4096]{1,0:T(8,128)(2,1)S(1)} %bitcast.21, f32[768,1024]{1,0:T(8,128)S(1)} %shard_map.94.refs_1_, bf16[3584,512]{1,0:T(8,128)(2,1)} %collective-permute-done.10.refs_2_, bf16[3584,512]{1,0:T(8,128)(2,1)} %collective-permute-done.11.refs_3_), custom_call_target="tpu_custom_call", output_to_operand_aliasing={{}: (1, {})} | custom-call | flops 1610612736 | bytes 5242880 | tf_op jit(solution)/shard_map/pallas_call | solution.py:115
  169.1 6.8 %shard_map.97.refs_1_ = f32[768,1792]{1,0:T(8,128)S(1)} custom-call(bf16[768,4096]{1,0:T(8,128)(2,1)S(1)} %bitcast.22, f32[768,1792]{1,0:T(8,128)S(1)} %shard_map.96.refs_1_, bf16[3584,512]{1,0:T(8,128)(2,1)} %collective-permute-done.10.refs_2_, bf16[3584,512]{1,0:T(8,128)(2,1)} %collective-permute-done.11.refs_3_), custom_call_target="tpu_custom_call", output_to_operand_aliasing={{}: (1, {})} | custom-call | flops 2818572288 | bytes 7995392 | tf_op jit(solution)/shard_map/pallas_call | solution.py:115
  176.0 2.4 %shard_map.91.refs_1_ = f32[768,512]{1,0:T(8,128)S(1)} custom-call(bf16[768,4096]{1,0:T(8,128)(2,1)S(1)} %bitcast.23, f32[768,512]{1,0:T(8,128)S(1)} %shard_map.90.refs_1_, bf16[3584,512]{1,0:T(8,128)(2,1)} %collective-permute-done.10.refs_2_, bf16[3584,512]{1,0:T(8,128)(2,1)} %collective-permute-done.11.refs_3_), custom_call_target="tpu_custom_call", output_to_operand_aliasing={{}: (1, {})} | custom-call | flops 805306368 | bytes 3407872 | tf_op jit(solution)/shard_map/pallas_call | solution.py:115
  178.4 7.5 %shard_map.98.refs_4_ = bf16[768,3584]{1,0:T(8,128)(2,1)} custom-call(bf16[768,4096]{1,0:T(8,128)(2,1)S(1)} %bitcast.24, f32[768,1792]{1,0:T(8,128)S(1)} %shard_map.97.refs_1_, bf16[1792,512]{1,0:T(8,128)(2,1)} %collective-permute-done.24.refs_2_, bf16[1792,512]{1,0:T(8,128)(2,1)S(1)} %collective-permute-done.25.refs_3_), custom_call_target="tpu_custom_call" | custom-call | flops 2818572288 | bytes 7995392 | tf_op jit(solution)/shard_map/pallas_call | solution.py:115
  185.8 1.7 shard_map.88.refs_1_
  187.6 0.4 shard_map.89.refs_1_
  188.0 0.9 shard_map.92.refs_1_
  189.0 3.4 %shard_map.99.refs_3_ = bf16[768,3584]{1,0:T(8,128)(2,1)} custom-call(bf16[768,4096]{1,0:T(8,128)(2,1)S(1)} %bitcast.28, f32[768,1024]{1,0:T(8,128)S(1)} %shard_map.95.refs_1_, bf16[1024,512]{1,0:T(8,128)(2,1)S(1)} %collective-permute-done.20.refs_2_, bf16[1024,512]{1,0:T(8,128)(2,1)S(1)} %collective-permute-done.21.refs_3_, ...), custom_call_target="tpu_custom_call", output_to_operand_aliasing={{}: (4, {})} | custom-call | flops 1610612736 | bytes 5242880 | tf_op jit(solution)/shard_map/pallas_call | solution.py:115
  192.3 1.6 shard_map.100.refs_3_
  193.9 1.1 shard_map.101
  (52 shorter events, 0.2 us)
Async XLA Ops:
  0.6 6.4 %copy-start.12 = (s32[48]{0:T(128)S(1)}, s32[48]{0:T(128)}, u32[]{:S(2)}) copy-start(s32[48]{0:T(128)} %param.11) | copy-start | bytes 580
  0.6 6.4 %copy-start.10 = (s32[48,2,8]{0,2,1:T(8,128)S(1)}, s32[48,2,8]{0,2,1:T(8,128)}, u32[]{:S(2)}) copy-start(s32[48,2,8]{0,2,1:T(8,128)} %param.12) | copy-start | bytes 9220
  0.6 7.0 %copy-start.2 = (bf16[1024,128]{1,0:T(8,128)(2,1)S(1)}, bf16[1024,128]{1,0:T(8,128)(2,1)}, u32[]{:S(2)}) copy-start(bf16[1024,128]{1,0:T(8,128)(2,1)} %refs_0_.1) | copy-start | bytes 786436
  0.7 78.6 %collective-permute-start.10 = (bf16[3584,512]{1,0:T(8,128)(2,1)}, bf16[3584,512]{1,0:T(8,128)(2,1)}, u32[]{:S(2)}, u32[]{:S(2)}) collective-permute-start(bf16[3584,512]{1,0:T(8,128)(2,1)} %weight_ref.1), channel_id=1, source_target_pairs={{0,16},{4,12},{8,24},{12,4},{16,0},{20,28},{24,8},{28,20},{1,17},{... | collective-permute-start | bytes 11010056 | tf_op jit(solution)/shard_map/ppermute | solution.py:272
  5.5 80.3 %collective-permute-start.22 = (bf16[1792,512]{1,0:T(8,128)(2,1)S(1)}, bf16[1792,512]{1,0:T(8,128)(2,1)S(1)}, u32[]{:S(2)}, u32[]{:S(2)}) collective-permute-start(bf16[1792,512]{1,0:T(8,128)(2,1)S(1)} %get-tuple-element.14), channel_id=1, source_target_pairs={{0,8},{4,20},{8,0},{12,28},{16,24},{20,4},{24,16},{28,12},{1,9},{5... | collective-permute-start | bytes 5505032 | tf_op jit(solution)/shard_map/ppermute | solution.py:272
  7.0 134.4 %collective-permute-start.7 = (bf16[3584,512]{1,0:T(8,128)(2,1)}, bf16[3584,512]{1,0:T(8,128)(2,1)}, u32[]{:S(2)}, u32[]{:S(2)}) collective-permute-start(bf16[3584,512]{1,0:T(8,128)(2,1)} %weight_ref.1), channel_id=1, source_target_pairs={{0,4},{4,0},{8,12},{12,8},{16,20},{20,16},{24,28},{28,24},{1,5},{5... | collective-permute-start | bytes 11010056 | tf_op jit(solution)/shard_map/ppermute | solution.py:267
  7.1 6.7 %collective-permute-start.3 = (s32[48,17]{0,1:T(8,128)S(1)}, s32[48,17]{0,1:T(8,128)S(1)}, u32[]{:S(2)}, u32[]{:S(2)}) collective-permute-start(s32[48,17]{0,1:T(8,128)S(1)} %pad_add_fusion.1), channel_id=1, source_target_pairs={{0,4},{4,0},{8,12},{12,8},{16,20},{20,16},{24,28},{28,24},{1,5},{5... | collective-permute-start | bytes 9800 | tf_op jit(solution)/shard_map/ppermute | solution.py:267
  7.6 51.5 %collective-permute-start = (bf16[1024,128]{1,0:T(8,128)(2,1)S(1)}, bf16[1024,128]{1,0:T(8,128)(2,1)S(1)}, u32[]{:S(2)}, u32[]{:S(2)}) collective-permute-start(bf16[1024,128]{1,0:T(8,128)(2,1)S(1)} %copy-done.2), channel_id=1, source_target_pairs={{0,3},{1,0},{2,1},{3,2},{4,7},{5,4},{6,5},{7,6},{8,11},{9,8},{10,9... | collective-permute-start | bytes 786440 | tf_op jit(solution)/shard_map/ppermute | solution.py:316
  13.9 34.8 %collective-permute-start.4 = (s32[96,17]{0,1:T(8,128)S(1)}, s32[96,17]{0,1:T(8,128)S(1)}, u32[]{:S(2)}, u32[]{:S(2)}) collective-permute-start(s32[96,17]{0,1:T(8,128)S(1)} %pad_add_fusion.2), channel_id=1, source_target_pairs={{0,8},{4,20},{8,0},{12,28},{16,24},{20,4},{24,16},{28,12},{1,9},{5... | collective-permute-start | bytes 19592 | tf_op jit(solution)/shard_map/ppermute | solution.py:272
  48.7 6.6 %collective-permute-start.5 = (s32[96,17]{0,1:T(8,128)S(1)}, s32[96,17]{0,1:T(8,128)S(1)}, u32[]{:S(2)}, u32[]{:S(2)}) collective-permute-start(s32[96,17]{0,1:T(8,128)S(1)} %pad_add_fusion.2), channel_id=1, source_target_pairs={{0,24},{8,16},{16,8},{24,0},{1,25},{9,17},{17,9},{25,1},{2,26},{10... | collective-permute-start | bytes 19592 | tf_op jit(solution)/shard_map/ppermute | solution.py:291
  55.4 1.2 collective-permute-start.6
  56.6 20.5 %collective-permute-start.1 = (bf16[1024,128]{1,0:T(8,128)(2,1)S(1)}, bf16[1024,128]{1,0:T(8,128)(2,1)S(1)}, u32[]{:S(2)}, u32[]{:S(2)}) collective-permute-start(bf16[1024,128]{1,0:T(8,128)(2,1)S(1)} %copy-done.2), channel_id=1, source_target_pairs={{0,2},{1,3},{2,0},{3,1},{4,6},{5,7},{6,4},{7,5},{8,10},{9,11},{10,... | collective-permute-start | bytes 786440 | tf_op jit(solution)/shard_map/ppermute | solution.py:316
  59.2 0.7 copy-start.4
  59.9 21.6 %collective-permute-start.2 = (bf16[1024,128]{1,0:T(8,128)(2,1)S(1)}, bf16[1024,128]{1,0:T(8,128)(2,1)S(1)}, u32[]{:S(2)}, u32[]{:S(2)}) collective-permute-start(bf16[1024,128]{1,0:T(8,128)(2,1)S(1)} %copy-done.2), channel_id=1, source_target_pairs={{0,1},{1,2},{2,3},{3,0},{4,5},{5,6},{6,7},{7,4},{8,9},{9,10},{10,1... | collective-permute-start | bytes 786440 | tf_op jit(solution)/shard_map/ppermute | solution.py:316
  77.1 0.7 copy-start.6
  77.8 43.2 %copy-start.11 = (s32[48,2,8]{0,2,1:T(8,128)S(1)}, s32[48,2,8]{0,2,1:T(8,128)}, u32[]{:S(2)}) copy-start(s32[48,2,8]{0,2,1:T(8,128)} %param.13) | copy-start | bytes 9220
  77.8 6.5 %collective-permute-start.8 = (bf16[256,512]{1,0:T(8,128)(2,1)S(1)}, bf16[256,512]{1,0:T(8,128)(2,1)}, u32[]{:S(2)}, u32[]{:S(2)}) collective-permute-start(bf16[256,512]{1,0:T(8,128)(2,1)S(1)} %get-tuple-element.12), channel_id=1, source_target_pairs={{0,8},{4,20},{8,0},{12,28},{16,24},{20,4},{24,16},{28,12},{1,9},{5... | collective-permute-start | bytes 786440 | tf_op jit(solution)/shard_map/ppermute | solution.py:272
  79.3 85.7 %collective-permute-start.11 = (bf16[3584,512]{1,0:T(8,128)(2,1)}, bf16[3584,512]{1,0:T(8,128)(2,1)}, u32[]{:S(2)}, u32[]{:S(2)}) collective-permute-start(bf16[3584,512]{1,0:T(8,128)(2,1)} %collective-permute-done.10.refs_2_), channel_id=1, source_target_pairs={{0,4},{4,0},{8,12},{12,8},{16,20},{20,16},{24,28},{28,24},{1,5},{5... | collective-permute-start | bytes 11010056 | tf_op jit(solution)/shard_map/ppermute | solution.py:267
  81.5 0.7 copy-start.8
  82.2 38.9 %collective-permute-start.18 = (bf16[1024,512]{1,0:T(8,128)(2,1)}, bf16[1024,512]{1,0:T(8,128)(2,1)S(1)}, u32[]{:S(2)}, u32[]{:S(2)}) collective-permute-start(bf16[1024,512]{1,0:T(8,128)(2,1)} %shard_map.93), channel_id=1, source_target_pairs={{0,8},{4,20},{8,0},{12,28},{16,24},{20,4},{24,16},{28,12},{1,9},{5... | collective-permute-start | bytes 3145736 | tf_op jit(solution)/shard_map/ppermute | solution.py:272
  84.3 34.6 %collective-permute-start.14 = (bf16[512,512]{1,0:T(8,128)(2,1)S(1)}, bf16[512,512]{1,0:T(8,128)(2,1)S(1)}, u32[]{:S(2)}, u32[]{:S(2)}) collective-permute-start(bf16[512,512]{1,0:T(8,128)(2,1)S(1)} %get-tuple-element.13), channel_id=1, source_target_pairs={{0,8},{4,20},{8,0},{12,28},{16,24},{20,4},{24,16},{28,12},{1,9},{5... | collective-permute-start | bytes 1572872 | tf_op jit(solution)/shard_map/ppermute | solution.py:272
  85.8 40.9 %collective-permute-start.24 = (bf16[1792,512]{1,0:T(8,128)(2,1)S(1)}, bf16[1792,512]{1,0:T(8,128)(2,1)}, u32[]{:S(2)}, u32[]{:S(2)}) collective-permute-start(bf16[1792,512]{1,0:T(8,128)(2,1)S(1)} %collective-permute-done.22.refs_5_), channel_id=1, source_target_pairs={{0,16},{4,12},{8,24},{12,4},{16,0},{20,28},{24,8},{28,20},{1,17},{... | collective-permute-start | bytes 5505032 | tf_op jit(solution)/shard_map/ppermute | solution.py:272
  118.9 1.9 collective-permute-start.9
  120.8 27.9 %collective-permute-start.23 = (bf16[1792,512]{1,0:T(8,128)(2,1)S(1)}, bf16[1792,512]{1,0:T(8,128)(2,1)}, u32[]{:S(2)}, u32[]{:S(2)}) collective-permute-start(bf16[1792,512]{1,0:T(8,128)(2,1)S(1)} %collective-permute-done.22.refs_5_), channel_id=1, source_target_pairs={{0,4},{4,0},{8,12},{12,8},{16,20},{20,16},{24,28},{28,24},{1,5},{5... | collective-permute-start | bytes 5505032 | tf_op jit(solution)/shard_map/ppermute | solution.py:267
  121.1 5.1 %collective-permute-start.19 = (bf16[1024,512]{1,0:T(8,128)(2,1)S(1)}, bf16[1024,512]{1,0:T(8,128)(2,1)}, u32[]{:S(2)}, u32[]{:S(2)}) collective-permute-start(bf16[1024,512]{1,0:T(8,128)(2,1)S(1)} %collective-permute-done.18.refs_5_), channel_id=1, source_target_pairs={{0,4},{4,0},{8,12},{12,8},{16,20},{20,16},{24,28},{28,24},{1,5},{5... | collective-permute-start | bytes 3145736 | tf_op jit(solution)/shard_map/ppermute | solution.py:267
  122.9 5.1 %copy-start.3 = (bf16[1024,128]{1,0:T(8,128)(2,1)S(1)}, bf16[1024,128]{1,0:T(8,128)(2,1)}, u32[]{:S(2)}) copy-start(bf16[1024,128]{1,0:T(8,128)(2,1)} %refs_0_.1) | copy-start | bytes 786436
  122.9 5.1 %copy-start.5 = (bf16[1024,128]{1,0:T(8,128)(2,1)S(1)}, bf16[1024,128]{1,0:T(8,128)(2,1)}, u32[]{:S(2)}) copy-start(bf16[1024,128]{1,0:T(8,128)(2,1)} %copy-done.4) | copy-start | bytes 786436
  123.0 5.1 %copy-start.7 = (bf16[1024,128]{1,0:T(8,128)(2,1)S(1)}, bf16[1024,128]{1,0:T(8,128)(2,1)}, u32[]{:S(2)}) copy-start(bf16[1024,128]{1,0:T(8,128)(2,1)} %copy-done.6) | copy-start | bytes 786436
  123.0 5.1 %copy-start.9 = (bf16[1024,128]{1,0:T(8,128)(2,1)S(1)}, bf16[1024,128]{1,0:T(8,128)(2,1)}, u32[]{:S(2)}) copy-start(bf16[1024,128]{1,0:T(8,128)(2,1)} %copy-done.8) | copy-start | bytes 786436
  126.2 32.4 %collective-permute-start.20 = (bf16[1024,512]{1,0:T(8,128)(2,1)S(1)}, bf16[1024,512]{1,0:T(8,128)(2,1)S(1)}, u32[]{:S(2)}, u32[]{:S(2)}) collective-permute-start(bf16[1024,512]{1,0:T(8,128)(2,1)S(1)} %collective-permute-done.18.refs_5_), channel_id=1, source_target_pairs={{0,16},{4,12},{8,24},{12,4},{16,0},{20,28},{24,8},{28,20},{1,17},{... | collective-permute-start | bytes 3145736 | tf_op jit(solution)/shard_map/ppermute | solution.py:272
  126.7 51.7 %collective-permute-start.25 = (bf16[1792,512]{1,0:T(8,128)(2,1)}, bf16[1792,512]{1,0:T(8,128)(2,1)S(1)}, u32[]{:S(2)}, u32[]{:S(2)}) collective-permute-start(bf16[1792,512]{1,0:T(8,128)(2,1)} %collective-permute-done.24.refs_2_), channel_id=1, source_target_pairs={{0,4},{4,0},{8,12},{12,8},{16,20},{20,16},{24,28},{28,24},{1,5},{5... | collective-permute-start | bytes 5505032 | tf_op jit(solution)/shard_map/ppermute | solution.py:267
  128.0 2.8 %copy-start = (bf16[48,16,4096]{2,1,0:T(8,128)(2,1)S(1)}, bf16[48,16,4096]{2,1,0:T(8,128)(2,1)}, u32[]{:S(2)}) copy-start(bf16[48,16,4096]{2,1,0:T(8,128)(2,1)} %param.7) | copy-start | bytes 18874372
  130.8 5.3 %copy-start.1 = (bf16[3584,128]{1,0:T(8,128)(2,1)S(1)}, bf16[3584,128]{1,0:T(8,128)(2,1)}, u32[]{:S(2)}) copy-start(bf16[3584,128]{1,0:T(8,128)(2,1)} %bank_ref.1) | copy-start | bytes 2752516
  130.8 12.1 %slice-start = ((s8[6291456]{0:T(1024)(128)(4,1)}), s8[4194304]{0:T(1024)(128)(4,1)S(1)}, s32[]{:S(2)}) async-start(s8[6291456]{0:T(1024)(128)(4,1)} %bitcast.15), calls=%async_computation | async-start | bytes 8388608
  136.1 6.9 %slice-start.1 = ((s8[6291456]{0:T(1024)(128)(4,1)}), s8[2097152]{0:T(1024)(128)(4,1)S(1)}, s32[]{:S(2)}) async-start(s8[6291456]{0:T(1024)(128)(4,1)} %bitcast.15), calls=%async_computation.1 | async-start | bytes 4194304
  141.4 7.2 %collective-permute-start.12 = (bf16[256,512]{1,0:T(8,128)(2,1)}, bf16[256,512]{1,0:T(8,128)(2,1)S(1)}, u32[]{:S(2)}, u32[]{:S(2)}) collective-permute-start(bf16[256,512]{1,0:T(8,128)(2,1)} %collective-permute-done.8.refs_5_), channel_id=1, source_target_pairs={{0,16},{4,12},{8,24},{12,4},{16,0},{20,28},{24,8},{28,20},{1,17},{... | collective-permute-start | bytes 786440 | tf_op jit(solution)/shard_map/ppermute | solution.py:272
  148.6 12.4 %collective-permute-start.15 = (bf16[512,512]{1,0:T(8,128)(2,1)S(1)}, bf16[512,512]{1,0:T(8,128)(2,1)S(1)}, u32[]{:S(2)}, u32[]{:S(2)}) collective-permute-start(bf16[512,512]{1,0:T(8,128)(2,1)S(1)} %collective-permute-done.14.refs_5_), channel_id=1, source_target_pairs={{0,4},{4,0},{8,12},{12,8},{16,20},{20,16},{24,28},{28,24},{1,5},{5... | collective-permute-start | bytes 1572872 | tf_op jit(solution)/shard_map/ppermute | solution.py:267
  148.7 12.8 %collective-permute-start.16 = (bf16[512,512]{1,0:T(8,128)(2,1)S(1)}, bf16[512,512]{1,0:T(8,128)(2,1)S(1)}, u32[]{:S(2)}, u32[]{:S(2)}) collective-permute-start(bf16[512,512]{1,0:T(8,128)(2,1)S(1)} %collective-permute-done.14.refs_5_), channel_id=1, source_target_pairs={{0,16},{4,12},{8,24},{12,4},{16,0},{20,28},{24,8},{28,20},{1,17},{... | collective-permute-start | bytes 1572872 | tf_op jit(solution)/shard_map/ppermute | solution.py:272
  158.6 30.4 %collective-permute-start.21 = (bf16[1024,512]{1,0:T(8,128)(2,1)S(1)}, bf16[1024,512]{1,0:T(8,128)(2,1)S(1)}, u32[]{:S(2)}, u32[]{:S(2)}) collective-permute-start(bf16[1024,512]{1,0:T(8,128)(2,1)S(1)} %collective-permute-done.20.refs_2_), channel_id=1, source_target_pairs={{0,4},{4,0},{8,12},{12,8},{16,20},{20,16},{24,28},{28,24},{1,5},{5... | collective-permute-start | bytes 3145736 | tf_op jit(solution)/shard_map/ppermute | solution.py:267
  161.0 32.9 %collective-permute-start.13 = (bf16[256,512]{1,0:T(8,128)(2,1)S(1)}, bf16[256,512]{1,0:T(8,128)(2,1)S(1)}, u32[]{:S(2)}, u32[]{:S(2)}) collective-permute-start(bf16[256,512]{1,0:T(8,128)(2,1)S(1)} %collective-permute-done.12.refs_2_), channel_id=1, source_target_pairs={{0,4},{4,0},{8,12},{12,8},{16,20},{20,16},{24,28},{28,24},{1,5},{5... | collective-permute-start | bytes 786440 | tf_op jit(solution)/shard_map/ppermute | solution.py:267
  161.5 30.8 %collective-permute-start.17 = (bf16[512,512]{1,0:T(8,128)(2,1)S(1)}, bf16[512,512]{1,0:T(8,128)(2,1)S(1)}, u32[]{:S(2)}, u32[]{:S(2)}) collective-permute-start(bf16[512,512]{1,0:T(8,128)(2,1)S(1)} %collective-permute-done.16.refs_2_), channel_id=1, source_target_pairs={{0,4},{4,0},{8,12},{12,8},{16,20},{20,16},{24,28},{28,24},{1,5},{5... | collective-permute-start | bytes 1572872 | tf_op jit(solution)/shard_map/ppermute | solution.py:267
